TPU v7x, 16 devices: a whole 2x2x2 slice. The times are simulated.
16 devices in a mesh: dp: 1, tp: 16 (over x, y, z, core).
Axes of the slice: x: 2, y: 2, z: 2, core: 2. Of those that a mesh axis runs over, the one named last changes fastest.
Arguments:
- x: bfloat16 [2048, 8192], P(('dp', 'tp'))
- dy: bfloat16 [2048, 8192], P(('dp', 'tp'))
- pre: bfloat16 [2048, 32768], P('dp', 'tp')
- w_in: bfloat16 [8192, 32768], P(None, 'tp')
- w_down: bfloat16 [32768, 8192], P('tp')
Outputs:
- output 1: bfloat16 [2048, 8192], P(('dp', 'tp'))
- output 2: bfloat16 [8192, 32768], P('dp', 'tp')
- output 3: bfloat16 [32768, 8192], P(('dp', 'tp'))
All inputs are finite; a program needn't handle non-finite values.
Results may differ from a plain program's by a relative error of at most 0.012.
Values are sent between devices in bfloat16 or wider.
A program may use at most 2 GiB of HBM per device.

v0:
```python
import jax
import jax.numpy as jnp


def act(pre):
    return jax.nn.gelu(pre)


def solution(mesh):
    def step(x, dy, pre, w_in, w_down):
        hidden, back = jax.vjp(act, pre.astype(jnp.float32))
        d_hidden = jnp.dot(dy, w_down.T, preferred_element_type=jnp.float32)
        d_pre = back(d_hidden)[0].astype(jnp.bfloat16)
        dx = jnp.dot(d_pre, w_in.T)
        groups = mesh.shape["dp"]

        def by_group(a, b):
            a, b = (t.reshape(groups, -1, t.shape[-1]) for t in (a, b))
            product = jnp.einsum("gta,gtb->gab", a, b, preferred_element_type=jnp.float32)
            return product.astype(jnp.bfloat16).reshape(-1, b.shape[-1])

        return dx, by_group(x, d_pre), by_group(hidden.astype(jnp.bfloat16), dy)

    return step
```

profile of v0, /device:TPU:0, one launch (start us, length us, event | category | flops | bytes accessed | tf_op | source)
XLA Modules:
  0.0 1429.1 jit_solution(14172593841940786071)
XLA Ops:
  7.2 3.1 copy.24
  11.1 147.7 %all-gather.5.cloned.1.call-done = bf16[2048,8192]{1,0:T(8,128)(2,1)} async-done(((bf16[128,8192]{1,0:T(8,128)(2,1)}), bf16[2048,8192]{1,0:T(8,128)(2,1)}) %all-gather.5.cloned.1.call-update) | async-done | bytes 33554448 | tf_op args[1]
  158.9 104.0 %fusion.34 = bf16[2048,2048]{1,0:T(8,128)(2,1)} fusion(bf16[2048,2048]{1,0:T(8,128)(2,1)} %param.6, bf16[2048,8192]{1,0:T(8,128)(2,1)} %all-gather.5.cloned.1.call-done, bf16[2048,8192]{1,0:T(8,128)(2,1)} %param.5), kind=kOutput, calls=%fused_computation.53 | convolution fusion | flops 68807557120 | bytes 83886080 | tf_op jit(solution)/dot_general | solution.py:12
  262.9 435.2 %while.4 = (bf16[2048,2048]{1,0:T(8,128)(2,1)}, bf16[8192,2048]{1,0:T(8,128)(2,1)}, bf16[128,8192]{1,0:T(8,128)(2,1)S(1)}, bf16[128,8192]{1,0:T(8,128)(2,1)}, u3...) while((bf16[2048,2048]{1,0:T(8,128)(2,1)}, ...), condition=%wide.windowed_dot_general_cond_rs.clone, body=%wide.windowed_dot_general_body_rs.clone.sunk | while | flops 17190354944 | bytes 167772800 | solution.py:14
  262.9 1.5 broadcast_select_fusion.4
  264.6 1.5 broadcast_select_fusion.5
  266.1 3.3 collective-permute-start.1
  269.4 16.7 %fusion.79 = bf16[2,128,8192]{2,1,0:T(8,128)(2,1)} fusion(bf16[8192,2048]{1,0:T(8,128)(2,1)} %get-tuple-element.175, s32[]{:T(128)S(6)} %multiply.28, bf16[1,2048,2048]{2,1,0:T(8,128)(2,1)} %bitcast.60, s32[]{:T(128)S(6)} %multiply.29), kind=kOutput, calls=%fused_computation.2.clone.1 | convolution fusion | flops 8592031744 | bytes 46137352 | tf_op jit(solution)/dot_general | solution.py:14
  286.1 5.6 collective-permute-done
  293.0 5.3 fusion.80
  298.3 43.4 %collective-permute-start.2 = (bf16[128,8192]{1,0:T(8,128)(2,1)}, bf16[128,8192]{1,0:T(8,128)(2,1)S(1)}, u32[]{:S(2)}, u32[]{:S(2)}) collective-permute-start(bf16[128,8192]{1,0:T(8,128)(2,1)} %get-tuple-element.141), channel_id=6, source_target_pairs={{0,1},{1,2},{2,3},{3,4},{4,5},{5,6},{6,7},{7,8},{8,9},{9,10},{10,1... | collective-permute-start | bytes 6291464 | tf_op jit(solution)/dot_general | solution.py:14
  341.7 16.8 %fusion.81 = bf16[2,128,8192]{2,1,0:T(8,128)(2,1)} fusion(bf16[8192,2048]{1,0:T(8,128)(2,1)} %get-tuple-element.175, s32[]{:T(128)S(6)} %multiply.30, bf16[1,2048,2048]{2,1,0:T(8,128)(2,1)} %bitcast.61, s32[]{:T(128)S(6)} %multiply.31), kind=kOutput, calls=%fused_computation.clone.1 | convolution fusion | flops 8592031744 | bytes 46137352 | tf_op jit(solution)/dot_general | solution.py:14
  359.8 5.5 collective-permute-done.3
  365.3 5.2 fusion.82
  370.5 3.0 broadcast_select_fusion.4
  373.6 23.1 %collective-permute-start = (bf16[128,8192]{1,0:T(8,128)(2,1)}, bf16[128,8192]{1,0:T(8,128)(2,1)}, u32[]{:S(2)}, u32[]{:S(2)}) collective-permute-start(bf16[128,8192]{1,0:T(8,128)(2,1)} %broadcast_select_fusion.4), channel_id=4, source_target_pairs={{0,1},{1,2},{2,3},{3,4},{4,5},{5,6},{6,7},{7,8},{8,9},{9,10},{10,1... | collective-permute-start | bytes 6291464 | tf_op jit(solution)/dot_general | solution.py:14
  398.2 16.8 %fusion.79 = bf16[2,128,8192]{2,1,0:T(8,128)(2,1)} fusion(bf16[8192,2048]{1,0:T(8,128)(2,1)} %get-tuple-element.175, s32[]{:T(128)S(6)} %multiply.28, bf16[1,2048,2048]{2,1,0:T(8,128)(2,1)} %bitcast.60, s32[]{:T(128)S(6)} %multiply.29), kind=kOutput, calls=%fused_computation.2.clone.1 | convolution fusion | flops 8592031744 | bytes 46137352 | tf_op jit(solution)/dot_general | solution.py:14
  414.9 6.9 collective-permute-done.1
  421.8 5.3 fusion.80
  427.1 22.5 %collective-permute-start.2 = (bf16[128,8192]{1,0:T(8,128)(2,1)}, bf16[128,8192]{1,0:T(8,128)(2,1)S(1)}, u32[]{:S(2)}, u32[]{:S(2)}) collective-permute-start(bf16[128,8192]{1,0:T(8,128)(2,1)} %get-tuple-element.141), channel_id=6, source_target_pairs={{0,1},{1,2},{2,3},{3,4},{4,5},{5,6},{6,7},{7,8},{8,9},{9,10},{10,1... | collective-permute-start | bytes 6291464 | tf_op jit(solution)/dot_general | solution.py:14
  449.6 16.7 %fusion.81 = bf16[2,128,8192]{2,1,0:T(8,128)(2,1)} fusion(bf16[8192,2048]{1,0:T(8,128)(2,1)} %get-tuple-element.175, s32[]{:T(128)S(6)} %multiply.30, bf16[1,2048,2048]{2,1,0:T(8,128)(2,1)} %bitcast.61, s32[]{:T(128)S(6)} %multiply.31), kind=kOutput, calls=%fused_computation.clone.1 | convolution fusion | flops 8592031744 | bytes 46137352 | tf_op jit(solution)/dot_general | solution.py:14
  467.7 5.5 collective-permute-done.3
  473.2 5.2 fusion.82
  478.4 3.0 broadcast_select_fusion.4
  481.5 24.2 %collective-permute-start = (bf16[128,8192]{1,0:T(8,128)(2,1)}, bf16[128,8192]{1,0:T(8,128)(2,1)}, u32[]{:S(2)}, u32[]{:S(2)}) collective-permute-start(bf16[128,8192]{1,0:T(8,128)(2,1)} %broadcast_select_fusion.4), channel_id=4, source_target_pairs={{0,1},{1,2},{2,3},{3,4},{4,5},{5,6},{6,7},{7,8},{8,9},{9,10},{10,1... | collective-permute-start | bytes 6291464 | tf_op jit(solution)/dot_general | solution.py:14
  507.1 16.8 %fusion.79 = bf16[2,128,8192]{2,1,0:T(8,128)(2,1)} fusion(bf16[8192,2048]{1,0:T(8,128)(2,1)} %get-tuple-element.175, s32[]{:T(128)S(6)} %multiply.28, bf16[1,2048,2048]{2,1,0:T(8,128)(2,1)} %bitcast.60, s32[]{:T(128)S(6)} %multiply.29), kind=kOutput, calls=%fused_computation.2.clone.1 | convolution fusion | flops 8592031744 | bytes 46137352 | tf_op jit(solution)/dot_general | solution.py:14
  523.9 6.9 collective-permute-done.1
  530.7 5.3 fusion.80
  536.0 22.8 %collective-permute-start.2 = (bf16[128,8192]{1,0:T(8,128)(2,1)}, bf16[128,8192]{1,0:T(8,128)(2,1)S(1)}, u32[]{:S(2)}, u32[]{:S(2)}) collective-permute-start(bf16[128,8192]{1,0:T(8,128)(2,1)} %get-tuple-element.141), channel_id=6, source_target_pairs={{0,1},{1,2},{2,3},{3,4},{4,5},{5,6},{6,7},{7,8},{8,9},{9,10},{10,1... | collective-permute-start | bytes 6291464 | tf_op jit(solution)/dot_general | solution.py:14
  558.9 16.7 %fusion.81 = bf16[2,128,8192]{2,1,0:T(8,128)(2,1)} fusion(bf16[8192,2048]{1,0:T(8,128)(2,1)} %get-tuple-element.175, s32[]{:T(128)S(6)} %multiply.30, bf16[1,2048,2048]{2,1,0:T(8,128)(2,1)} %bitcast.61, s32[]{:T(128)S(6)} %multiply.31), kind=kOutput, calls=%fused_computation.clone.1 | convolution fusion | flops 8592031744 | bytes 46137352 | tf_op jit(solution)/dot_general | solution.py:14
  576.9 5.5 collective-permute-done.3
  582.5 5.2 fusion.82
  587.7 3.0 broadcast_select_fusion.4
  590.8 25.3 %collective-permute-start = (bf16[128,8192]{1,0:T(8,128)(2,1)}, bf16[128,8192]{1,0:T(8,128)(2,1)}, u32[]{:S(2)}, u32[]{:S(2)}) collective-permute-start(bf16[128,8192]{1,0:T(8,128)(2,1)} %broadcast_select_fusion.4), channel_id=4, source_target_pairs={{0,1},{1,2},{2,3},{3,4},{4,5},{5,6},{6,7},{7,8},{8,9},{9,10},{10,1... | collective-permute-start | bytes 6291464 | tf_op jit(solution)/dot_general | solution.py:14
  617.5 16.8 %fusion.79 = bf16[2,128,8192]{2,1,0:T(8,128)(2,1)} fusion(bf16[8192,2048]{1,0:T(8,128)(2,1)} %get-tuple-element.175, s32[]{:T(128)S(6)} %multiply.28, bf16[1,2048,2048]{2,1,0:T(8,128)(2,1)} %bitcast.60, s32[]{:T(128)S(6)} %multiply.29), kind=kOutput, calls=%fused_computation.2.clone.1 | convolution fusion | flops 8592031744 | bytes 46137352 | tf_op jit(solution)/dot_general | solution.py:14
  634.3 6.8 collective-permute-done.1
  641.1 5.3 fusion.80
  646.4 22.8 %collective-permute-start.2 = (bf16[128,8192]{1,0:T(8,128)(2,1)}, bf16[128,8192]{1,0:T(8,128)(2,1)S(1)}, u32[]{:S(2)}, u32[]{:S(2)}) collective-permute-start(bf16[128,8192]{1,0:T(8,128)(2,1)} %get-tuple-element.141), channel_id=6, source_target_pairs={{0,1},{1,2},{2,3},{3,4},{4,5},{5,6},{6,7},{7,8},{8,9},{9,10},{10,1... | collective-permute-start | bytes 6291464 | tf_op jit(solution)/dot_general | solution.py:14
  669.3 16.7 %fusion.81 = bf16[2,128,8192]{2,1,0:T(8,128)(2,1)} fusion(bf16[8192,2048]{1,0:T(8,128)(2,1)} %get-tuple-element.175, s32[]{:T(128)S(6)} %multiply.30, bf16[1,2048,2048]{2,1,0:T(8,128)(2,1)} %bitcast.61, s32[]{:T(128)S(6)} %multiply.31), kind=kOutput, calls=%fused_computation.clone.1 | convolution fusion | flops 8592031744 | bytes 46137352 | tf_op jit(solution)/dot_general | solution.py:14
  687.3 5.6 collective-permute-done.3
  692.9 5.2 fusion.82
  698.1 24.2 %collective-permute-start.8 = (bf16[128,8192]{1,0:T(8,128)(2,1)}, bf16[128,8192]{1,0:T(8,128)(2,1)}, u32[]{:S(2)}, u32[]{:S(2)}) collective-permute-start(bf16[128,8192]{1,0:T(8,128)(2,1)} %get-tuple-element.13), channel_id=7, source_target_pairs={{0,1},{1,2},{2,3},{3,4},{4,5},{5,6},{6,7},{7,8},{8,9},{9,10},{10,1... | collective-permute-start | bytes 6291464 | tf_op jit(solution)/dot_general | solution.py:14
  722.3 113.0 %convolution_convert_fusion = bf16[2048,8192]{1,0:T(8,128)(2,1)} fusion(bf16[2048,8192]{1,0:T(8,128)(2,1)} %all-gather.5.cloned.1.call-done, bf16[2048,2048]{1,0:T(8,128)(2,1)} %param.6), kind=kOutput, calls=%fused_computation.49 | convolution fusion | flops 68778196992 | bytes 75497472 | tf_op jit(solution)/gta,gtb->gab/dot_general | solution.py:19
  835.3 12.4 copy
  847.7 519.8 %while.5 = (bf16[2048,2048]{0,1:T(8,128)(2,1)}, bf16[1,128,8192]{2,1,0:T(8,128)(2,1)}, f32[2048,8192]{1,0:T(8,128)}, bf16[1,128,8192]{2,1,0:T(8,128)(2,1)}, u32[...) while((bf16[2048,2048]{0,1:T(8,128)(2,1)}, ...), condition=%wide.windowed_dot_general_cond_ag.clone, body=%wide.windowed_dot_general_body_ag.clone.sunk | while | flops 17238589440 | bytes 327156288 | solution.py:19
  847.7 2.5 collective-permute-start.6
  850.2 26.6 %fusion.87 = f32[2048,8192,1]{1,0,2:T(8,128)} fusion(bf16[1,128,8192]{2,1,0:T(8,128)(2,1)} %get-tuple-element.199, bf16[1,128,8192]{2,1,0:T(8,128)(2,1)} %get-tuple-element.197, s32[]{:T(128)S(6)} %multiply.32, bf16[1,2048,2048]{1,2,0:T(8,128)(2,1)} %bitcast.57, s32[]{:T(128)S(6)} %multiply.33), kind=kOutput, calls=%fused_computation.30.clone.1 | convolution fusion | flops 8594128896 | bytes 79691784 | tf_op jit(solution)/gta,gtb->gab/dot_general | solution.py:19
  876.8 2.2 collective-permute-start.5
  879.0 37.8 %collective-permute-start.7 = (bf16[1,128,8192]{2,1,0:T(8,128)(2,1)}, bf16[1,128,8192]{2,1,0:T(8,128)(2,1)}, u32[]{:S(2)}, u32[]{:S(2)}) collective-permute-start(bf16[1,128,8192]{2,1,0:T(8,128)(2,1)} %collective-permute-done.6), channel_id=13, source_target_pairs={{0,1},{1,2},{2,3},{3,4},{4,5},{5,6},{6,7},{7,8},{8,9},{9,10},{10,1... | collective-permute-start | bytes 6291464 | tf_op jit(solution)/gta,gtb->gab/dot_general | solution.py:19
  916.8 43.7 %bitcast_add_fusion.3 = f32[2048,8192]{1,0:T(8,128)} fusion(f32[2048,8192,1]{1,0,2:T(8,128)} %fusion.87, f32[2048,8192]{1,0:T(8,128)} %get-tuple-element.198, pred[]{:T(512)S(6)} %compare.13, bf16[1,128,8192]{2,1,0:T(8,128)(2,1)} %collective-permute-done.6, bf16[1,128,8192]{2,1,0:T(8,128)(2,1)S(1)} %collective-permute-done.4, s32[]{:T(128)S(6)} %multiply.34, ...), kind=kOutput, calls=%fused_computation.24.clone.3 | convolution fusion | flops 8644460544 | bytes 213909520 | tf_op jit(solution)/gta,gtb->gab/dot_general | solution.py:19
  960.6 2.5 collective-permute-start.6
  963.1 26.6 %fusion.87 = f32[2048,8192,1]{1,0,2:T(8,128)} fusion(bf16[1,128,8192]{2,1,0:T(8,128)(2,1)} %get-tuple-element.199, bf16[1,128,8192]{2,1,0:T(8,128)(2,1)} %get-tuple-element.197, s32[]{:T(128)S(6)} %multiply.32, bf16[1,2048,2048]{1,2,0:T(8,128)(2,1)} %bitcast.57, s32[]{:T(128)S(6)} %multiply.33), kind=kOutput, calls=%fused_computation.30.clone.1 | convolution fusion | flops 8594128896 | bytes 79691784 | tf_op jit(solution)/gta,gtb->gab/dot_general | solution.py:19
  990.9 38.5 %collective-permute-start.7 = (bf16[1,128,8192]{2,1,0:T(8,128)(2,1)}, bf16[1,128,8192]{2,1,0:T(8,128)(2,1)}, u32[]{:S(2)}, u32[]{:S(2)}) collective-permute-start(bf16[1,128,8192]{2,1,0:T(8,128)(2,1)} %collective-permute-done.6), channel_id=13, source_target_pairs={{0,1},{1,2},{2,3},{3,4},{4,5},{5,6},{6,7},{7,8},{8,9},{9,10},{10,1... | collective-permute-start | bytes 6291464 | tf_op jit(solution)/gta,gtb->gab/dot_general | solution.py:19
  1029.5 66.3 %bitcast_add_fusion.3 = f32[2048,8192]{1,0:T(8,128)} fusion(f32[2048,8192,1]{1,0,2:T(8,128)} %fusion.87, f32[2048,8192]{1,0:T(8,128)} %get-tuple-element.198, pred[]{:T(512)S(6)} %compare.13, bf16[1,128,8192]{2,1,0:T(8,128)(2,1)} %collective-permute-done.6, bf16[1,128,8192]{2,1,0:T(8,128)(2,1)S(1)} %collective-permute-done.4, s32[]{:T(128)S(6)} %multiply.34, ...), kind=kOutput, calls=%fused_computation.24.clone.3 | convolution fusion | flops 8644460544 | bytes 213909520 | tf_op jit(solution)/gta,gtb->gab/dot_general | solution.py:19
  1095.8 2.5 collective-permute-start.6
  1098.4 26.6 %fusion.87 = f32[2048,8192,1]{1,0,2:T(8,128)} fusion(bf16[1,128,8192]{2,1,0:T(8,128)(2,1)} %get-tuple-element.199, bf16[1,128,8192]{2,1,0:T(8,128)(2,1)} %get-tuple-element.197, s32[]{:T(128)S(6)} %multiply.32, bf16[1,2048,2048]{1,2,0:T(8,128)(2,1)} %bitcast.57, s32[]{:T(128)S(6)} %multiply.33), kind=kOutput, calls=%fused_computation.30.clone.1 | convolution fusion | flops 8594128896 | bytes 79691784 | tf_op jit(solution)/gta,gtb->gab/dot_general | solution.py:19
  1126.4 39.5 %collective-permute-start.7 = (bf16[1,128,8192]{2,1,0:T(8,128)(2,1)}, bf16[1,128,8192]{2,1,0:T(8,128)(2,1)}, u32[]{:S(2)}, u32[]{:S(2)}) collective-permute-start(bf16[1,128,8192]{2,1,0:T(8,128)(2,1)} %collective-permute-done.6), channel_id=13, source_target_pairs={{0,1},{1,2},{2,3},{3,4},{4,5},{5,6},{6,7},{7,8},{8,9},{9,10},{10,1... | collective-permute-start | bytes 6291464 | tf_op jit(solution)/gta,gtb->gab/dot_general | solution.py:19
  1165.9 66.3 %bitcast_add_fusion.3 = f32[2048,8192]{1,0:T(8,128)} fusion(f32[2048,8192,1]{1,0,2:T(8,128)} %fusion.87, f32[2048,8192]{1,0:T(8,128)} %get-tuple-element.198, pred[]{:T(512)S(6)} %compare.13, bf16[1,128,8192]{2,1,0:T(8,128)(2,1)} %collective-permute-done.6, bf16[1,128,8192]{2,1,0:T(8,128)(2,1)S(1)} %collective-permute-done.4, s32[]{:T(128)S(6)} %multiply.34, ...), kind=kOutput, calls=%fused_computation.24.clone.3 | convolution fusion | flops 8644460544 | bytes 213909520 | tf_op jit(solution)/gta,gtb->gab/dot_general | solution.py:19
  1232.3 2.5 collective-permute-start.6
  1234.8 26.6 %fusion.87 = f32[2048,8192,1]{1,0,2:T(8,128)} fusion(bf16[1,128,8192]{2,1,0:T(8,128)(2,1)} %get-tuple-element.199, bf16[1,128,8192]{2,1,0:T(8,128)(2,1)} %get-tuple-element.197, s32[]{:T(128)S(6)} %multiply.32, bf16[1,2048,2048]{1,2,0:T(8,128)(2,1)} %bitcast.57, s32[]{:T(128)S(6)} %multiply.33), kind=kOutput, calls=%fused_computation.30.clone.1 | convolution fusion | flops 8594128896 | bytes 79691784 | tf_op jit(solution)/gta,gtb->gab/dot_general | solution.py:19
  1262.5 38.7 %collective-permute-start.7 = (bf16[1,128,8192]{2,1,0:T(8,128)(2,1)}, bf16[1,128,8192]{2,1,0:T(8,128)(2,1)}, u32[]{:S(2)}, u32[]{:S(2)}) collective-permute-start(bf16[1,128,8192]{2,1,0:T(8,128)(2,1)} %collective-permute-done.6), channel_id=13, source_target_pairs={{0,1},{1,2},{2,3},{3,4},{4,5},{5,6},{6,7},{7,8},{8,9},{9,10},{10,1... | collective-permute-start | bytes 6291464 | tf_op jit(solution)/gta,gtb->gab/dot_general | solution.py:19
  1301.2 66.3 %bitcast_add_fusion.3 = f32[2048,8192]{1,0:T(8,128)} fusion(f32[2048,8192,1]{1,0,2:T(8,128)} %fusion.87, f32[2048,8192]{1,0:T(8,128)} %get-tuple-element.198, pred[]{:T(512)S(6)} %compare.13, bf16[1,128,8192]{2,1,0:T(8,128)(2,1)} %collective-permute-done.6, bf16[1,128,8192]{2,1,0:T(8,128)(2,1)S(1)} %collective-permute-done.4, s32[]{:T(128)S(6)} %multiply.34, ...), kind=kOutput, calls=%fused_computation.24.clone.3 | convolution fusion | flops 8644460544 | bytes 213909520 | tf_op jit(solution)/gta,gtb->gab/dot_general | solution.py:19
  1367.5 51.0 %copy.1 = bf16[2048,8192]{0,1:T(8,128)(2,1)} copy(f32[2048,8192]{1,0:T(8,128)} %get-tuple-element.14) | data formatting | bytes 100663296 | tf_op jit(solution)/gta,gtb->gab/dot_general | solution.py:19
  1418.5 3.4 add.32
  (64 shorter events, 16.0 us)
Async XLA Ops:
  7.2 151.7 %all-gather.5.cloned.1.call-start = ((), (), s32[]{:S(2)}) async-start(), calls=%async_computation | async-start | bytes 35651584 | tf_op args[1]
  10.3 837.3 %collective-permute-start.9 = (bf16[1,128,8192]{2,1,0:T(8,128)(2,1)}, bf16[1,128,8192]{2,1,0:T(8,128)(2,1)}, u32[]{:S(2)}, u32[]{:S(2)}) collective-permute-start(bf16[1,128,8192]{2,1,0:T(8,128)(2,1)} %bitcast), channel_id=9, source_target_pairs={{0,1},{1,2},{2,3},{3,4},{4,5},{5,6},{6,7},{7,8},{8,9},{9,10},{10,1... | collective-permute-start | bytes 6291464 | tf_op jit(solution)/gta,gtb->gab/dot_general | solution.py:19
  158.9 104.0 %copy-start = (bf16[128,8192]{1,0:T(8,128)(2,1)S(1)}, bf16[128,8192]{1,0:T(8,128)(2,1)}, u32[]{:S(2)}) copy-start(bf16[128,8192]{1,0:T(8,128)(2,1)} %custom-call) | copy-start | bytes 6291460
  264.4 27.3 %collective-permute-start = (bf16[128,8192]{1,0:T(8,128)(2,1)}, bf16[128,8192]{1,0:T(8,128)(2,1)}, u32[]{:S(2)}, u32[]{:S(2)}) collective-permute-start(bf16[128,8192]{1,0:T(8,128)(2,1)} %broadcast_select_fusion.4), channel_id=4, source_target_pairs={{0,1},{1,2},{2,3},{3,4},{4,5},{5,6},{6,7},{7,8},{8,9},{9,10},{10,1... | collective-permute-start | bytes 6291464 | tf_op jit(solution)/dot_general | solution.py:14
  266.1 26.9 %collective-permute-start.1 = (bf16[128,8192]{1,0:T(8,128)(2,1)}, bf16[128,8192]{1,0:T(8,128)(2,1)S(1)}, u32[]{:S(2)}, u32[]{:S(2)}) collective-permute-start(bf16[128,8192]{1,0:T(8,128)(2,1)} %broadcast_select_fusion.5), channel_id=3, source_target_pairs={{0,15},{1,0},{2,1},{3,2},{4,3},{5,4},{6,5},{7,6},{8,7},{9,8},{10,9... | collective-permute-start | bytes 6291464 | tf_op jit(solution)/dot_general | solution.py:14
  298.3 60.2 %collective-permute-start.2 = (bf16[128,8192]{1,0:T(8,128)(2,1)}, bf16[128,8192]{1,0:T(8,128)(2,1)S(1)}, u32[]{:S(2)}, u32[]{:S(2)}) collective-permute-start(bf16[128,8192]{1,0:T(8,128)(2,1)} %get-tuple-element.141), channel_id=6, source_target_pairs={{0,1},{1,2},{2,3},{3,4},{4,5},{5,6},{6,7},{7,8},{8,9},{9,10},{10,1... | collective-permute-start | bytes 6291464 | tf_op jit(solution)/dot_general | solution.py:14
  341.7 23.6 %collective-permute-start.3 = (bf16[128,8192]{1,0:T(8,128)(2,1)}, bf16[128,8192]{1,0:T(8,128)(2,1)}, u32[]{:S(2)}, u32[]{:S(2)}) collective-permute-start(bf16[128,8192]{1,0:T(8,128)(2,1)} %get-tuple-element.142), channel_id=5, source_target_pairs={{0,15},{1,0},{2,1},{3,2},{4,3},{5,4},{6,5},{7,6},{8,7},{9,8},{10,9... | collective-permute-start | bytes 6291464 | tf_op jit(solution)/dot_general | solution.py:14
  358.5 1.3 copy-start.3
  373.6 41.4 %collective-permute-start = (bf16[128,8192]{1,0:T(8,128)(2,1)}, bf16[128,8192]{1,0:T(8,128)(2,1)}, u32[]{:S(2)}, u32[]{:S(2)}) collective-permute-start(bf16[128,8192]{1,0:T(8,128)(2,1)} %broadcast_select_fusion.4), channel_id=4, source_target_pairs={{0,1},{1,2},{2,3},{3,4},{4,5},{5,6},{6,7},{7,8},{8,9},{9,10},{10,1... | collective-permute-start | bytes 6291464 | tf_op jit(solution)/dot_general | solution.py:14
  398.2 23.6 %collective-permute-start.1 = (bf16[128,8192]{1,0:T(8,128)(2,1)}, bf16[128,8192]{1,0:T(8,128)(2,1)S(1)}, u32[]{:S(2)}, u32[]{:S(2)}) collective-permute-start(bf16[128,8192]{1,0:T(8,128)(2,1)} %broadcast_select_fusion.5), channel_id=3, source_target_pairs={{0,15},{1,0},{2,1},{3,2},{4,3},{5,4},{6,5},{7,6},{8,7},{9,8},{10,9... | collective-permute-start | bytes 6291464 | tf_op jit(solution)/dot_general | solution.py:14
  427.1 39.3 %collective-permute-start.2 = (bf16[128,8192]{1,0:T(8,128)(2,1)}, bf16[128,8192]{1,0:T(8,128)(2,1)S(1)}, u32[]{:S(2)}, u32[]{:S(2)}) collective-permute-start(bf16[128,8192]{1,0:T(8,128)(2,1)} %get-tuple-element.141), channel_id=6, source_target_pairs={{0,1},{1,2},{2,3},{3,4},{4,5},{5,6},{6,7},{7,8},{8,9},{9,10},{10,1... | collective-permute-start | bytes 6291464 | tf_op jit(solution)/dot_general | solution.py:14
  449.6 23.6 %collective-permute-start.3 = (bf16[128,8192]{1,0:T(8,128)(2,1)}, bf16[128,8192]{1,0:T(8,128)(2,1)}, u32[]{:S(2)}, u32[]{:S(2)}) collective-permute-start(bf16[128,8192]{1,0:T(8,128)(2,1)} %get-tuple-element.142), channel_id=5, source_target_pairs={{0,15},{1,0},{2,1},{3,2},{4,3},{5,4},{6,5},{7,6},{8,7},{9,8},{10,9... | collective-permute-start | bytes 6291464 | tf_op jit(solution)/dot_general | solution.py:14
  466.4 1.3 copy-start.3
  481.5 42.4 %collective-permute-start = (bf16[128,8192]{1,0:T(8,128)(2,1)}, bf16[128,8192]{1,0:T(8,128)(2,1)}, u32[]{:S(2)}, u32[]{:S(2)}) collective-permute-start(bf16[128,8192]{1,0:T(8,128)(2,1)} %broadcast_select_fusion.4), channel_id=4, source_target_pairs={{0,1},{1,2},{2,3},{3,4},{4,5},{5,6},{6,7},{7,8},{8,9},{9,10},{10,1... | collective-permute-start | bytes 6291464 | tf_op jit(solution)/dot_general | solution.py:14
  507.1 23.6 %collective-permute-start.1 = (bf16[128,8192]{1,0:T(8,128)(2,1)}, bf16[128,8192]{1,0:T(8,128)(2,1)S(1)}, u32[]{:S(2)}, u32[]{:S(2)}) collective-permute-start(bf16[128,8192]{1,0:T(8,128)(2,1)} %broadcast_select_fusion.5), channel_id=3, source_target_pairs={{0,15},{1,0},{2,1},{3,2},{4,3},{5,4},{6,5},{7,6},{8,7},{9,8},{10,9... | collective-permute-start | bytes 6291464 | tf_op jit(solution)/dot_general | solution.py:14
  536.0 39.6 %collective-permute-start.2 = (bf16[128,8192]{1,0:T(8,128)(2,1)}, bf16[128,8192]{1,0:T(8,128)(2,1)S(1)}, u32[]{:S(2)}, u32[]{:S(2)}) collective-permute-start(bf16[128,8192]{1,0:T(8,128)(2,1)} %get-tuple-element.141), channel_id=6, source_target_pairs={{0,1},{1,2},{2,3},{3,4},{4,5},{5,6},{6,7},{7,8},{8,9},{9,10},{10,1... | collective-permute-start | bytes 6291464 | tf_op jit(solution)/dot_general | solution.py:14
  558.9 23.6 %collective-permute-start.3 = (bf16[128,8192]{1,0:T(8,128)(2,1)}, bf16[128,8192]{1,0:T(8,128)(2,1)}, u32[]{:S(2)}, u32[]{:S(2)}) collective-permute-start(bf16[128,8192]{1,0:T(8,128)(2,1)} %get-tuple-element.142), channel_id=5, source_target_pairs={{0,15},{1,0},{2,1},{3,2},{4,3},{5,4},{6,5},{7,6},{8,7},{9,8},{10,9... | collective-permute-start | bytes 6291464 | tf_op jit(solution)/dot_general | solution.py:14
  575.6 1.3 copy-start.3
  590.8 43.5 %collective-permute-start = (bf16[128,8192]{1,0:T(8,128)(2,1)}, bf16[128,8192]{1,0:T(8,128)(2,1)}, u32[]{:S(2)}, u32[]{:S(2)}) collective-permute-start(bf16[128,8192]{1,0:T(8,128)(2,1)} %broadcast_select_fusion.4), channel_id=4, source_target_pairs={{0,1},{1,2},{2,3},{3,4},{4,5},{5,6},{6,7},{7,8},{8,9},{9,10},{10,1... | collective-permute-start | bytes 6291464 | tf_op jit(solution)/dot_general | solution.py:14
  617.5 23.6 %collective-permute-start.1 = (bf16[128,8192]{1,0:T(8,128)(2,1)}, bf16[128,8192]{1,0:T(8,128)(2,1)S(1)}, u32[]{:S(2)}, u32[]{:S(2)}) collective-permute-start(bf16[128,8192]{1,0:T(8,128)(2,1)} %broadcast_select_fusion.5), channel_id=3, source_target_pairs={{0,15},{1,0},{2,1},{3,2},{4,3},{5,4},{6,5},{7,6},{8,7},{9,8},{10,9... | collective-permute-start | bytes 6291464 | tf_op jit(solution)/dot_general | solution.py:14
  646.4 39.6 %collective-permute-start.2 = (bf16[128,8192]{1,0:T(8,128)(2,1)}, bf16[128,8192]{1,0:T(8,128)(2,1)S(1)}, u32[]{:S(2)}, u32[]{:S(2)}) collective-permute-start(bf16[128,8192]{1,0:T(8,128)(2,1)} %get-tuple-element.141), channel_id=6, source_target_pairs={{0,1},{1,2},{2,3},{3,4},{4,5},{5,6},{6,7},{7,8},{8,9},{9,10},{10,1... | collective-permute-start | bytes 6291464 | tf_op jit(solution)/dot_general | solution.py:14
  669.3 23.6 %collective-permute-start.3 = (bf16[128,8192]{1,0:T(8,128)(2,1)}, bf16[128,8192]{1,0:T(8,128)(2,1)}, u32[]{:S(2)}, u32[]{:S(2)}) collective-permute-start(bf16[128,8192]{1,0:T(8,128)(2,1)} %get-tuple-element.142), channel_id=5, source_target_pairs={{0,15},{1,0},{2,1},{3,2},{4,3},{5,4},{6,5},{7,6},{8,7},{9,8},{10,9... | collective-permute-start | bytes 6291464 | tf_op jit(solution)/dot_general | solution.py:14
  686.0 1.3 copy-start.3
  698.1 137.2 %copy-start.1 = (bf16[128,8192]{1,0:T(8,128)(2,1)}, bf16[128,8192]{1,0:T(8,128)(2,1)S(1)}, u32[]{:S(2)}) copy-start(bf16[128,8192]{1,0:T(8,128)(2,1)S(1)} %get-tuple-element.12) | copy-start | bytes 6291460
  698.1 720.4 %collective-permute-start.8 = (bf16[128,8192]{1,0:T(8,128)(2,1)}, bf16[128,8192]{1,0:T(8,128)(2,1)}, u32[]{:S(2)}, u32[]{:S(2)}) collective-permute-start(bf16[128,8192]{1,0:T(8,128)(2,1)} %get-tuple-element.13), channel_id=7, source_target_pairs={{0,1},{1,2},{2,3},{3,4},{4,5},{5,6},{6,7},{7,8},{8,9},{9,10},{10,1... | collective-permute-start | bytes 6291464 | tf_op jit(solution)/dot_general | solution.py:14
  847.7 29.2 %collective-permute-start.4 = (bf16[1,128,8192]{2,1,0:T(8,128)(2,1)}, bf16[1,128,8192]{2,1,0:T(8,128)(2,1)S(1)}, u32[]{:S(2)}, u32[]{:S(2)}) collective-permute-start(bf16[1,128,8192]{2,1,0:T(8,128)(2,1)} %get-tuple-element.197), channel_id=10, source_target_pairs={{0,15},{1,0},{2,1},{3,2},{4,3},{5,4},{6,5},{7,6},{8,7},{9,8},{10,9... | collective-permute-start | bytes 6291464 | tf_op jit(solution)/gta,gtb->gab/dot_general | solution.py:19
  847.7 31.3 %collective-permute-start.6 = (bf16[1,128,8192]{2,1,0:T(8,128)(2,1)}, bf16[1,128,8192]{2,1,0:T(8,128)(2,1)}, u32[]{:S(2)}, u32[]{:S(2)}) collective-permute-start(bf16[1,128,8192]{2,1,0:T(8,128)(2,1)} %get-tuple-element.199), channel_id=11, source_target_pairs={{0,1},{1,2},{2,3},{3,4},{4,5},{5,6},{6,7},{7,8},{8,9},{9,10},{10,1... | collective-permute-start | bytes 6291464 | tf_op jit(solution)/gta,gtb->gab/dot_general | solution.py:19
  876.8 83.7 %collective-permute-start.5 = (bf16[1,128,8192]{2,1,0:T(8,128)(2,1)S(1)}, bf16[1,128,8192]{2,1,0:T(8,128)(2,1)}, u32[]{:S(2)}, u32[]{:S(2)}) collective-permute-start(bf16[1,128,8192]{2,1,0:T(8,128)(2,1)S(1)} %collective-permute-done.4), channel_id=12, source_target_pairs={{0,15},{1,0},{2,1},{3,2},{4,3},{5,4},{6,5},{7,6},{8,7},{9,8},{10,9... | collective-permute-start | bytes 6291464 | tf_op jit(solution)/gta,gtb->gab/dot_general | solution.py:19
  879.0 81.5 %collective-permute-start.7 = (bf16[1,128,8192]{2,1,0:T(8,128)(2,1)}, bf16[1,128,8192]{2,1,0:T(8,128)(2,1)}, u32[]{:S(2)}, u32[]{:S(2)}) collective-permute-start(bf16[1,128,8192]{2,1,0:T(8,128)(2,1)} %collective-permute-done.6), channel_id=13, source_target_pairs={{0,1},{1,2},{2,3},{3,4},{4,5},{5,6},{6,7},{7,8},{8,9},{9,10},{10,1... | collective-permute-start | bytes 6291464 | tf_op jit(solution)/gta,gtb->gab/dot_general | solution.py:19
  960.5 29.2 %collective-permute-start.4 = (bf16[1,128,8192]{2,1,0:T(8,128)(2,1)}, bf16[1,128,8192]{2,1,0:T(8,128)(2,1)S(1)}, u32[]{:S(2)}, u32[]{:S(2)}) collective-permute-start(bf16[1,128,8192]{2,1,0:T(8,128)(2,1)} %get-tuple-element.197), channel_id=10, source_target_pairs={{0,15},{1,0},{2,1},{3,2},{4,3},{5,4},{6,5},{7,6},{8,7},{9,8},{10,9... | collective-permute-start | bytes 6291464 | tf_op jit(solution)/gta,gtb->gab/dot_general | solution.py:19
  960.6 30.4 %collective-permute-start.6 = (bf16[1,128,8192]{2,1,0:T(8,128)(2,1)}, bf16[1,128,8192]{2,1,0:T(8,128)(2,1)}, u32[]{:S(2)}, u32[]{:S(2)}) collective-permute-start(bf16[1,128,8192]{2,1,0:T(8,128)(2,1)} %get-tuple-element.199), channel_id=11, source_target_pairs={{0,1},{1,2},{2,3},{3,4},{4,5},{5,6},{6,7},{7,8},{8,9},{9,10},{10,1... | collective-permute-start | bytes 6291464 | tf_op jit(solution)/gta,gtb->gab/dot_general | solution.py:19
  989.7 106.1 %collective-permute-start.5 = (bf16[1,128,8192]{2,1,0:T(8,128)(2,1)S(1)}, bf16[1,128,8192]{2,1,0:T(8,128)(2,1)}, u32[]{:S(2)}, u32[]{:S(2)}) collective-permute-start(bf16[1,128,8192]{2,1,0:T(8,128)(2,1)S(1)} %collective-permute-done.4), channel_id=12, source_target_pairs={{0,15},{1,0},{2,1},{3,2},{4,3},{5,4},{6,5},{7,6},{8,7},{9,8},{10,9... | collective-permute-start | bytes 6291464 | tf_op jit(solution)/gta,gtb->gab/dot_general | solution.py:19
  990.9 104.8 %collective-permute-start.7 = (bf16[1,128,8192]{2,1,0:T(8,128)(2,1)}, bf16[1,128,8192]{2,1,0:T(8,128)(2,1)}, u32[]{:S(2)}, u32[]{:S(2)}) collective-permute-start(bf16[1,128,8192]{2,1,0:T(8,128)(2,1)} %collective-permute-done.6), channel_id=13, source_target_pairs={{0,1},{1,2},{2,3},{3,4},{4,5},{5,6},{6,7},{7,8},{8,9},{9,10},{10,1... | collective-permute-start | bytes 6291464 | tf_op jit(solution)/gta,gtb->gab/dot_general | solution.py:19
  1095.8 29.2 %collective-permute-start.4 = (bf16[1,128,8192]{2,1,0:T(8,128)(2,1)}, bf16[1,128,8192]{2,1,0:T(8,128)(2,1)S(1)}, u32[]{:S(2)}, u32[]{:S(2)}) collective-permute-start(bf16[1,128,8192]{2,1,0:T(8,128)(2,1)} %get-tuple-element.197), channel_id=10, source_target_pairs={{0,15},{1,0},{2,1},{3,2},{4,3},{5,4},{6,5},{7,6},{8,7},{9,8},{10,9... | collective-permute-start | bytes 6291464 | tf_op jit(solution)/gta,gtb->gab/dot_general | solution.py:19
  1095.8 30.6 %collective-permute-start.6 = (bf16[1,128,8192]{2,1,0:T(8,128)(2,1)}, bf16[1,128,8192]{2,1,0:T(8,128)(2,1)}, u32[]{:S(2)}, u32[]{:S(2)}) collective-permute-start(bf16[1,128,8192]{2,1,0:T(8,128)(2,1)} %get-tuple-element.199), channel_id=11, source_target_pairs={{0,1},{1,2},{2,3},{3,4},{4,5},{5,6},{6,7},{7,8},{8,9},{9,10},{10,1... | collective-permute-start | bytes 6291464 | tf_op jit(solution)/gta,gtb->gab/dot_general | solution.py:19
  1125.0 107.2 %collective-permute-start.5 = (bf16[1,128,8192]{2,1,0:T(8,128)(2,1)S(1)}, bf16[1,128,8192]{2,1,0:T(8,128)(2,1)}, u32[]{:S(2)}, u32[]{:S(2)}) collective-permute-start(bf16[1,128,8192]{2,1,0:T(8,128)(2,1)S(1)} %collective-permute-done.4), channel_id=12, source_target_pairs={{0,15},{1,0},{2,1},{3,2},{4,3},{5,4},{6,5},{7,6},{8,7},{9,8},{10,9... | collective-permute-start | bytes 6291464 | tf_op jit(solution)/gta,gtb->gab/dot_general | solution.py:19
  1126.4 105.8 %collective-permute-start.7 = (bf16[1,128,8192]{2,1,0:T(8,128)(2,1)}, bf16[1,128,8192]{2,1,0:T(8,128)(2,1)}, u32[]{:S(2)}, u32[]{:S(2)}) collective-permute-start(bf16[1,128,8192]{2,1,0:T(8,128)(2,1)} %collective-permute-done.6), channel_id=13, source_target_pairs={{0,1},{1,2},{2,3},{3,4},{4,5},{5,6},{6,7},{7,8},{8,9},{9,10},{10,1... | collective-permute-start | bytes 6291464 | tf_op jit(solution)/gta,gtb->gab/dot_general | solution.py:19
  1232.2 29.2 %collective-permute-start.4 = (bf16[1,128,8192]{2,1,0:T(8,128)(2,1)}, bf16[1,128,8192]{2,1,0:T(8,128)(2,1)S(1)}, u32[]{:S(2)}, u32[]{:S(2)}) collective-permute-start(bf16[1,128,8192]{2,1,0:T(8,128)(2,1)} %get-tuple-element.197), channel_id=10, source_target_pairs={{0,15},{1,0},{2,1},{3,2},{4,3},{5,4},{6,5},{7,6},{8,7},{9,8},{10,9... | collective-permute-start | bytes 6291464 | tf_op jit(solution)/gta,gtb->gab/dot_general | solution.py:19
  1232.3 30.2 %collective-permute-start.6 = (bf16[1,128,8192]{2,1,0:T(8,128)(2,1)}, bf16[1,128,8192]{2,1,0:T(8,128)(2,1)}, u32[]{:S(2)}, u32[]{:S(2)}) collective-permute-start(bf16[1,128,8192]{2,1,0:T(8,128)(2,1)} %get-tuple-element.199), channel_id=11, source_target_pairs={{0,1},{1,2},{2,3},{3,4},{4,5},{5,6},{6,7},{7,8},{8,9},{9,10},{10,1... | collective-permute-start | bytes 6291464 | tf_op jit(solution)/gta,gtb->gab/dot_general | solution.py:19
  1261.4 106.1 %collective-permute-start.5 = (bf16[1,128,8192]{2,1,0:T(8,128)(2,1)S(1)}, bf16[1,128,8192]{2,1,0:T(8,128)(2,1)}, u32[]{:S(2)}, u32[]{:S(2)}) collective-permute-start(bf16[1,128,8192]{2,1,0:T(8,128)(2,1)S(1)} %collective-permute-done.4), channel_id=12, source_target_pairs={{0,15},{1,0},{2,1},{3,2},{4,3},{5,4},{6,5},{7,6},{8,7},{9,8},{10,9... | collective-permute-start | bytes 6291464 | tf_op jit(solution)/gta,gtb->gab/dot_general | solution.py:19
  1262.5 105.0 %collective-permute-start.7 = (bf16[1,128,8192]{2,1,0:T(8,128)(2,1)}, bf16[1,128,8192]{2,1,0:T(8,128)(2,1)}, u32[]{:S(2)}, u32[]{:S(2)}) collective-permute-start(bf16[1,128,8192]{2,1,0:T(8,128)(2,1)} %collective-permute-done.6), channel_id=13, source_target_pairs={{0,1},{1,2},{2,3},{3,4},{4,5},{5,6},{6,7},{7,8},{8,9},{9,10},{10,1... | collective-permute-start | bytes 6291464 | tf_op jit(solution)/gta,gtb->gab/dot_general | solution.py:19
  1367.5 51.0 %copy-start.2 = (bf16[128,8192]{1,0:T(8,128)(2,1)S(1)}, bf16[128,8192]{1,0:T(8,128)(2,1)}, u32[]{:S(2)}) copy-start(bf16[128,8192]{1,0:T(8,128)(2,1)} %copy-done.1) | copy-start | bytes 6291460
Sparse Core Ops, SparseCore 0:
  10.5 148.3 all-gather.4
where the time goes:
time: 1440 us; the launch traced here: 1430 us
  matrix products  700 us (49%)
  starting transfers between devices  383 us (27%)
  waiting for transfers between devices  197 us (14%)
  local copies, waits for them, and re-layouts  71.8 us (5%)
  other arithmetic  61.9 us (4%)
  between operations  14.4 us (1%)
    dot_general x9, matrix products, by_group(): jnp.einsum('gta,gtb->gab', a, b, preferred_element_type=jnp.float32)  462 us
    dot_general x17, starting transfers between devices, step(): dx = jnp.dot(d_pre, w_in.T)  212 us
    dot_general x17, starting transfers between devices, by_group(): jnp.einsum('gta,gtb->gab', a, b, preferred_element_type=jnp.float32)  172 us
    unnamed x2, waiting for transfers between devices  148 us
    dot_general x8, matrix products, step(): dx = jnp.dot(d_pre, w_in.T)  134 us
    dot_general x1, matrix products, step(): d_hidden = jnp.dot(dy, w_down.T, preferred_element_type=jnp.float32)  104 us
    dot_general x1, local copies, waits for them, and re-layouts, by_group(): jnp.einsum('gta,gtb->gab', a, b, preferred_element_type=jnp.float32)  51 us
    dot_general x17, waiting for transfers between devices, step(): dx = jnp.dot(d_pre, w_in.T)  49.6 us
  transfers between devices with their start and end apart: 35, of which 10 were waited for; matrix products, arithmetic and copies ran while one was open for 58% of the time, Pallas kernels for 0%

commit v1 on v0

v1 whole, which is shorter than its diff:
```python
import functools

import jax
import jax.numpy as jnp
from jax import lax
from jax.experimental import pallas as pl
from jax.experimental.pallas import tpu as pltpu
from jax.sharding import PartitionSpec as P

VMEM_LIMIT = 60 * 1024 * 1024


def act(pre):
    return jax.nn.gelu(pre)


def params(*semantics):
    return pltpu.CompilerParams(dimension_semantics=semantics, vmem_limit_bytes=VMEM_LIMIT)


def cost(m, n, k):
    return pl.CostEstimate(flops=2 * m * n * k, bytes_accessed=2 * (m * k + k * n + m * n), transcendentals=0)


def pre_kernel(dy_ref, w_ref, pre_ref, d_pre_ref, hidden_ref):
    d_hidden = lax.dot_general(dy_ref[...], w_ref[...], (((1,), (1,)), ((), ())), preferred_element_type=jnp.float32)
    hidden, back = jax.vjp(act, pre_ref[...].astype(jnp.float32))
    d_pre_ref[...] = back(d_hidden)[0].astype(jnp.bfloat16)
    hidden_ref[...] = hidden.astype(jnp.bfloat16)


def pre_grad(dy, w_down, pre, tm=512, tn=512):
    (m, k), n = dy.shape, w_down.shape[0]
    return pl.pallas_call(
        pre_kernel,
        grid=(n // tn, m // tm),
        in_specs=[
            pl.BlockSpec((tm, k), lambda j, i: (i, 0)),
            pl.BlockSpec((tn, k), lambda j, i: (j, 0)),
            pl.BlockSpec((tm, tn), lambda j, i: (i, j)),
        ],
        out_specs=[pl.BlockSpec((tm, tn), lambda j, i: (i, j))] * 2,
        out_shape=[jax.ShapeDtypeStruct((m, n), jnp.bfloat16)] * 2,
        compiler_params=params("arbitrary", "arbitrary"),
        cost_estimate=cost(m, n, k),
        name="pre_grad",
    )(dy, w_down, pre)


def dot_kernel(dims, a_ref, b_ref, o_ref):
    o_ref[...] = lax.dot_general(a_ref[...], b_ref[...], (dims, ((), ())), preferred_element_type=jnp.float32).astype(jnp.bfloat16)


def matmul_nt(a, b, tm=1024, tn=1024):
    (m, k), n = a.shape, b.shape[0]
    return pl.pallas_call(
        functools.partial(dot_kernel, ((1,), (1,))),
        grid=(m // tm, n // tn),
        in_specs=[pl.BlockSpec((tm, k), lambda i, j: (i, 0)), pl.BlockSpec((tn, k), lambda i, j: (j, 0))],
        out_specs=pl.BlockSpec((tm, tn), lambda i, j: (i, j)),
        out_shape=jax.ShapeDtypeStruct((m, n), jnp.bfloat16),
        compiler_params=params("arbitrary", "arbitrary"),
        cost_estimate=cost(m, n, k),
        name="nt",
    )(a, b)


def matmul_tn(a, b, name, tm=1024, tn=1024):
    (k, m), n = a.shape, b.shape[1]
    return pl.pallas_call(
        functools.partial(dot_kernel, ((0,), (0,))),
        grid=(m // tm, n // tn),
        in_specs=[pl.BlockSpec((k, tm), lambda i, j: (0, i)), pl.BlockSpec((k, tn), lambda i, j: (0, j))],
        out_specs=pl.BlockSpec((tm, tn), lambda i, j: (i, j)),
        out_shape=jax.ShapeDtypeStruct((m, n), jnp.bfloat16),
        compiler_params=params("arbitrary", "arbitrary"),
        cost_estimate=cost(m, n, k),
        name=name,
    )(a, b)


def solution(mesh):
    def body(x, dy, pre, w_in, w_down):
        dy_all = lax.all_gather(dy, "tp", axis=0, tiled=True)
        x_all = lax.all_gather(x, "tp", axis=0, tiled=True)
        d_pre, hidden = pre_grad(dy_all, w_down, pre)
        dx = lax.psum_scatter(matmul_nt(d_pre, w_in), "tp", scatter_dimension=0, tiled=True)
        dw_down = matmul_tn(hidden, dy_all, "dw_down")
        dw_in = matmul_tn(x_all, d_pre, "dw_in")
        return dx, dw_in, dw_down

    return jax.shard_map(
        body,
        mesh=mesh,
        in_specs=(P(("dp", "tp")), P(("dp", "tp")), P("dp", "tp"), P(None, "tp"), P("tp", None)),
        out_specs=(P(("dp", "tp")), P("dp", "tp"), P(("dp", "tp"))),
        check_vma=False,
    )
```

time: 1440 us -> 666 us (0.46)
  matrix products: 700 us -> 0 us
  starting transfers between devices: 383 us -> 0.11 us
  Pallas kernels: 0 us -> 326 us
  waiting for transfers between devices: 197 us -> 322 us
  local copies, waits for them, and re-layouts: 71.8 us -> 0 us
  other arithmetic: 61.9 us -> 0 us
    dot_general x18 -> x0, matrix products: 700 us -> none  [the longest x9 462 us: by_group(): jnp.einsum('gta,gtb->gab', a, b, preferred_element_type=jnp.float32)]
    dot_general x34 -> x0, starting transfers between devices: 383 us -> none  [the longest x17 212 us: step(): dx = jnp.dot(d_pre, w_in.T)]
    pallas_call x0 -> x4, Pallas kernels: none -> 326 us  [the longest x2 155 us: matmul_tn(): pl.pallas_call(functools.partial(dot_kernel, ((0,), (0,))), grid=(m // tm...]
    reduce_scatter x0 -> x1, waiting for transfers between devices: none -> 185 us  [body(): lax.psum_scatter(matmul_nt(d_pre, w_in), 'tp', scatter_dimension=0, tiled...]
    unnamed x2 -> x3, waiting for transfers between devices: 148 us -> 1.39 us
    all_gather x0 -> x2, waiting for transfers between devices: none -> 136 us  [the longest x1 136 us: body(): dy_all = lax.all_gather(dy, 'tp', axis=0, tiled=True)]
    dot_general x17 -> x0, other arithmetic: 61.9 us -> none  [the longest x9 45.4 us: step(): dx = jnp.dot(d_pre, w_in.T)]
    dot_general x9 -> x0, local copies, waits for them, and re-layouts: 56.3 us -> none  [the longest x1 51 us: by_group(): jnp.einsum('gta,gtb->gab', a, b, preferred_element_type=jnp.float32)]
  transfers between devices with their start and end apart: 35 -> 3, of which waited for: 10 -> 2; matrix products, arithmetic and copies ran while one was open for 58% -> 0% of each run, Pallas kernels for 0% -> 49%
where the time goes in v1:
time: 666 us; the launch traced here: 663 us
  Pallas kernels  326 us (49%)
  waiting for transfers between devices  322 us (48%)
  between operations  13.7 us (2%)
    reduce_scatter x1, waiting for transfers between devices, body(): lax.psum_scatter(matmul_nt(d_pre, w_in), 'tp', scatter_dimension=0, tiled...  185 us
    pallas_call x2, Pallas kernels, matmul_tn(): pl.pallas_call(functools.partial(dot_kernel, ((0,), (0,))), grid=(m // tm...  155 us
    all_gather x1, waiting for transfers between devices, body(): dy_all = lax.all_gather(dy, 'tp', axis=0, tiled=True)  136 us
    pallas_call x1, Pallas kernels, pre_grad(): pl.pallas_call(pre_kernel, grid=(n // tn, m // tm), in_specs=[pl.BlockSpe...  93.3 us
    pallas_call x1, Pallas kernels, matmul_nt(): pl.pallas_call(functools.partial(dot_kernel, ((1,), (1,))), grid=(m // tm...  77.6 us
  transfers between devices with their start and end apart: 3, of which 2 were waited for; matrix products, arithmetic and copies ran while one was open for 0% of the time, Pallas kernels for 49%

profile of v1, /device:TPU:0, one launch (start us, length us, event | category | flops | bytes accessed | tf_op | source)
XLA Modules:
  0.0 662.7 jit_solution(4907446225185454223)
XLA Ops:
  7.2 0.0 all-gather.3.cloned.1.call-start
  7.2 0.7 all-gather.3.cloned.1.call-update
  7.9 0.0 all-gather.5.cloned.1.call-start
  7.9 0.7 all-gather.5.cloned.1.call-update
  8.6 0.0 reduce-scatter.2.cloned.1.call-start
  8.7 135.7 %all-gather.3.cloned.1.call-done.dy_ref.b_ref = bf16[2048,8192]{1,0:T(8,128)(2,1)} async-done(((bf16[128,8192]{1,0:T(8,128)(2,1)}), bf16[2048,8192]{1,0:T(8,128)(2,1)}) %all-gather.3.cloned.1.call-update) | async-done | bytes 33554448 | tf_op jit(solution)/shard_map/all_gather | solution.py:84
  144.3 93.3 %pre_grad.1 = (bf16[2048,2048]{1,0:T(8,128)(2,1)}, bf16[2048,2048]{1,0:T(8,128)(2,1)}) custom-call(bf16[2048,8192]{1,0:T(8,128)(2,1)} %all-gather.3.cloned.1.call-done.dy_ref.b_ref, bf16[2048,8192]{1,0:T(8,128)(2,1)} %w_ref.1, bf16[2048,2048]{1,0:T(8,128)(2,1)} %pre_ref.1), custom_call_target="tpu_custom_call" | custom-call | flops 68719476736 | bytes 75497472 | tf_op jit(solution)/shard_map/pre_grad/pallas_call | solution.py:34
  237.6 77.6 %nt.1 = bf16[2048,8192]{1,0:T(8,128)(2,1)} custom-call(bf16[2048,2048]{1,0:T(8,128)(2,1)} %get-tuple-element.5.a_ref.b_ref, bf16[8192,2048]{1,0:T(8,128)(2,1)} %b_ref.1), custom_call_target="tpu_custom_call" | custom-call | flops 68719476736 | bytes 75497472 | tf_op jit(solution)/shard_map/nt/pallas_call | solution.py:56
  315.2 0.0 reduce-scatter.2.cloned.1.call-update
  315.3 77.6 %dw_down.1 = bf16[2048,8192]{1,0:T(8,128)(2,1)} custom-call(bf16[2048,2048]{1,0:T(8,128)(2,1)} %get-tuple-element.6.a_ref, bf16[2048,8192]{1,0:T(8,128)(2,1)} %all-gather.3.cloned.1.call-done.dy_ref.b_ref), custom_call_target="tpu_custom_call" | custom-call | flops 68719476736 | bytes 75497472 | tf_op jit(solution)/shard_map/dw_down/pallas_call | solution.py:70
  392.9 0.0 all-gather.5.cloned.1.call-done.a_ref
  392.9 77.8 %dw_in.1 = bf16[8192,2048]{1,0:T(8,128)(2,1)} custom-call(bf16[2048,8192]{1,0:T(8,128)(2,1)} %all-gather.5.cloned.1.call-done.a_ref, bf16[2048,2048]{1,0:T(8,128)(2,1)} %get-tuple-element.5.a_ref.b_ref), custom_call_target="tpu_custom_call" | custom-call | flops 68719476736 | bytes 75497472 | tf_op jit(solution)/shard_map/dw_in/pallas_call | solution.py:70
  470.7 185.4 %reduce-scatter.2.cloned.1.call-done = bf16[128,8192]{1,0:T(8,128)(2,1)} async-done(((bf16[2048,8192]{1,0:T(8,128)(2,1)}), bf16[128,8192]{1,0:T(8,128)(2,1)}) %reduce-scatter.2.cloned.1.call-update) | async-done | bytes 2097168 | tf_op jit(solution)/shard_map/reduce_scatter | solution.py:87
Async XLA Ops:
  7.2 137.2 %all-gather.3.cloned.1.call-start = ((), (), s32[]{:S(2)}) async-start(), calls=%async_computation.1 | async-start | bytes 35651584 | tf_op jit(solution)/shard_map/all_gather | solution.py:84
  7.9 385.0 %all-gather.5.cloned.1.call-start = ((), (), s32[]{:S(2)}) async-start(), calls=%async_computation.3 | async-start | bytes 35651584 | tf_op jit(solution)/shard_map/all_gather | solution.py:85
  8.6 647.5 %reduce-scatter.2.cloned.1.call-start = ((), (), s32[]{:S(2)}) async-start(), calls=%async_computation.2 | async-start | bytes 35651584 | tf_op jit(solution)/shard_map/reduce_scatter | solution.py:87
Sparse Core Ops, SparseCore 0:
  10.2 134.0 all-gather.2
  146.6 131.2 all-gather.4
  315.4 340.7 reduce-scatter.1

commit v2 on v0

v2 whole, which is shorter than its diff:
```python
import functools

import jax
import jax.numpy as jnp
from jax import lax
from jax.experimental import pallas as pl
from jax.experimental.pallas import tpu as pltpu
from jax.sharding import PartitionSpec as P

VMEM_LIMIT = 66_000_000
WEIGHT = (4, 2, 1)
F32, BF16 = jnp.float32, jnp.bfloat16
ANY = pl.BlockSpec(memory_space=pl.ANY)
CHIPS = [(a, b, c) for a in (0, 1) for b in (0, 1) for c in (0, 1)]


def act(pre):
    return jax.nn.gelu(pre)


def dot(a, b, dims):
    return lax.dot_general(a, b, (dims, ((), ())), preferred_element_type=F32)


NT, TN = ((1,), (1,)), ((0,), (0,))


def rows(start, size):
    return pl.ds(pl.multiple_of(start, 16), size)


def lanes(start, size):
    return pl.ds(pl.multiple_of(start, 128), size)


class Place:
    def __init__(self):
        me = lax.axis_index("tp")
        self.chip, self.core = lax.div(me, 2), lax.rem(me, 2)
        self.step = [w * (1 - 2 * lax.rem(lax.div(self.chip, w), 2)) for w in WEIGHT]
        self.sibling = self.device(self.chip, 1 - self.core)

    def chip_at(self, r):
        return self.chip + sum(self.step[d] * r[d] for d in range(3) if isinstance(r[d], jax.Array) or r[d])

    def device(self, chip, core):
        return {"tp": 2 * chip + core}

    def across(self, d):
        if isinstance(d, int):
            return self.device(self.chip + self.step[d], self.core)
        r = (lax.div(2 - d, 2), lax.rem(d, 2), lax.div(d, 2))
        return self.device(self.chip_at(r), self.core)

    def barrier(self):
        sem = pltpu.get_barrier_semaphore()
        for peer in [self.sibling] + [self.across(d) for d in range(3)]:
            pl.semaphore_signal(sem, inc=1, device_id=peer, device_id_type=pl.DeviceIdType.MESH)
        pl.semaphore_wait(sem, 4)


def remote(src, dst, send, recv, device):
    return pltpu.make_async_remote_copy(src, dst, send, recv, device_id=device, device_id_type=pl.DeviceIdType.MESH)


def order(p):
    return p, (p + 1) % 3, (p + 2) % 3


def across(*dims):
    return tuple(int(d in dims) for d in range(3))


class Gather:
    def __init__(self, place, src, dst, sems, base):
        self.place, self.src, self.dst = place, src, dst
        self.shard, width = src.shape
        self.send, self.recv, self.out, self.back = (functools.partial(lambda s, i: s.at[base + i], s) for s in sems)
        tiles = width // 128
        ends = [128 * (tiles * k // 3) for k in range(4)]
        self.columns = [pl.ds(ends[k], ends[k + 1] - ends[k]) for k in range(3)]

    def rows_of(self, r, core):
        return rows((2 * self.place.chip_at(r) + core) * self.shard, self.shard)

    def piece(self, p, r, core):
        return self.dst.at[self.rows_of(r, core), self.columns[p]]

    @staticmethod
    def index(p, r):
        return 8 * p + 4 * r[0] + 2 * r[1] + r[2]

    def hop(self, p, r):
        d = [d for d in order(p) if r[d]][-1]
        q = tuple(r[e] * (e != d) for e in range(3))
        dst = self.piece(p, q, self.place.core)
        src = dst if any(q) else self.src.at[:, self.columns[p]]
        i = self.index(p, r)
        return remote(src, dst, self.send(i), self.recv(i), self.place.across(d))

    def arrive(self, p, r):
        view, i = self.piece(p, r, self.place.core), self.index(p, r)
        remote(view, view, self.send(i), self.recv(i), self.place.sibling).wait_recv()

    def share(self, p, r):
        view, i = self.piece(p, r, self.place.core), self.index(p, r)
        return remote(view, view, self.out(i), self.back(i), self.place.sibling)

    def shared(self, p, r):
        view, i = self.piece(p, r, 1 - self.place.core), self.index(p, r)
        remote(view, view, self.out(i), self.back(i), self.place.sibling).wait_recv()

    def share_own(self):
        return remote(self.src, self.dst.at[self.rows_of((0, 0, 0), self.place.core)], self.out(0), self.back(0), self.place.sibling)

    def shared_own(self):
        view = self.dst.at[self.rows_of((0, 0, 0), 1 - self.place.core)]
        remote(view, view, self.out(0), self.back(0), self.place.sibling).wait_recv()

    def begin(self):
        self.share_own().start()
        for k in range(3):
            for d in range(3):
                self.hop((d - k) % 3, across(d)).start()

    def act(self, n):
        for p in range(3):
            a, b, c = order(p)
            seq = [across(a), across(b), across(c), across(a, b), across(a, c), across(b, c), across(a, b, c)]
            follow = {0: [across(a, b), across(a, c)], 1: [across(b, c)], 3: [across(a, b, c)]}
            self.arrive(p, seq[n])
            for r in follow.get(n, []):
                self.hop(p, r).start()
            self.share(p, seq[n]).start()

    def drain(self):
        self.share_own().wait_send()
        for p in range(3):
            for r in CHIPS[1:]:
                self.hop(p, r).wait_send()
                self.share(p, r).wait_send()


NEAR = [(1, 0, 0), (0, 1, 0), (0, 0, 1)]
MIDDLE = [(1, 1, 0), (0, 1, 1), (1, 0, 1)]
FAR = [(1, 1, 1)]


def forward_kernel(x, dy, pre, w_down, x_all, dy_all, d_pre, hidden, slope, dw_down, send, recv, out, back, w_sem, load_sem, store_sem):
    place = Place()
    shard, width = dy.shape
    tokens, ff = pre.shape
    block = ff // 4
    place.barrier()
    sems = (send, recv, out, back)
    gather_dy = Gather(place, dy, dy_all, sems, 0)
    gather_x = Gather(place, x, x_all, sems, 24)
    gather_dy.begin()
    here = (0, 0, 0)

    def gradient(weights):
        def load_weights(j):
            part = pl.ds(j * block, block)
            return pltpu.make_async_copy(w_down.at[part], weights.at[part], w_sem.at[j])

        for j in range(4):
            load_weights(j).start()

        def gelu(pre_ref, hidden_ref, slope_ref):
            value, pull = jax.vjp(act, pre_ref[...].astype(F32))
            hidden_ref[...] = value.astype(BF16)
            slope_ref[...] = pull(jnp.ones_like(value))[0]

        spec = pl.BlockSpec((shard, ff), lambda i: (i, 0))
        pltpu.emit_pipeline(gelu, grid=(tokens // shard,), in_specs=[spec], out_specs=[spec, spec])(pre, hidden, slope)

        def chunks(lhs, slopes, result):
            def part(k):
                return pl.ds(k * shard, shard)

            def stores(chips):
                parts = [(r, core) for r in chips for core in (0, 1)]
                return [
                    pltpu.make_async_copy(
                        result.at[part(k)], d_pre.at[gather_dy.rows_of(r, place.core + core - 2 * core * place.core)], store_sem.at[k]
                    )
                    for k, (r, core) in enumerate(parts)
                ]

            def chunk(chips, before, first=False):
                shards = [(r, place.core + core - 2 * core * place.core) for r in chips for core in (0, 1)]
                copies = []
                for k, (r, core) in enumerate(shards):
                    src = dy if (first and k == 0) else dy_all.at[gather_dy.rows_of(r, core)]
                    copies.append(pltpu.make_async_copy(src, lhs.at[part(k)], load_sem.at[k]))
                    copies.append(pltpu.make_async_copy(slope.at[gather_dy.rows_of(r, core)], slopes.at[part(k)], load_sem.at[6 + k]))
                for copy in copies:
                    copy.start()
                for copy in copies:
                    copy.wait()
                if first:
                    own = pltpu.make_async_copy(lhs.at[part(0)], dy_all.at[gather_dy.rows_of(here, place.core)], load_sem.at[0])
                    own.start()
                    for j in range(4):
                        load_weights(j).wait()
                for copy in before:
                    copy.wait()
                size = len(shards) * shard

                @pl.loop(0, 4)
                def _(j):
                    columns = lanes(j * block, block)
                    d_hidden = dot(lhs[:size], weights[rows(j * block, block), :], NT)
                    result[:size, columns] = (d_hidden * slopes[:size, columns]).astype(BF16)

                if first:
                    own.wait()
                done = stores(chips)
                for copy in done:
                    copy.start()
                return done

            gather_dy.act(0)
            gather_dy.shared_own()
            done = chunk([here], [], first=True)
            gather_dy.act(1)
            gather_dy.act(2)
            for p in range(3):
                for r in NEAR:
                    gather_dy.shared(p, r)
            done = chunk(NEAR, done)
            gather_dy.act(3)
            gather_x.begin()
            gather_dy.act(4)
            gather_dy.act(5)
            for p in range(3):
                for r in MIDDLE:
                    gather_dy.shared(p, r)
            done = chunk(MIDDLE, done)
            gather_dy.act(6)
            for p in range(3):
                gather_dy.shared(p, FAR[0])
            done = chunk(FAR, done)
            own = [
                pltpu.make_async_copy(x, lhs.at[part(0)], load_sem.at[0]),
                pltpu.make_async_copy(lhs.at[part(0)], x_all.at[gather_dy.rows_of(here, place.core)], load_sem.at[0]),
            ]
            for copy in own:
                copy.start()
                copy.wait()
            for copy in done:
                copy.wait()

        pl.run_scoped(chunks, pltpu.VMEM((6 * shard, width), BF16), pltpu.VMEM((6 * shard, ff), F32), pltpu.VMEM((6 * shard, ff), BF16))

    pl.run_scoped(gradient, pltpu.VMEM((ff, width), BF16))

    tm, tn = ff // 2, width // 8

    def product(h_ref, dy_ref, o_ref):
        at = pl.program_id(0) * 8 + pl.program_id(1)
        for n, when in enumerate((1, 2, 5, 8, 11, 14)):
            @pl.when(at == when)
            def _():
                gather_x.act(n)

        o_ref[...] = dot(h_ref[...], dy_ref[...], TN).astype(BF16)

    pltpu.emit_pipeline(
        product,
        grid=(2, 8),
        in_specs=[pl.BlockSpec((tokens, tm), lambda i, j: (0, i)), pl.BlockSpec((tokens, tn), lambda i, j: (0, j))],
        out_specs=[pl.BlockSpec((tm, tn), lambda i, j: (i, j))],
    )(hidden, dy_all, dw_down)
    gather_x.act(6)
    gather_x.shared_own()
    for p in range(3):
        for r in CHIPS[1:]:
            gather_x.shared(p, r)
    gather_dy.drain()
    gather_x.drain()


def forward(x, dy, pre, w_down):
    shard, width = dy.shape
    tokens, ff = pre.shape
    dma = pltpu.SemaphoreType.DMA
    whole = jax.ShapeDtypeStruct((tokens, width), BF16)
    return pl.pallas_call(
        forward_kernel,
        in_specs=[ANY] * 4,
        out_specs=[ANY] * 6,
        out_shape=[
            whole,
            whole,
            jax.ShapeDtypeStruct((tokens, ff), BF16),
            jax.ShapeDtypeStruct((tokens, ff), BF16),
            jax.ShapeDtypeStruct((tokens, ff), F32),
            jax.ShapeDtypeStruct((ff, width), BF16),
        ],
        scratch_shapes=[dma((48,)), dma((48,)), dma((48,)), dma((48,)), dma((4,)), dma((12,)), dma((6,))],
        compiler_params=pltpu.CompilerParams(collective_id=0, has_side_effects=True, vmem_limit_bytes=VMEM_LIMIT),
        cost_estimate=pl.CostEstimate(flops=4 * tokens * ff * width, bytes_accessed=400_000_000, transcendentals=tokens * ff),
        name="gather_gradient",
    )(x, dy, pre, w_down)


def scatter_kernel(x_all, d_pre, w_in, dx, dw_in, ici, d2d, out1, out2, out3, out4, lhs2, lhs3, lhs4, weights,
                   ici_send, ici_recv, d2d_send, d2d_recv, w_sem, load_sem, stage_sem, dx_sem, x_sem, dw_sem):
    place = Place()
    chip, core = place.chip, place.core
    shard, width = dx.shape
    tokens, ff = d_pre.shape
    n1, n2 = width // 16, width // 8

    def pick(i, group):
        k = lax.div(i, 3 * group)
        p = (1 - k) * lax.rem(i, 3) + k * lax.rem(i, 2)
        t = (1 - k) * lax.div(i, 3) + k * (group + lax.div(i - 3 * group, 2))
        return p, t

    def unpick(p, t, group):
        k = lax.div(t, group)
        return (1 - k) * (3 * t + p) + k * (3 * group + 2 * (t - group) + p)

    def turn(p, k):
        return lax.rem(p + k, 3)

    def narrow(i):
        p, t = pick(i, 4)
        return p, t, p * (3 * n2) + t * n1

    def wide(i):
        p, t = pick(i, 2)
        return p, t, p * (3 * n2) + t * n2

    def narrow_weights(i):
        slot = lax.rem(i, 4)
        return [pltpu.make_async_copy(w_in.at[rows(narrow(i)[2], n1)], weights.at[rows(slot * n1, n1)], w_sem.at[slot])]

    def wide_weights(i):
        start, slot = wide(i)[2], lax.rem(i, 2)
        return [
            pltpu.make_async_copy(w_in.at[rows(start + h * n1, n1)], weights.at[rows(slot * n2 + h * n1, n1)], w_sem.at[2 * slot + h])
            for h in (0, 1)
        ]

    def go(copies):
        for copy in copies:
            copy.start()

    def wait(copies):
        for copy in copies:
            copy.wait()

    def lhs_loads(ref, p, chips, base):
        loads = []
        for half, c in enumerate((1 - core, core)):
            for k, r in enumerate(chips):
                src = d_pre.at[rows((2 * place.chip_at(r) + c) * shard, shard)]
                n = half * len(chips) + k
                view = ref if p is None else ref.at[p]
                loads.append(pltpu.make_async_copy(src, view.at[pl.ds(n * shard, shard)], load_sem.at[base + n]))
        return loads

    place.barrier()
    for i in range(4):
        go(narrow_weights(i))

    def exchange(k, i, count, size, columns, base, part):
        region = (0, 4, 6, 7)[k]
        dst = d2d.at[pl.ds(region * shard, count * shard), columns]
        return remote(part, dst, d2d_send.at[base + i], d2d_recv.at[base + i], place.sibling)

    def onward(k, i, count, p, columns, base, part):
        region = (0, 4, 6)[k]
        dst = ici.at[pl.ds(region * shard, count * shard), columns]
        return remote(part, dst, ici_send.at[base + i], ici_recv.at[base + i], place.across(turn(p, k)))

    def stage_chips(p, k):
        a, b, c = order(p)
        tail = [(0, 0), (0, 1), (1, 0), (1, 1)]
        if k == 0:
            return [tuple(across(a)[d] + s * across(b)[d] + t * across(c)[d] for d in range(3)) for s, t in tail]
        if k == 1:
            return [across(b), across(b, c)]
        return [across(c)] if k == 2 else [(0, 0, 0)]

    def stage(k, items, lhs, out, group, lag_b, lag_c, filler=None):
        count = (4, 2, 1, 1)[k]
        size = n1 if k == 0 else n2
        base = (0, 16, 24, 32)[k]
        locate = narrow if k == 0 else wide
        slots = lag_c + 1
        n_in = 1 + k
        from_ici = [(), ((2, 4),), ((1, 2), (5, 6)), ((0, 1), (4, 5), (6, 7))][k]

        def body(acc, term, staged):
            def columns(i):
                return lanes(locate(i)[2], size)

            def sources(i):
                region = (0, 4, 6, 7)[k]
                views = [d2d.at[pl.ds(region * shard, count * shard), columns(i)]]
                views += [ici.at[pl.ds(a * shard, (b - a) * shard), columns(i)] for a, b in from_ici]
                slot = lax.rem(i, slots)
                return [
                    pltpu.make_async_copy(view, staged.at[slot, n], stage_sem.at[slot * n_in + n]) for n, view in enumerate(views)
                ]

            def send(i):
                slot = lax.rem(i, slots)
                return exchange(k, i, count, size, columns(i), base, term.at[slot])

            def leave(i):
                if k < 3:
                    return onward(k, i, count, locate(i)[0], columns(i), base, out.at[i])
                return pltpu.make_async_copy(out.at[i], dx.at[:, columns(i)], dx_sem.at[i])

            @pl.loop(0, items + lag_c)
            def _(i):
                @pl.when(i < items)
                def _():
                    p, _, start = locate(i)
                    slot = lax.rem(i, slots)
                    if k == 0:
                        wait(narrow_weights(i))
                        w = weights[rows(lax.rem(i, 4) * n1, n1), :]
                    else:
                        wait(wide_weights(i))
                        w = weights[rows(lax.rem(i, 2) * n2, n2), :]

                    @pl.when(i >= slots)
                    def _():
                        send(i - slots).wait_send()

                    left = lhs[...] if k == 3 else lhs[p]
                    value = dot(left, w, NT)
                    term[slot] = value[: count * shard].astype(BF16)
                    acc[slot] = value[count * shard :]
                    send(i).start()
                    if k == 0:
                        @pl.when(i + 4 < items)
                        def _():
                            go(narrow_weights(i + 4))

                        @pl.when(i == items - 3)
                        def _():
                            go(wide_weights(0))

                        @pl.when(i == items - 1)
                        def _():
                            go(wide_weights(1))
                    elif k < 3:
                        go(wide_weights(lax.rem(i + 2, 8)))
                    else:
                        @pl.when(i + 2 < items)
                        def _():
                            go(wide_weights(i + 2))

                    if filler is not None:
                        filler(i)

                @pl.when((i >= lag_b) & (i < items + lag_b))
                def _():
                    j = i - lag_b
                    view = d2d.at[pl.ds(0, count * shard), columns(j)]
                    remote(view, view, d2d_send.at[base + j], d2d_recv.at[base + j], place.sibling).wait_recv()
                    p, t, _ = locate(j)
                    if k == 1:
                        for h in (0, 1):
                            n = unpick(p, 2 * t + h, 4)
                            view = ici.at[pl.ds(0, 4 * shard), lanes(locate(j)[2] + h * n1, n1)]
                            remote(view, view, ici_send.at[n], ici_recv.at[n], place.sibling).wait_recv()
                    elif k > 1:
                        n = (16, 24)[k - 2] + j
                        view = ici.at[pl.ds(0, (2, 1)[k - 2] * shard), columns(j)]
                        remote(view, view, ici_send.at[n], ici_recv.at[n], place.sibling).wait_recv()
                    go(sources(j))

                @pl.when(i >= lag_c)
                def _():
                    j = i - lag_c
                    slot = lax.rem(j, slots)
                    wait(sources(j))
                    total = acc[slot]
                    for n in range(n_in):
                        total = total + staged[slot, n].astype(F32)
                    out[j] = total.astype(BF16)
                    leave(j).start()

            for i in range(max(items - slots, 0), items):
                send(i).wait_send()

        pl.run_scoped(
            body,
            pltpu.VMEM((slots, count * shard, size), F32),
            pltpu.VMEM((slots, count * shard, size), BF16),
            pltpu.VMEM((slots, n_in, count * shard, size), BF16),
        )

    def first(lhs1):
        loads = [lhs_loads(lhs1, p, stage_chips(p, 0), 8 * p) for p in range(3)]
        loads.append([c for p in range(3) for c in lhs_loads(lhs2, p, stage_chips(p, 1), 24 + 4 * p)])
        loads.append([c for p in range(3) for c in lhs_loads(lhs3, p, stage_chips(p, 2), 36 + 2 * p)])
        loads.append(lhs_loads(lhs4, None, stage_chips(0, 3), 42))
        for some in loads:
            go(some)
        for some in loads:
            wait(some)
        stage(0, 16, lhs1, out1, 4, 1, 2)

    pl.run_scoped(first, pltpu.VMEM((3, 8 * shard, ff), BF16))

    def second(right, x_buf, dw_buf, right_sem):
        copy = pltpu.make_async_copy(d_pre, right, right_sem.at[0])
        copy.start()

        def x_load(i):
            slot = lax.rem(i, 2)
            return pltpu.make_async_copy(x_all.at[:, lanes(i * n1, n1)], x_buf.at[slot], x_sem.at[slot])

        def dw_store(i):
            slot = lax.rem(i, 2)
            return pltpu.make_async_copy(dw_buf.at[slot], dw_in.at[rows(i * n1, n1)], dw_sem.at[slot])

        x_load(0).start()
        x_load(1).start()
        copy.wait()

        def tile(i):
            slot = lax.rem(i, 2)
            x_load(i).wait()

            @pl.when(i >= 2)
            def _():
                dw_store(i - 2).wait()

            @pl.loop(0, 2)
            def _(h):
                half = lanes(h * (ff // 2), ff // 2)
                dw_buf[slot, :, half] = dot(x_buf[slot], right[:, half], TN).astype(BF16)

            dw_store(i).start()

            @pl.when(i + 2 < 8)
            def _():
                x_load(i + 2).start()

        stage(1, 8, lhs2, out2, 2, 0, 1, filler=tile)
        dw_store(6).wait()
        dw_store(7).wait()

    pl.run_scoped(
        second,
        pltpu.VMEM((tokens, ff), BF16),
        pltpu.VMEM((2, tokens, n1), BF16),
        pltpu.VMEM((2, n1, ff), BF16),
        pltpu.SemaphoreType.DMA((1,)),
    )
    stage(2, 8, lhs3, out3, 2, 2, 4)
    stage(3, 8, lhs4, out4, 2, 2, 4)
    for i in range(16):
        onward(0, i, 4, narrow(i)[0], lanes(narrow(i)[2], n1), 0, out1.at[i]).wait_send()
    for i in range(8):
        onward(1, i, 2, wide(i)[0], lanes(wide(i)[2], n2), 16, out2.at[i]).wait_send()
        onward(2, i, 1, wide(i)[0], lanes(wide(i)[2], n2), 24, out3.at[i]).wait_send()
        pltpu.make_async_copy(out4.at[i], dx.at[:, lanes(wide(i)[2], n2)], dx_sem.at[i]).wait()


def scatter(x_all, d_pre, w_in, shard):
    tokens, ff = d_pre.shape
    width = x_all.shape[1]
    n1, n2 = width // 16, width // 8
    dma, vmem = pltpu.SemaphoreType.DMA, pltpu.VMEM
    return pl.pallas_call(
        scatter_kernel,
        in_specs=[ANY] * 3,
        out_specs=[ANY] * 4,
        out_shape=[
            jax.ShapeDtypeStruct((shard, width), BF16),
            jax.ShapeDtypeStruct((width // 2, ff), BF16),
            jax.ShapeDtypeStruct((7 * shard, width), BF16),
            jax.ShapeDtypeStruct((8 * shard, width), BF16),
        ],
        scratch_shapes=[
            vmem((16, 4 * shard, n1), BF16),
            vmem((8, 2 * shard, n2), BF16),
            vmem((8, shard, n2), BF16),
            vmem((8, shard, n2), BF16),
            vmem((3, 4 * shard, ff), BF16),
            vmem((3, 2 * shard, ff), BF16),
            vmem((2 * shard, ff), BF16),
            vmem((4 * n1, ff), BF16),
            dma((32,)), dma((32,)), dma((40,)), dma((40,)), dma((4,)), dma((44,)), dma((20,)), dma((8,)), dma((2,)), dma((2,)),
        ],
        compiler_params=pltpu.CompilerParams(collective_id=1, has_side_effects=True, vmem_limit_bytes=VMEM_LIMIT),
        cost_estimate=pl.CostEstimate(flops=3 * tokens * ff * width, bytes_accessed=400_000_000, transcendentals=0),
        name="scatter_dx",
    )(x_all, d_pre, w_in)[:2]


def finish_kernel(x_ref, d_pre_ref, part_ref, down_ref, dw_in, dw_down, buf, copy_sem, buf_sem):
    i = pl.program_id(0)
    n, ff = part_ref.shape
    count = pl.num_programs(0)
    slot = lax.rem(i, 2)
    copies = [
        pltpu.make_async_copy(part_ref, dw_in.at[rows(i * n, n)], copy_sem.at[0]),
        pltpu.make_async_copy(down_ref, dw_down.at[rows(i * down_ref.shape[0], down_ref.shape[0])], copy_sem.at[1]),
    ]

    def store(i):
        slot = lax.rem(i, 2)
        return pltpu.make_async_copy(buf.at[slot], dw_in.at[rows((count + i) * n, n)], buf_sem.at[slot])

    for copy in copies:
        copy.start()

    @pl.when(i >= 2)
    def _():
        store(i - 2).wait()

    @pl.loop(0, 2)
    def _(h):
        half = lanes(h * (ff // 2), ff // 2)
        buf[slot, :, half] = dot(x_ref[...], d_pre_ref[:, half], TN).astype(BF16)

    store(i).start()
    for copy in copies:
        copy.wait()

    @pl.when(i == count - 1)
    def _():
        store(i - 1).wait()
        store(i).wait()


def finish(x_all, d_pre, dw_in_part, dw_down_part):
    tokens, ff = d_pre.shape
    width = x_all.shape[1]
    n = width // 16
    return pl.pallas_call(
        finish_kernel,
        grid=(8,),
        in_specs=[
            pl.BlockSpec((tokens, n), lambda i: (0, 8 + i)),
            pl.BlockSpec((tokens, ff), lambda i: (0, 0)),
            pl.BlockSpec((n, ff), lambda i: (i, 0)),
            pl.BlockSpec((ff // 8, width), lambda i: (i, 0)),
        ],
        out_specs=[ANY] * 2,
        out_shape=[jax.ShapeDtypeStruct((width, ff), BF16), jax.ShapeDtypeStruct((ff, width), BF16)],
        scratch_shapes=[pltpu.VMEM((2, n, ff), BF16), pltpu.SemaphoreType.DMA((2,)), pltpu.SemaphoreType.DMA((2,))],
        compiler_params=pltpu.CompilerParams(dimension_semantics=("arbitrary",), vmem_limit_bytes=VMEM_LIMIT),
        cost_estimate=pl.CostEstimate(flops=tokens * ff * width, bytes_accessed=140_000_000, transcendentals=0),
        name="finish",
    )(x_all, d_pre, dw_in_part, dw_down_part)


def solution(mesh):
    def body(x, dy, pre, w_in, w_down):
        x_all, _, d_pre, _, _, dw_down = forward(x, dy, pre, w_down)
        dx, dw_in = scatter(x_all, d_pre, w_in, x.shape[0])
        dw_in, dw_down = finish(x_all, d_pre, dw_in, dw_down)
        return dx, dw_in, dw_down

    return jax.shard_map(
        body,
        mesh=mesh,
        in_specs=(P(("dp", "tp")), P(("dp", "tp")), P("dp", "tp"), P(None, "tp"), P("tp", None)),
        out_specs=(P(("dp", "tp")), P("dp", "tp"), P(("dp", "tp"))),
        check_vma=False,
    )
```

time: 1440 us -> 457 us (0.32)
  matrix products: 700 us -> 0 us
  Pallas kernels: 0 us -> 453 us
  starting transfers between devices: 383 us -> 0 us
  waiting for transfers between devices: 197 us -> 0 us
  local copies, waits for them, and re-layouts: 71.8 us -> 3.1 us
  other arithmetic: 61.9 us -> 0 us
    dot_general x18 -> x0, matrix products: 700 us -> none  [the longest x9 462 us: by_group(): jnp.einsum('gta,gtb->gab', a, b, preferred_element_type=jnp.float32)]
    pallas_call x0 -> x3, Pallas kernels: none -> 453 us  [the longest x1 240 us: forward(): pl.pallas_call(forward_kernel, in_specs=[ANY] * 4, out_specs=[ANY] * 6, o...]
    dot_general x34 -> x0, starting transfers between devices: 383 us -> none  [the longest x17 212 us: step(): dx = jnp.dot(d_pre, w_in.T)]
    unnamed x2 -> x0, waiting for transfers between devices: 148 us -> none
    dot_general x17 -> x0, other arithmetic: 61.9 us -> none  [the longest x9 45.4 us: step(): dx = jnp.dot(d_pre, w_in.T)]
    dot_general x9 -> x0, local copies, waits for them, and re-layouts: 56.3 us -> none  [the longest x1 51 us: by_group(): jnp.einsum('gta,gtb->gab', a, b, preferred_element_type=jnp.float32)]
    dot_general x34 -> x0, waiting for transfers between devices: 49.7 us -> none  [the longest x17 49.6 us: step(): dx = jnp.dot(d_pre, w_in.T)]
  transfers between devices with their start and end apart: 35 -> 0, of which waited for: 10 -> 0; matrix products, arithmetic and copies ran while one was open for 58% -> 0% of each run, Pallas kernels for 0% -> 0%
where the time goes in v2:
time: 457 us; the launch traced here: 456 us
  Pallas kernels  453 us (99%)
    pallas_call x1, Pallas kernels, forward(): pl.pallas_call(forward_kernel, in_specs=[ANY] * 4, out_specs=[ANY] * 6, o...  240 us
    pallas_call x1, Pallas kernels, scatter(): pl.pallas_call(scatter_kernel, in_specs=[ANY] * 3, out_specs=[ANY] * 4, o...  160 us
    pallas_call x1, Pallas kernels, finish(): pl.pallas_call(finish_kernel, grid=(8,), in_specs=[pl.BlockSpec((tokens,...  52.8 us

profile of v2, /device:TPU:0, one launch (start us, length us, event | category | flops | bytes accessed | tf_op | source)
XLA Modules:
  0.0 456.4 jit_solution(14763941850585090620)
XLA Ops:
  0.6 239.5 %gather_gradient.1 = (bf16[2048,8192]{1,0:T(8,128)(2,1)}, bf16[2048,8192]{1,0:T(8,128)(2,1)}, bf16[2048,2048]{1,0:T(8,128)(2,1)}, bf16[2048,2048]{1,0:T(8,128)(2...) custom-call(bf16[128,8192]{1,0:T(8,128)(2,1)} %x.1, bf16[128,8192]{1,0:T(8,128)(2,1)} %dy.1, ...), custom_call_target="tpu_custom_call" | custom-call | flops 137438953472 | bytes 400000000 | tf_op jit(solution)/shard_map/gather_gradient/pallas_call | solution.py:289
  240.2 160.4 %scatter_dx.1 = (bf16[128,8192]{1,0:T(8,128)(2,1)}, bf16[4096,2048]{1,0:T(8,128)(2,1)}, bf16[896,8192]{1,0:T(8,128)(2,1)}, bf16[1024,8192]{1,0:T(8,128)(2,1)}) custom-call(bf16[2048,8192]{1,0:T(8,128)(2,1)} %get-tuple-element.10.x_all.x_ref, bf16[2048,2048]{1,0:T(8,128)(2,1)} %get-tuple-element.11.d_pre.d_pre_ref, bf16[8192,2048]{1,0:T(8,128)(2,1)} %w_in.1), custom_call_target="tpu_custom_call" | custom-call | flops 103079215104 | bytes 400000000 | tf_op jit(solution)/shard_map/scatter_dx/pallas_call | solution.py:576
  400.6 52.8 %finish.1 = (bf16[8192,2048]{1,0:T(8,128)(2,1)}, bf16[2048,8192]{1,0:T(8,128)(2,1)}) custom-call(bf16[2048,8192]{1,0:T(8,128)(2,1)} %get-tuple-element.10.x_all.x_ref, bf16[2048,2048]{1,0:T(8,128)(2,1)} %get-tuple-element.11.d_pre.d_pre_ref, bf16[4096,2048]{1,0:T(8,128)(2,1)} %get-tuple-element.13.part_ref, bf16[2048,8192]{1,0:T(8,128)(2,1)} %get-tuple-element.14.down_ref), custom_call_target="tpu_custom_call" | custom-call | flops 34359738368 | bytes 140000000 | tf_op jit(solution)/shard_map/finish/pallas_call | solution.py:643
  453.3 3.1 copy.9

commit v3 on v2

v3 whole, which is shorter than its diff:
```python
import functools

import jax
import jax.numpy as jnp
from jax import lax
from jax.experimental import pallas as pl
from jax.experimental.pallas import tpu as pltpu
from jax.sharding import PartitionSpec as P

VMEM_LIMIT = 66_000_000
WEIGHT = (4, 2, 1)
F32, BF16 = jnp.float32, jnp.bfloat16
ANY = pl.BlockSpec(memory_space=pl.ANY)
CHIPS = [(a, b, c) for a in (0, 1) for b in (0, 1) for c in (0, 1)]


def act(pre):
    return jax.nn.gelu(pre)


def dot(a, b, dims):
    return lax.dot_general(a, b, (dims, ((), ())), preferred_element_type=F32)


NT, TN = ((1,), (1,)), ((0,), (0,))


def rows(start, size):
    return pl.ds(pl.multiple_of(start, 16), size)


def lanes(start, size):
    return pl.ds(pl.multiple_of(start, 128), size)


class Place:
    def __init__(self):
        me = lax.axis_index("tp")
        self.chip, self.core = lax.div(me, 2), lax.rem(me, 2)
        self.step = [w * (1 - 2 * lax.rem(lax.div(self.chip, w), 2)) for w in WEIGHT]
        self.sibling = self.device(self.chip, 1 - self.core)

    def chip_at(self, r):
        return self.chip + sum(self.step[d] * r[d] for d in range(3) if isinstance(r[d], jax.Array) or r[d])

    def device(self, chip, core):
        return {"tp": 2 * chip + core}

    def across(self, d):
        if isinstance(d, int):
            return self.device(self.chip + self.step[d], self.core)
        r = (lax.div(2 - d, 2), lax.rem(d, 2), lax.div(d, 2))
        return self.device(self.chip_at(r), self.core)

    def barrier(self):
        sem = pltpu.get_barrier_semaphore()
        for peer in [self.sibling] + [self.across(d) for d in range(3)]:
            pl.semaphore_signal(sem, inc=1, device_id=peer, device_id_type=pl.DeviceIdType.MESH)
        pl.semaphore_wait(sem, 4)


def remote(src, dst, send, recv, device):
    return pltpu.make_async_remote_copy(src, dst, send, recv, device_id=device, device_id_type=pl.DeviceIdType.MESH)


def order(p):
    return p, (p + 1) % 3, (p + 2) % 3


def across(*dims):
    return tuple(int(d in dims) for d in range(3))


class Gather:
    def __init__(self, place, src, dst, sems, base, halves):
        self.place, self.src, self.dst, self.halves = place, src, dst, halves
        self.shard, width = src.shape
        self.size = self.shard // halves
        self.send, self.recv, self.out, self.back = (functools.partial(lambda s, i: s.at[base + i], s) for s in sems)
        tiles = width // 128
        ends = [128 * (tiles * k // 3) for k in range(4)]
        self.columns = [pl.ds(ends[k], ends[k + 1] - ends[k]) for k in range(3)]

    def rows_of(self, r, core, h=None):
        start = (2 * self.place.chip_at(r) + core) * self.shard
        return rows(start, self.shard) if h is None else rows(start + h * self.size, self.size)

    def piece(self, p, r, core, h):
        return self.dst.at[self.rows_of(r, core, h), self.columns[p]]

    @staticmethod
    def index(p, r, h):
        return 24 * h + 8 * p + 4 * r[0] + 2 * r[1] + r[2]

    def hop(self, p, r, h):
        d = [d for d in order(p) if r[d]][-1]
        q = tuple(r[e] * (e != d) for e in range(3))
        dst = self.piece(p, q, self.place.core, h)
        src = dst if any(q) else self.src.at[pl.ds(h * self.size, self.size), self.columns[p]]
        i = self.index(p, r, h)
        return remote(src, dst, self.send(i), self.recv(i), self.place.across(d))

    def arrive(self, p, r, h):
        view, i = self.piece(p, r, self.place.core, h), self.index(p, r, h)
        remote(view, view, self.send(i), self.recv(i), self.place.sibling).wait_recv()

    def share(self, p, r, h):
        view, i = self.piece(p, r, self.place.core, h), self.index(p, r, h)
        return remote(view, view, self.out(i), self.back(i), self.place.sibling)

    def shared(self, p, r, h):
        view, i = self.piece(p, r, 1 - self.place.core, h), self.index(p, r, h)
        remote(view, view, self.out(i), self.back(i), self.place.sibling).wait_recv()

    def share_own(self):
        return remote(self.src, self.dst.at[self.rows_of((0, 0, 0), self.place.core)], self.out(0), self.back(0), self.place.sibling)

    def shared_own(self):
        view = self.dst.at[self.rows_of((0, 0, 0), 1 - self.place.core)]
        remote(view, view, self.out(0), self.back(0), self.place.sibling).wait_recv()

    def shared_all(self, chips, h):
        for p in range(3):
            for r in chips:
                self.shared(p, r, h)

    def begin(self):
        self.share_own().start()
        for h in range(self.halves):
            for k in range(3):
                for d in range(3):
                    self.hop((d - k) % 3, across(d), h).start()

    def act(self, n, h=0):
        for p in range(3):
            a, b, c = order(p)
            seq = [across(a), across(b), across(c), across(a, b), across(a, c), across(b, c), across(a, b, c)]
            follow = {0: [across(a, b), across(a, c)], 1: [across(b, c)], 3: [across(a, b, c)]}
            self.arrive(p, seq[n], h)
            for r in follow.get(n, []):
                self.hop(p, r, h).start()
            self.share(p, seq[n], h).start()

    def drain(self):
        self.share_own().wait_send()
        for h in range(self.halves):
            for p in range(3):
                for r in CHIPS[1:]:
                    self.hop(p, r, h).wait_send()
                    self.share(p, r, h).wait_send()


NEAR = [(1, 0, 0), (0, 1, 0), (0, 0, 1)]
MIDDLE = [(1, 1, 0), (0, 1, 1), (1, 0, 1)]
FAR = [(1, 1, 1)]
HERE = [(0, 0, 0)]


def forward_kernel(x, dy, pre, w_down, x_all, dy_all, d_pre, hidden, slope, dw_down, send, recv, out, back, w_sem, load_sem, store_sem, own_sem):
    place = Place()
    shard, width = dy.shape
    half = shard // 2
    tokens, ff = pre.shape
    block = ff // 4
    place.barrier()
    sems = (send, recv, out, back)
    gather_dy = Gather(place, dy, dy_all, sems, 0, 2)
    gather_x = Gather(place, x, x_all, sems, 48, 1)
    gather_dy.begin()
    mine = gather_dy.rows_of(HERE[0], place.core)

    def gradient(weights):
        def load_weights(j):
            part = pl.ds(j * block, block)
            return pltpu.make_async_copy(w_down.at[part], weights.at[part], w_sem.at[j])

        for j in range(4):
            load_weights(j).start()

        def before(x_buf):
            taken = pltpu.make_async_copy(x, x_buf, own_sem.at[0])
            taken.start()

            def gelu(pre_ref, hidden_ref, slope_ref):
                value, pull = jax.vjp(act, pre_ref[...].astype(F32))
                hidden_ref[...] = value.astype(BF16)
                slope_ref[...] = pull(jnp.ones_like(value))[0]

            spec = pl.BlockSpec((shard, ff), lambda i: (i, 0))
            pltpu.emit_pipeline(gelu, grid=(tokens // shard,), in_specs=[spec], out_specs=[spec, spec])(pre, hidden, slope)
            taken.wait()
            put = pltpu.make_async_copy(x_buf, x_all.at[mine], own_sem.at[1])
            put.start()
            for n in range(3):
                gather_dy.act(n, 0)
            gather_dy.shared_own()
            put.wait()

        pl.run_scoped(before, pltpu.VMEM((shard, width), BF16))

        def chunks(lhs, slopes, result):
            batches = [(HERE, None), (NEAR, 0), (NEAR, 1), (MIDDLE, 0), (MIDDLE, 1), (FAR, None)]

            def parts(n):
                chips, h = batches[n]
                size = shard if h is None else half
                cores = (place.core, 1 - place.core)
                return [(gather_dy.rows_of(r, c, h), pl.ds(k * size, size)) for k, (r, c) in enumerate((r, c) for r in chips for c in cores)]

            def rows_in(n):
                return sum(part.size for _, part in parts(n))

            def loads(n):
                copies = []
                for k, (src, part) in enumerate(parts(n)):
                    at = 12 * (n % 2) + k
                    there = dy if (n == 0 and k == 0) else dy_all.at[src]
                    copies.append(pltpu.make_async_copy(there, lhs.at[n % 2, part], load_sem.at[at]))
                    copies.append(pltpu.make_async_copy(slope.at[src], slopes.at[n % 2, part], load_sem.at[at + 6]))
                return copies

            def stores(n):
                return [
                    pltpu.make_async_copy(result.at[n % 2, part], d_pre.at[dst], store_sem.at[6 * (n % 2) + k])
                    for k, (dst, part) in enumerate(parts(n))
                ]

            own = pltpu.make_async_copy(lhs.at[0, pl.ds(0, shard)], dy_all.at[mine], own_sem.at[0])

            def ready(n):
                chips, h = batches[n]
                if n == 2:
                    for k in range(3):
                        gather_dy.act(k, 1)
                if n in (3, 4):
                    for k in (3, 4, 5):
                        gather_dy.act(k, h)
                if n == 5:
                    gather_dy.act(6, 0)
                    gather_dy.act(6, 1)
                for h in (0, 1) if h is None else (h,):
                    gather_dy.shared_all(chips, h)
                if n == 2:
                    own.wait()
                for copy in loads(n):
                    copy.start()

            when = (2, 3, 4, 4, 3)
            for copy in loads(0):
                copy.start()
            for n in range(6):
                for copy in loads(n):
                    copy.wait()
                if n == 0:
                    own.start()
                    for j in range(4):
                        load_weights(j).wait()
                if n >= 2:
                    for copy in stores(n - 2):
                        copy.wait()
                size, slot = rows_in(n), n % 2

                @pl.loop(0, 4)
                def _(j):
                    if n < 5 and when[n] < 4:
                        @pl.when(j == when[n])
                        def _():
                            ready(n + 1)

                    columns = lanes(j * block, block)
                    d_hidden = dot(lhs[slot, :size], weights[rows(j * block, block), :], NT)
                    result[slot, :size, columns] = (d_hidden * slopes[slot, :size, columns]).astype(BF16)

                for copy in stores(n):
                    copy.start()
                if n < 5 and when[n] == 4:
                    ready(n + 1)
                if n == 3:
                    gather_x.begin()
            for n in (4, 5):
                for copy in stores(n):
                    copy.wait()

        pl.run_scoped(chunks, pltpu.VMEM((2, 6 * half, width), BF16), pltpu.VMEM((2, 6 * half, ff), F32), pltpu.VMEM((2, 6 * half, ff), BF16))

    pl.run_scoped(gradient, pltpu.VMEM((ff, width), BF16))

    tm, tn = ff // 2, width // 8

    def product(h_ref, dy_ref, o_ref):
        at = pl.program_id(0) * 8 + pl.program_id(1)
        for n, when in enumerate((1, 4, 7, 10, 13, 15)):
            @pl.when(at == when)
            def _():
                gather_x.act(n)

        o_ref[...] = dot(h_ref[...], dy_ref[...], TN).astype(BF16)

    pltpu.emit_pipeline(
        product,
        grid=(2, 8),
        in_specs=[pl.BlockSpec((tokens, tm), lambda i, j: (0, i)), pl.BlockSpec((tokens, tn), lambda i, j: (0, j))],
        out_specs=[pl.BlockSpec((tm, tn), lambda i, j: (i, j))],
    )(hidden, dy_all, dw_down)
    gather_x.act(6)
    gather_x.shared_own()
    gather_x.shared_all(CHIPS[1:], 0)
    gather_dy.drain()
    gather_x.drain()


def forward(x, dy, pre, w_down):
    shard, width = dy.shape
    tokens, ff = pre.shape
    dma = pltpu.SemaphoreType.DMA
    whole = jax.ShapeDtypeStruct((tokens, width), BF16)
    return pl.pallas_call(
        forward_kernel,
        in_specs=[ANY] * 4,
        out_specs=[ANY] * 6,
        out_shape=[
            whole,
            whole,
            jax.ShapeDtypeStruct((tokens, ff), BF16),
            jax.ShapeDtypeStruct((tokens, ff), BF16),
            jax.ShapeDtypeStruct((tokens, ff), F32),
            jax.ShapeDtypeStruct((ff, width), BF16),
        ],
        scratch_shapes=[dma((72,)), dma((72,)), dma((72,)), dma((72,)), dma((4,)), dma((24,)), dma((12,)), dma((2,))],
        compiler_params=pltpu.CompilerParams(collective_id=0, has_side_effects=True, vmem_limit_bytes=VMEM_LIMIT),
        cost_estimate=pl.CostEstimate(flops=4 * tokens * ff * width, bytes_accessed=400_000_000, transcendentals=tokens * ff),
        name="gather_gradient",
    )(x, dy, pre, w_down)


def scatter_kernel(x_all, d_pre, w_in, dx, dw_in, ici, d2d, out1, out2, lhs2, lhs3, lhs4, weights,
                   ici_send, ici_recv, d2d_send, d2d_recv, w_sem, load_sem, stage_sem, dx_sem, x_sem, dw_sem):
    place = Place()
    chip, core = place.chip, place.core
    shard, width = dx.shape
    tokens, ff = d_pre.shape
    n1, n2 = width // 16, width // 8

    def pick(i, group):
        k = lax.div(i, 3 * group)
        p = (1 - k) * lax.rem(i, 3) + k * lax.rem(i, 2)
        t = (1 - k) * lax.div(i, 3) + k * (group + lax.div(i - 3 * group, 2))
        return p, t

    def unpick(p, t, group):
        k = lax.div(t, group)
        return (1 - k) * (3 * t + p) + k * (3 * group + 2 * (t - group) + p)

    def turn(p, k):
        return lax.rem(p + k, 3)

    def narrow(i):
        p, t = pick(i, 4)
        return p, t, p * (3 * n2) + t * n1

    def wide(i):
        p, t = pick(i, 2)
        return p, t, p * (3 * n2) + t * n2

    def narrow_weights(i):
        slot = lax.rem(i, 4)
        return [pltpu.make_async_copy(w_in.at[rows(narrow(i)[2], n1)], weights.at[rows(slot * n1, n1)], w_sem.at[slot])]

    def wide_weights(i):
        start, slot = wide(i)[2], lax.rem(i, 2)
        return [
            pltpu.make_async_copy(w_in.at[rows(start + h * n1, n1)], weights.at[rows(slot * n2 + h * n1, n1)], w_sem.at[2 * slot + h])
            for h in (0, 1)
        ]

    def go(copies):
        for copy in copies:
            copy.start()

    def wait(copies):
        for copy in copies:
            copy.wait()

    def lhs_loads(ref, p, chips, base):
        loads = []
        for half, c in enumerate((1 - core, core)):
            for k, r in enumerate(chips):
                src = d_pre.at[rows((2 * place.chip_at(r) + c) * shard, shard)]
                n = half * len(chips) + k
                view = ref if p is None else ref.at[p]
                loads.append(pltpu.make_async_copy(src, view.at[pl.ds(n * shard, shard)], load_sem.at[base + n]))
        return loads

    place.barrier()
    for i in range(4):
        go(narrow_weights(i))

    def exchange(k, i, count, size, columns, base, part):
        region = (0, 4, 6, 7)[k]
        dst = d2d.at[pl.ds(region * shard, count * shard), columns]
        return remote(part, dst, d2d_send.at[base + i], d2d_recv.at[base + i], place.sibling)

    def onward(k, i, count, p, columns, base, part):
        region = (0, 4, 6)[k]
        dst = ici.at[pl.ds(region * shard, count * shard), columns]
        return remote(part, dst, ici_send.at[base + i], ici_recv.at[base + i], place.across(turn(p, k)))

    def stage_chips(p, k):
        a, b, c = order(p)
        tail = [(0, 0), (0, 1), (1, 0), (1, 1)]
        if k == 0:
            return [tuple(across(a)[d] + s * across(b)[d] + t * across(c)[d] for d in range(3)) for s, t in tail]
        if k == 1:
            return [across(b), across(b, c)]
        return [across(c)] if k == 2 else [(0, 0, 0)]

    def stage(k, items, lhs, out, lag_b, lag_c, prepare=None, filler=None):
        count = (4, 2, 1, 1)[k]
        size = n1 if k == 0 else n2
        base = (0, 16, 24, 32)[k]
        locate = narrow if k == 0 else wide
        slots = lag_c + 1
        n_in = 1 + k
        from_ici = [(), ((2, 4),), ((1, 2), (5, 6)), ((0, 1), (4, 5), (6, 7))][k]

        def body(acc, term, staged):
            def columns(i):
                return lanes(locate(i)[2], size)

            def sources(i):
                region = (0, 4, 6, 7)[k]
                views = [d2d.at[pl.ds(region * shard, count * shard), columns(i)]]
                views += [ici.at[pl.ds(a * shard, (b - a) * shard), columns(i)] for a, b in from_ici]
                slot = lax.rem(i, slots)
                return [
                    pltpu.make_async_copy(view, staged.at[slot, n], stage_sem.at[slot * n_in + n]) for n, view in enumerate(views)
                ]

            def send(i):
                slot = lax.rem(i, slots)
                return exchange(k, i, count, size, columns(i), base, term.at[slot])

            def leave(i):
                if k < 3:
                    return onward(k, i, count, locate(i)[0], columns(i), base, out.at[i])
                return pltpu.make_async_copy(out.at[i], dx.at[:, columns(i)], dx_sem.at[i])

            def fetch(j):
                view = d2d.at[pl.ds(0, count * shard), columns(j)]
                remote(view, view, d2d_send.at[base + j], d2d_recv.at[base + j], place.sibling).wait_recv()
                p, t, start = locate(j)
                if k == 1:
                    for h in (0, 1):
                        n = unpick(p, 2 * t + h, 4)
                        view = ici.at[pl.ds(0, 4 * shard), lanes(start + h * n1, n1)]
                        remote(view, view, ici_send.at[n], ici_recv.at[n], place.sibling).wait_recv()
                elif k > 1:
                    n = (16, 24)[k - 2] + j
                    view = ici.at[pl.ds(0, (2, 1)[k - 2] * shard), columns(j)]
                    remote(view, view, ici_send.at[n], ici_recv.at[n], place.sibling).wait_recv()
                go(sources(j))

            def add(j, slot):
                total = acc[slot]
                for n in range(n_in):
                    total = total + staged[slot, n].astype(F32)
                out[j] = total.astype(BF16)

            @pl.loop(0, items)
            def _(i):
                p, _, start = locate(i)
                slot = lax.rem(i, slots)
                wait(narrow_weights(i) if k == 0 else wide_weights(i))
                if prepare is not None:
                    prepare(i)

                @pl.when(i >= slots)
                def _():
                    send(i - slots).wait_send()

                @pl.when(i >= lag_c)
                def _():
                    wait(sources(i - lag_c))

                add(lax.max(i - lag_c, 0), lax.rem(i + slots - lag_c, slots))
                if k == 0:
                    w = weights[rows(lax.rem(i, 4) * n1, n1), :]
                else:
                    w = weights[rows(lax.rem(i, 2) * n2, n2), :]
                value = dot(lhs[...] if k == 3 else lhs[p], w, NT)
                term[slot] = value[: count * shard].astype(BF16)
                acc[slot] = value[count * shard :]
                send(i).start()

                @pl.when(i >= lag_c)
                def _():
                    leave(i - lag_c).start()

                if k == 0:
                    @pl.when(i + 4 < items)
                    def _():
                        go(narrow_weights(i + 4))

                    @pl.when(i == items - 3)
                    def _():
                        go(wide_weights(0))

                    @pl.when(i == items - 1)
                    def _():
                        go(wide_weights(1))
                elif k < 3:
                    go(wide_weights(lax.rem(i + 2, 8)))
                else:
                    @pl.when(i + 2 < items)
                    def _():
                        go(wide_weights(i + 2))

                if filler is not None:
                    filler(i)

                @pl.when(i >= lag_b)
                def _():
                    fetch(i - lag_b)

            for j in range(items - lag_b, items):
                fetch(j)
            for j in range(items - lag_c, items):
                wait(sources(j))
                add(j, j % slots)
                leave(j).start()

            for i in range(max(items - slots, 0), items):
                send(i).wait_send()

        pl.run_scoped(
            body,
            pltpu.VMEM((slots, count * shard, size), F32),
            pltpu.VMEM((slots, count * shard, size), BF16),
            pltpu.VMEM((slots, n_in, count * shard, size), BF16),
        )

    loads2 = [c for p in range(3) for c in lhs_loads(lhs2, p, stage_chips(p, 1), 24 + 4 * p)]
    loads3 = [c for p in range(3) for c in lhs_loads(lhs3, p, stage_chips(p, 2), 36 + 2 * p)]
    loads4 = lhs_loads(lhs4, None, stage_chips(0, 3), 42)

    def main(right, right_sem):
        right_load = pltpu.make_async_copy(d_pre, right, right_sem.at[0])

        def first(lhs1):
            loads = [lhs_loads(lhs1, p, stage_chips(p, 0), 8 * p) for p in range(3)]
            for some in loads + [loads2, [right_load], loads3, loads4]:
                go(some)

            def prepare(i):
                for p in range(3):
                    @pl.when(i == p)
                    def _():
                        wait(loads[p])

            stage(0, 16, lhs1, out1, 1, 2, prepare=prepare)

        pl.run_scoped(first, pltpu.VMEM((3, 8 * shard, ff), BF16))

        def second(x_buf, dw_buf):
            def x_load(i):
                slot = lax.rem(i, 2)
                return pltpu.make_async_copy(x_all.at[:, lanes(i * n1, n1)], x_buf.at[slot], x_sem.at[slot])

            def dw_store(i):
                slot = lax.rem(i, 2)
                return pltpu.make_async_copy(dw_buf.at[slot], dw_in.at[rows(i * n1, n1)], dw_sem.at[slot])

            x_load(0).start()
            x_load(1).start()
            wait(loads2)
            right_load.wait()

            def tile(i):
                slot = lax.rem(i, 2)
                x_load(i).wait()

                @pl.when(i >= 2)
                def _():
                    dw_store(i - 2).wait()

                @pl.loop(0, 2)
                def _(h):
                    part = lanes(h * (ff // 2), ff // 2)
                    dw_buf[slot, :, part] = dot(x_buf[slot], right[:, part], TN).astype(BF16)

                dw_store(i).start()

                @pl.when(i + 2 < 8)
                def _():
                    x_load(i + 2).start()

            stage(1, 8, lhs2, out2, 0, 1, filler=tile)
            dw_store(6).wait()
            dw_store(7).wait()

        pl.run_scoped(second, pltpu.VMEM((2, tokens, n1), BF16), pltpu.VMEM((2, n1, ff), BF16))

    pl.run_scoped(main, pltpu.VMEM((tokens, ff), BF16), pltpu.SemaphoreType.DMA((1,)))
    def last(out3, out4):
        wait(loads3)
        wait(loads4)
        stage(2, 8, lhs3, out3, 2, 4)
        stage(3, 8, lhs4, out4, 2, 4)
        for i in range(16):
            onward(0, i, 4, narrow(i)[0], lanes(narrow(i)[2], n1), 0, out1.at[i]).wait_send()
        for i in range(8):
            onward(1, i, 2, wide(i)[0], lanes(wide(i)[2], n2), 16, out2.at[i]).wait_send()
            onward(2, i, 1, wide(i)[0], lanes(wide(i)[2], n2), 24, out3.at[i]).wait_send()
            pltpu.make_async_copy(out4.at[i], dx.at[:, lanes(wide(i)[2], n2)], dx_sem.at[i]).wait()

    pl.run_scoped(last, pltpu.VMEM((8, shard, n2), BF16), pltpu.VMEM((8, shard, n2), BF16))


def scatter(x_all, d_pre, w_in, shard):
    tokens, ff = d_pre.shape
    width = x_all.shape[1]
    n1, n2 = width // 16, width // 8
    dma, vmem = pltpu.SemaphoreType.DMA, pltpu.VMEM
    return pl.pallas_call(
        scatter_kernel,
        in_specs=[ANY] * 3,
        out_specs=[ANY] * 4,
        out_shape=[
            jax.ShapeDtypeStruct((shard, width), BF16),
            jax.ShapeDtypeStruct((width // 2, ff), BF16),
            jax.ShapeDtypeStruct((7 * shard, width), BF16),
            jax.ShapeDtypeStruct((8 * shard, width), BF16),
        ],
        scratch_shapes=[
            vmem((16, 4 * shard, n1), BF16),
            vmem((8, 2 * shard, n2), BF16),
            vmem((3, 4 * shard, ff), BF16),
            vmem((3, 2 * shard, ff), BF16),
            vmem((2 * shard, ff), BF16),
            vmem((4 * n1, ff), BF16),
            dma((32,)), dma((32,)), dma((40,)), dma((40,)), dma((4,)), dma((44,)), dma((20,)), dma((8,)), dma((2,)), dma((2,)),
        ],
        compiler_params=pltpu.CompilerParams(collective_id=1, has_side_effects=True, vmem_limit_bytes=VMEM_LIMIT),
        cost_estimate=pl.CostEstimate(flops=3 * tokens * ff * width, bytes_accessed=400_000_000, transcendentals=0),
        name="scatter_dx",
    )(x_all, d_pre, w_in)[:2]


def finish_kernel(x_ref, d_pre_ref, part_ref, down_ref, dw_in, dw_down, buf, copy_sem, buf_sem):
    i = pl.program_id(0)
    n, ff = part_ref.shape
    count = pl.num_programs(0)
    slot = lax.rem(i, 2)
    copies = [
        pltpu.make_async_copy(part_ref, dw_in.at[rows(i * n, n)], copy_sem.at[0]),
        pltpu.make_async_copy(down_ref, dw_down.at[rows(i * down_ref.shape[0], down_ref.shape[0])], copy_sem.at[1]),
    ]

    def store(i):
        slot = lax.rem(i, 2)
        return pltpu.make_async_copy(buf.at[slot], dw_in.at[rows((count + i) * n, n)], buf_sem.at[slot])

    for copy in copies:
        copy.start()

    @pl.when(i >= 2)
    def _():
        store(i - 2).wait()

    @pl.loop(0, 2)
    def _(h):
        half = lanes(h * (ff // 2), ff // 2)
        buf[slot, :, half] = dot(x_ref[...], d_pre_ref[:, half], TN).astype(BF16)

    store(i).start()
    for copy in copies:
        copy.wait()

    @pl.when(i == count - 1)
    def _():
        store(i - 1).wait()
        store(i).wait()


def finish(x_all, d_pre, dw_in_part, dw_down_part):
    tokens, ff = d_pre.shape
    width = x_all.shape[1]
    n = width // 16
    return pl.pallas_call(
        finish_kernel,
        grid=(8,),
        in_specs=[
            pl.BlockSpec((tokens, n), lambda i: (0, 8 + i)),
            pl.BlockSpec((tokens, ff), lambda i: (0, 0)),
            pl.BlockSpec((n, ff), lambda i: (i, 0)),
            pl.BlockSpec((ff // 8, width), lambda i: (i, 0)),
        ],
        out_specs=[ANY] * 2,
        out_shape=[jax.ShapeDtypeStruct((width, ff), BF16), jax.ShapeDtypeStruct((ff, width), BF16)],
        scratch_shapes=[pltpu.VMEM((2, n, ff), BF16), pltpu.SemaphoreType.DMA((2,)), pltpu.SemaphoreType.DMA((2,))],
        compiler_params=pltpu.CompilerParams(dimension_semantics=("arbitrary",), vmem_limit_bytes=VMEM_LIMIT),
        cost_estimate=pl.CostEstimate(flops=tokens * ff * width, bytes_accessed=140_000_000, transcendentals=0),
        name="finish",
    )(x_all, d_pre, dw_in_part, dw_down_part)


def solution(mesh):
    def body(x, dy, pre, w_in, w_down):
        x_all, _, d_pre, _, _, dw_down = forward(x, dy, pre, w_down)
        dx, dw_in = scatter(x_all, d_pre, w_in, x.shape[0])
        dw_in, dw_down = finish(x_all, d_pre, dw_in, dw_down)
        return dx, dw_in, dw_down

    return jax.shard_map(
        body,
        mesh=mesh,
        in_specs=(P(("dp", "tp")), P(("dp", "tp")), P("dp", "tp"), P(None, "tp"), P("tp", None)),
        out_specs=(P(("dp", "tp")), P("dp", "tp"), P(("dp", "tp"))),
        check_vma=False,
    )
```

time: 457 us -> 477 us (1.044)
  Pallas kernels: 453 us -> 472 us
    pallas_call x1, Pallas kernels: 160 us -> 193 us  [scatter(): pl.pallas_call(scatter_kernel, in_specs=[ANY] * 3, out_specs=[ANY] * 4, o...]
    pallas_call x1, Pallas kernels: 240 us -> 227 us  [forward(): pl.pallas_call(forward_kernel, in_specs=[ANY] * 4, out_specs=[ANY] * 6, o...]
where the time goes in v3:
time: 477 us; the launch traced here: 476 us
  Pallas kernels  472 us (99%)
    pallas_call x1, Pallas kernels, forward(): pl.pallas_call(forward_kernel, in_specs=[ANY] * 4, out_specs=[ANY] * 6, o...  227 us
    pallas_call x1, Pallas kernels, scatter(): pl.pallas_call(scatter_kernel, in_specs=[ANY] * 3, out_specs=[ANY] * 4, o...  193 us
    pallas_call x1, Pallas kernels, finish(): pl.pallas_call(finish_kernel, grid=(8,), in_specs=[pl.BlockSpec((tokens,...  52.8 us

profile of v3, /device:TPU:0, one launch (start us, length us, event | category | flops | bytes accessed | tf_op | source)
XLA Modules:
  0.0 476.1 jit_solution(12981525545182060680)
XLA Ops:
  0.6 226.8 %gather_gradient.1 = (bf16[2048,8192]{1,0:T(8,128)(2,1)}, bf16[2048,8192]{1,0:T(8,128)(2,1)}, bf16[2048,2048]{1,0:T(8,128)(2,1)}, bf16[2048,2048]{1,0:T(8,128)(2...) custom-call(bf16[128,8192]{1,0:T(8,128)(2,1)} %x.1, bf16[128,8192]{1,0:T(8,128)(2,1)} %dy.1, ...), custom_call_target="tpu_custom_call" | custom-call | flops 137438953472 | bytes 400000000 | tf_op jit(solution)/shard_map/gather_gradient/pallas_call | solution.py:317
  227.5 192.7 %scatter_dx.1 = (bf16[128,8192]{1,0:T(8,128)(2,1)}, bf16[4096,2048]{1,0:T(8,128)(2,1)}, bf16[896,8192]{1,0:T(8,128)(2,1)}, bf16[1024,8192]{1,0:T(8,128)(2,1)}) custom-call(bf16[2048,8192]{1,0:T(8,128)(2,1)} %get-tuple-element.10.x_all.x_ref, bf16[2048,2048]{1,0:T(8,128)(2,1)} %get-tuple-element.11.d_pre.d_pre_ref, bf16[8192,2048]{1,0:T(8,128)(2,1)} %w_in.1), custom_call_target="tpu_custom_call" | custom-call | flops 103079215104 | bytes 400000000 | tf_op jit(solution)/shard_map/scatter_dx/pallas_call | solution.py:624
  420.2 52.8 %finish.1 = (bf16[8192,2048]{1,0:T(8,128)(2,1)}, bf16[2048,8192]{1,0:T(8,128)(2,1)}) custom-call(bf16[2048,8192]{1,0:T(8,128)(2,1)} %get-tuple-element.10.x_all.x_ref, bf16[2048,2048]{1,0:T(8,128)(2,1)} %get-tuple-element.11.d_pre.d_pre_ref, bf16[4096,2048]{1,0:T(8,128)(2,1)} %get-tuple-element.13.part_ref, bf16[2048,8192]{1,0:T(8,128)(2,1)} %get-tuple-element.14.down_ref), custom_call_target="tpu_custom_call" | custom-call | flops 34359738368 | bytes 140000000 | tf_op jit(solution)/shard_map/finish/pallas_call | solution.py:689
  473.0 3.1 copy.9

commit v4 on v3

--- a/solution.py
+++ b/solution.py
@@ -557,7 +557,7 @@
                     def _():
                         wait(loads[p])
 
-            stage(0, 16, lhs1, out1, 1, 2, prepare=prepare)
+            stage(0, 16, lhs1, out1, 1, 3, prepare=prepare)
 
         pl.run_scoped(first, pltpu.VMEM((3, 8 * shard, ff), BF16))
 
@@ -594,7 +594,7 @@
                 def _():
                     x_load(i + 2).start()
 
-            stage(1, 8, lhs2, out2, 0, 1, filler=tile)
+            stage(1, 8, lhs2, out2, 0, 2, filler=tile)
             dw_store(6).wait()
             dw_store(7).wait()
 
@@ -604,8 +604,8 @@
     def last(out3, out4):
         wait(loads3)
         wait(loads4)
-        stage(2, 8, lhs3, out3, 2, 4)
-        stage(3, 8, lhs4, out4, 2, 4)
+        stage(2, 8, lhs3, out3, 2, 5)
+        stage(3, 8, lhs4, out4, 2, 5)
         for i in range(16):
             onward(0, i, 4, narrow(i)[0], lanes(narrow(i)[2], n1), 0, out1.at[i]).wait_send()
         for i in range(8):
@@ -638,7 +638,7 @@
             vmem((3, 2 * shard, ff), BF16),
             vmem((2 * shard, ff), BF16),
             vmem((4 * n1, ff), BF16),
-            dma((32,)), dma((32,)), dma((40,)), dma((40,)), dma((4,)), dma((44,)), dma((20,)), dma((8,)), dma((2,)), dma((2,)),
+            dma((32,)), dma((32,)), dma((40,)), dma((40,)), dma((4,)), dma((44,)), dma((24,)), dma((8,)), dma((2,)), dma((2,)),
         ],
         compiler_params=pltpu.CompilerParams(collective_id=1, has_side_effects=True, vmem_limit_bytes=VMEM_LIMIT),
         cost_estimate=pl.CostEstimate(flops=3 * tokens * ff * width, bytes_accessed=400_000_000, transcendentals=0),

time: 477 us -> 436 us (0.914)
  Pallas kernels: 472 us -> 432 us
    pallas_call x1, Pallas kernels: 193 us -> 152 us  [scatter(): pl.pallas_call(scatter_kernel, in_specs=[ANY] * 3, out_specs=[ANY] * 4, o...]
where the time goes in v4:
time: 436 us
  Pallas kernels  432 us (99%)
    pallas_call x1, Pallas kernels, forward(): pl.pallas_call(forward_kernel, in_specs=[ANY] * 4, out_specs=[ANY] * 6, o...  227 us
    pallas_call x1, Pallas kernels, scatter(): pl.pallas_call(scatter_kernel, in_specs=[ANY] * 3, out_specs=[ANY] * 4, o...  152 us
    pallas_call x1, Pallas kernels, finish(): pl.pallas_call(finish_kernel, grid=(8,), in_specs=[pl.BlockSpec((tokens,...  52.8 us

profile of v4, /device:TPU:0, one launch (start us, length us, event | category | flops | bytes accessed | tf_op | source)
XLA Modules:
  0.0 435.6 jit_solution(17792444060212968757)
XLA Ops:
  0.6 226.8 %gather_gradient.1 = (bf16[2048,8192]{1,0:T(8,128)(2,1)}, bf16[2048,8192]{1,0:T(8,128)(2,1)}, bf16[2048,2048]{1,0:T(8,128)(2,1)}, bf16[2048,2048]{1,0:T(8,128)(2...) custom-call(bf16[128,8192]{1,0:T(8,128)(2,1)} %x.1, bf16[128,8192]{1,0:T(8,128)(2,1)} %dy.1, ...), custom_call_target="tpu_custom_call" | custom-call | flops 137438953472 | bytes 400000000 | tf_op jit(solution)/shard_map/gather_gradient/pallas_call | solution.py:317
  227.5 152.2 %scatter_dx.1 = (bf16[128,8192]{1,0:T(8,128)(2,1)}, bf16[4096,2048]{1,0:T(8,128)(2,1)}, bf16[896,8192]{1,0:T(8,128)(2,1)}, bf16[1024,8192]{1,0:T(8,128)(2,1)}) custom-call(bf16[2048,8192]{1,0:T(8,128)(2,1)} %get-tuple-element.10.x_all.x_ref, bf16[2048,2048]{1,0:T(8,128)(2,1)} %get-tuple-element.11.d_pre.d_pre_ref, bf16[8192,2048]{1,0:T(8,128)(2,1)} %w_in.1), custom_call_target="tpu_custom_call" | custom-call | flops 103079215104 | bytes 400000000 | tf_op jit(solution)/shard_map/scatter_dx/pallas_call | solution.py:624
  379.7 52.8 %finish.1 = (bf16[8192,2048]{1,0:T(8,128)(2,1)}, bf16[2048,8192]{1,0:T(8,128)(2,1)}) custom-call(bf16[2048,8192]{1,0:T(8,128)(2,1)} %get-tuple-element.10.x_all.x_ref, bf16[2048,2048]{1,0:T(8,128)(2,1)} %get-tuple-element.11.d_pre.d_pre_ref, bf16[4096,2048]{1,0:T(8,128)(2,1)} %get-tuple-element.13.part_ref, bf16[2048,8192]{1,0:T(8,128)(2,1)} %get-tuple-element.14.down_ref), custom_call_target="tpu_custom_call" | custom-call | flops 34359738368 | bytes 140000000 | tf_op jit(solution)/shard_map/finish/pallas_call | solution.py:689
  432.5 3.1 copy.9

commit v5 on v4

--- a/solution.py
+++ b/solution.py
@@ -7,7 +7,7 @@
 from jax.experimental.pallas import tpu as pltpu
 from jax.sharding import PartitionSpec as P
 
-VMEM_LIMIT = 66_000_000
+VMEM_LIMIT = 67_000_000
 WEIGHT = (4, 2, 1)
 F32, BF16 = jnp.float32, jnp.bfloat16
 ANY = pl.BlockSpec(memory_space=pl.ANY)
@@ -156,7 +156,8 @@
 HERE = [(0, 0, 0)]
 
 
-def forward_kernel(x, dy, pre, w_down, x_all, dy_all, d_pre, hidden, slope, dw_down, send, recv, out, back, w_sem, load_sem, store_sem, own_sem):
+def backward_kernel(x, dy, pre, w_down, w_in, x_all, dy_all, d_pre, hidden, slope, dw_down, dx, dw_in, ici, d2d,
+                    send, recv, out, back, w_sem, load_sem, store_sem, own_sem, *scatter_sems):
     place = Place()
     shard, width = dy.shape
     half = shard // 2
@@ -296,47 +297,27 @@
 
         o_ref[...] = dot(h_ref[...], dy_ref[...], TN).astype(BF16)
 
-    pltpu.emit_pipeline(
-        product,
-        grid=(2, 8),
-        in_specs=[pl.BlockSpec((tokens, tm), lambda i, j: (0, i)), pl.BlockSpec((tokens, tn), lambda i, j: (0, j))],
-        out_specs=[pl.BlockSpec((tm, tn), lambda i, j: (i, j))],
-    )(hidden, dy_all, dw_down)
-    gather_x.act(6)
-    gather_x.shared_own()
-    gather_x.shared_all(CHIPS[1:], 0)
+    def down():
+        pltpu.emit_pipeline(
+            product,
+            grid=(2, 8),
+            in_specs=[pl.BlockSpec((tokens, tm), lambda i, j: (0, i)), pl.BlockSpec((tokens, tn), lambda i, j: (0, j))],
+            out_specs=[pl.BlockSpec((tm, tn), lambda i, j: (i, j))],
+        )(hidden, dy_all, dw_down)
+
+    def rest(lhs, weights, right):
+        scatter(place, gather_x, down, x_all, d_pre, w_in, dx, dw_in, ici, d2d, lhs, weights, right, *scatter_sems)
+
+    pl.run_scoped(
+        rest, pltpu.VMEM((3, 8 * shard, ff), BF16), pltpu.VMEM((width // 4, ff), BF16), pltpu.VMEM((tokens, ff), BF16)
+    )
     gather_dy.drain()
     gather_x.drain()
 
 
-def forward(x, dy, pre, w_down):
-    shard, width = dy.shape
-    tokens, ff = pre.shape
-    dma = pltpu.SemaphoreType.DMA
-    whole = jax.ShapeDtypeStruct((tokens, width), BF16)
-    return pl.pallas_call(
-        forward_kernel,
-        in_specs=[ANY] * 4,
-        out_specs=[ANY] * 6,
-        out_shape=[
-            whole,
-            whole,
-            jax.ShapeDtypeStruct((tokens, ff), BF16),
-            jax.ShapeDtypeStruct((tokens, ff), BF16),
-            jax.ShapeDtypeStruct((tokens, ff), F32),
-            jax.ShapeDtypeStruct((ff, width), BF16),
-        ],
-        scratch_shapes=[dma((72,)), dma((72,)), dma((72,)), dma((72,)), dma((4,)), dma((24,)), dma((12,)), dma((2,))],
-        compiler_params=pltpu.CompilerParams(collective_id=0, has_side_effects=True, vmem_limit_bytes=VMEM_LIMIT),
-        cost_estimate=pl.CostEstimate(flops=4 * tokens * ff * width, bytes_accessed=400_000_000, transcendentals=tokens * ff),
-        name="gather_gradient",
-    )(x, dy, pre, w_down)
-
-
-def scatter_kernel(x_all, d_pre, w_in, dx, dw_in, ici, d2d, out1, out2, lhs2, lhs3, lhs4, weights,
-                   ici_send, ici_recv, d2d_send, d2d_recv, w_sem, load_sem, stage_sem, dx_sem, x_sem, dw_sem):
-    place = Place()
-    chip, core = place.chip, place.core
+def scatter(place, gather_x, down, x_all, d_pre, w_in, dx, dw_in, ici, d2d, lhs_buf, weights, right,
+            ici_send, ici_recv, d2d_send, d2d_recv, w_sem, load_sem, stage_sem, dx_sem, x_sem, dw_sem, right_sem):
+    core = place.core
     shard, width = dx.shape
     tokens, ff = d_pre.shape
     n1, n2 = width // 16, width // 8
@@ -381,19 +362,14 @@
         for copy in copies:
             copy.wait()
 
-    def lhs_loads(ref, p, chips, base):
+    def lhs_loads(p, first, chips, base):
         loads = []
         for half, c in enumerate((1 - core, core)):
             for k, r in enumerate(chips):
                 src = d_pre.at[rows((2 * place.chip_at(r) + c) * shard, shard)]
                 n = half * len(chips) + k
-                view = ref if p is None else ref.at[p]
-                loads.append(pltpu.make_async_copy(src, view.at[pl.ds(n * shard, shard)], load_sem.at[base + n]))
+                loads.append(pltpu.make_async_copy(src, lhs_buf.at[p, pl.ds(first + n * shard, shard)], load_sem.at[base + n]))
         return loads
-
-    place.barrier()
-    for i in range(4):
-        go(narrow_weights(i))
 
     def exchange(k, i, count, size, columns, base, part):
         region = (0, 4, 6, 7)[k]
@@ -414,12 +390,12 @@
             return [across(b), across(b, c)]
         return [across(c)] if k == 2 else [(0, 0, 0)]
 
-    def stage(k, items, lhs, out, lag_b, lag_c, prepare=None, filler=None):
+    def stage(k, items, out, lag_b, lag_c, prepare=None, filler=None):
         count = (4, 2, 1, 1)[k]
         size = n1 if k == 0 else n2
         base = (0, 16, 24, 32)[k]
         locate = narrow if k == 0 else wide
-        slots = lag_c + 1
+        slots, n_term, n_staged = lag_c, 2, lag_c - lag_b + 1
         n_in = 1 + k
         from_ici = [(), ((2, 4),), ((1, 2), (5, 6)), ((0, 1), (4, 5), (6, 7))][k]
 
@@ -431,14 +407,13 @@
                 region = (0, 4, 6, 7)[k]
                 views = [d2d.at[pl.ds(region * shard, count * shard), columns(i)]]
                 views += [ici.at[pl.ds(a * shard, (b - a) * shard), columns(i)] for a, b in from_ici]
-                slot = lax.rem(i, slots)
+                slot = lax.rem(i, n_staged)
                 return [
                     pltpu.make_async_copy(view, staged.at[slot, n], stage_sem.at[slot * n_in + n]) for n, view in enumerate(views)
                 ]
 
             def send(i):
-                slot = lax.rem(i, slots)
-                return exchange(k, i, count, size, columns(i), base, term.at[slot])
+                return exchange(k, i, count, size, columns(i), base, term.at[lax.rem(i, n_term)])
 
             def leave(i):
                 if k < 3:
@@ -460,10 +435,10 @@
                     remote(view, view, ici_send.at[n], ici_recv.at[n], place.sibling).wait_recv()
                 go(sources(j))
 
-            def add(j, slot):
+            def add(j, slot, there):
                 total = acc[slot]
                 for n in range(n_in):
-                    total = total + staged[slot, n].astype(F32)
+                    total = total + staged[there, n].astype(F32)
                 out[j] = total.astype(BF16)
 
             @pl.loop(0, items)
@@ -474,21 +449,22 @@
                 if prepare is not None:
                     prepare(i)
 
-                @pl.when(i >= slots)
+                @pl.when(i >= n_term)
                 def _():
-                    send(i - slots).wait_send()
+                    send(i - n_term).wait_send()
 
                 @pl.when(i >= lag_c)
                 def _():
                     wait(sources(i - lag_c))
 
-                add(lax.max(i - lag_c, 0), lax.rem(i + slots - lag_c, slots))
+                add(lax.max(i - lag_c, 0), slot, lax.rem(i + n_staged * lag_c - lag_c, n_staged))
                 if k == 0:
                     w = weights[rows(lax.rem(i, 4) * n1, n1), :]
                 else:
                     w = weights[rows(lax.rem(i, 2) * n2, n2), :]
-                value = dot(lhs[...] if k == 3 else lhs[p], w, NT)
-                term[slot] = value[: count * shard].astype(BF16)
+                where = ((0, 8), (0, 4), (4, 2), (6, 2))[k]
+                value = dot(lhs_buf[0 if k == 3 else p, pl.ds(where[0] * shard, where[1] * shard)], w, NT)
+                term[lax.rem(i, n_term)] = value[: count * shard].astype(BF16)
                 acc[slot] = value[count * shard :]
                 send(i).start()
 
@@ -522,60 +498,49 @@
                 def _():
                     fetch(i - lag_b)
 
-            for j in range(items - lag_b, items):
-                fetch(j)
-            for j in range(items - lag_c, items):
+            for i in range(items, items + lag_c):
+                j = i - lag_c
                 wait(sources(j))
-                add(j, j % slots)
+                add(j, j % slots, j % n_staged)
                 leave(j).start()
-
-            for i in range(max(items - slots, 0), items):
+                if i - lag_b < items:
+                    fetch(i - lag_b)
+            for i in range(items - n_term, items):
                 send(i).wait_send()
 
         pl.run_scoped(
             body,
             pltpu.VMEM((slots, count * shard, size), F32),
-            pltpu.VMEM((slots, count * shard, size), BF16),
-            pltpu.VMEM((slots, n_in, count * shard, size), BF16),
+            pltpu.VMEM((n_term, count * shard, size), BF16),
+            pltpu.VMEM((n_staged, n_in, count * shard, size), BF16),
         )
 
-    loads2 = [c for p in range(3) for c in lhs_loads(lhs2, p, stage_chips(p, 1), 24 + 4 * p)]
-    loads3 = [c for p in range(3) for c in lhs_loads(lhs3, p, stage_chips(p, 2), 36 + 2 * p)]
-    loads4 = lhs_loads(lhs4, None, stage_chips(0, 3), 42)
-
-    def main(right, right_sem):
-        right_load = pltpu.make_async_copy(d_pre, right, right_sem.at[0])
-
-        def first(lhs1):
-            loads = [lhs_loads(lhs1, p, stage_chips(p, 0), 8 * p) for p in range(3)]
-            for some in loads + [loads2, [right_load], loads3, loads4]:
-                go(some)
-
-            def prepare(i):
-                for p in range(3):
-                    @pl.when(i == p)
-                    def _():
-                        wait(loads[p])
-
-            stage(0, 16, lhs1, out1, 1, 3, prepare=prepare)
-
-        pl.run_scoped(first, pltpu.VMEM((3, 8 * shard, ff), BF16))
-
-        def second(x_buf, dw_buf):
-            def x_load(i):
-                slot = lax.rem(i, 2)
-                return pltpu.make_async_copy(x_all.at[:, lanes(i * n1, n1)], x_buf.at[slot], x_sem.at[slot])
-
-            def dw_store(i):
-                slot = lax.rem(i, 2)
-                return pltpu.make_async_copy(dw_buf.at[slot], dw_in.at[rows(i * n1, n1)], dw_sem.at[slot])
-
-            x_load(0).start()
-            x_load(1).start()
-            wait(loads2)
-            right_load.wait()
-
-            def tile(i):
+    loads1 = [lhs_loads(p, 0, stage_chips(p, 0), 8 * p) for p in range(3)]
+    loads2 = [c for p in range(3) for c in lhs_loads(p, 0, stage_chips(p, 1), 24 + 4 * p)]
+    loads3 = [c for p in range(3) for c in lhs_loads(p, 4 * shard, stage_chips(p, 2), 36 + 2 * p)]
+    loads4 = lhs_loads(0, 6 * shard, stage_chips(0, 3), 42)
+    right_load = pltpu.make_async_copy(d_pre, right, right_sem.at[0])
+    for i in range(4):
+        go(narrow_weights(i))
+    for some in loads1:
+        go(some)
+    right_load.start()
+    down()
+    for some in loads1:
+        wait(some)
+
+    def main(out2, x_buf, dw_buf):
+        def x_load(i):
+            slot = lax.rem(i, 2)
+            return pltpu.make_async_copy(x_all.at[:, lanes(i * n1, n1)], x_buf.at[slot], x_sem.at[slot])
+
+        def dw_store(i):
+            slot = lax.rem(i, 2)
+            return pltpu.make_async_copy(dw_buf.at[slot], dw_in.at[rows(i * n1, n1)], dw_sem.at[slot])
+
+        def tiles(a, b):
+            @pl.loop(a, b)
+            def _(i):
                 slot = lax.rem(i, 2)
                 x_load(i).wait()
 
@@ -594,56 +559,91 @@
                 def _():
                     x_load(i + 2).start()
 
-            stage(1, 8, lhs2, out2, 0, 2, filler=tile)
+        def fill2(i):
+            turn, on = lax.div(i + 1, 3), lax.div(lax.rem(i, 3), 2)
+            tiles(turn - on, turn - on + on * (2 * turn - 1))
+
+        def fill3(i):
+            turn, on = lax.div(i + 1, 3), lax.div(lax.rem(i, 3), 2)
+            tiles(4 + turn, 4 + turn + on)
+
+        def fill4(i):
+            on = lax.div(lax.rem(i, 3), 2) * lax.div(i, 3)
+            tiles(7, 7 + on)
+
+        def early(out1):
+            def prepare(i):
+                @pl.when(i == 5)
+                def _():
+                    gather_x.act(6)
+
+            stage(0, 16, out1, 1, 3, prepare=prepare)
+            for some in (loads2, loads3, loads4):
+                go(some)
+            gather_x.shared_own()
+            gather_x.shared_all(CHIPS[1:], 0)
+            x_load(0).start()
+            x_load(1).start()
+            right_load.wait()
+            for some in (loads2, loads3, loads4):
+                wait(some)
+            stage(1, 8, out2, 0, 2, filler=fill2)
+            for i in range(16):
+                onward(0, i, 4, narrow(i)[0], lanes(narrow(i)[2], n1), 0, out1.at[i]).wait_send()
+
+        pl.run_scoped(early, pltpu.VMEM((16, 4 * shard, n1), BF16))
+        tiles(4, 5)
+
+        def late(out3, out4):
+            stage(2, 8, out3, 2, 5, filler=fill3)
+            stage(3, 8, out4, 2, 5, filler=fill4)
             dw_store(6).wait()
             dw_store(7).wait()
-
-        pl.run_scoped(second, pltpu.VMEM((2, tokens, n1), BF16), pltpu.VMEM((2, n1, ff), BF16))
-
-    pl.run_scoped(main, pltpu.VMEM((tokens, ff), BF16), pltpu.SemaphoreType.DMA((1,)))
-    def last(out3, out4):
-        wait(loads3)
-        wait(loads4)
-        stage(2, 8, lhs3, out3, 2, 5)
-        stage(3, 8, lhs4, out4, 2, 5)
-        for i in range(16):
-            onward(0, i, 4, narrow(i)[0], lanes(narrow(i)[2], n1), 0, out1.at[i]).wait_send()
-        for i in range(8):
-            onward(1, i, 2, wide(i)[0], lanes(wide(i)[2], n2), 16, out2.at[i]).wait_send()
-            onward(2, i, 1, wide(i)[0], lanes(wide(i)[2], n2), 24, out3.at[i]).wait_send()
-            pltpu.make_async_copy(out4.at[i], dx.at[:, lanes(wide(i)[2], n2)], dx_sem.at[i]).wait()
-
-    pl.run_scoped(last, pltpu.VMEM((8, shard, n2), BF16), pltpu.VMEM((8, shard, n2), BF16))
-
-
-def scatter(x_all, d_pre, w_in, shard):
-    tokens, ff = d_pre.shape
-    width = x_all.shape[1]
-    n1, n2 = width // 16, width // 8
-    dma, vmem = pltpu.SemaphoreType.DMA, pltpu.VMEM
-    return pl.pallas_call(
-        scatter_kernel,
-        in_specs=[ANY] * 3,
-        out_specs=[ANY] * 4,
+            for i in range(8):
+                onward(1, i, 2, wide(i)[0], lanes(wide(i)[2], n2), 16, out2.at[i]).wait_send()
+                onward(2, i, 1, wide(i)[0], lanes(wide(i)[2], n2), 24, out3.at[i]).wait_send()
+                pltpu.make_async_copy(out4.at[i], dx.at[:, lanes(wide(i)[2], n2)], dx_sem.at[i]).wait()
+
+        pl.run_scoped(late, pltpu.VMEM((8, shard, n2), BF16), pltpu.VMEM((8, shard, n2), BF16))
+
+    pl.run_scoped(
+        main,
+        pltpu.VMEM((8, 2 * shard, n2), BF16),
+        pltpu.VMEM((2, tokens, n1), BF16),
+        pltpu.VMEM((2, n1, ff), BF16),
+    )
+
+
+def backward(x, dy, pre, w_in, w_down):
+    shard, width = dy.shape
+    tokens, ff = pre.shape
+    dma = pltpu.SemaphoreType.DMA
+
+    def shape(*size, dtype=BF16):
+        return jax.ShapeDtypeStruct(size, dtype)
+
+    x_all, _, d_pre, _, _, dw_down, dx, dw_in, _, _ = pl.pallas_call(
+        backward_kernel,
+        in_specs=[ANY] * 5,
+        out_specs=[ANY] * 10,
         out_shape=[
-            jax.ShapeDtypeStruct((shard, width), BF16),
-            jax.ShapeDtypeStruct((width // 2, ff), BF16),
-            jax.ShapeDtypeStruct((7 * shard, width), BF16),
-            jax.ShapeDtypeStruct((8 * shard, width), BF16),
+            shape(tokens, width),
+            shape(tokens, width),
+            shape(tokens, ff),
+            shape(tokens, ff),
+            shape(tokens, ff, dtype=F32),
+            shape(ff, width),
+            shape(shard, width),
+            shape(width // 2, ff),
+            shape(7 * shard, width),
+            shape(8 * shard, width),
         ],
-        scratch_shapes=[
-            vmem((16, 4 * shard, n1), BF16),
-            vmem((8, 2 * shard, n2), BF16),
-            vmem((3, 4 * shard, ff), BF16),
-            vmem((3, 2 * shard, ff), BF16),
-            vmem((2 * shard, ff), BF16),
-            vmem((4 * n1, ff), BF16),
-            dma((32,)), dma((32,)), dma((40,)), dma((40,)), dma((4,)), dma((44,)), dma((24,)), dma((8,)), dma((2,)), dma((2,)),
-        ],
-        compiler_params=pltpu.CompilerParams(collective_id=1, has_side_effects=True, vmem_limit_bytes=VMEM_LIMIT),
-        cost_estimate=pl.CostEstimate(flops=3 * tokens * ff * width, bytes_accessed=400_000_000, transcendentals=0),
-        name="scatter_dx",
-    )(x_all, d_pre, w_in)[:2]
+        scratch_shapes=[dma((n,)) for n in (72, 72, 72, 72, 4, 24, 12, 2, 32, 32, 40, 40, 4, 44, 24, 8, 2, 2, 1)],
+        compiler_params=pltpu.CompilerParams(collective_id=0, has_side_effects=True, vmem_limit_bytes=VMEM_LIMIT),
+        cost_estimate=pl.CostEstimate(flops=7 * tokens * ff * width, bytes_accessed=800_000_000, transcendentals=tokens * ff),
+        name="backward",
+    )(x, dy, pre, w_down, w_in)
+    return x_all, d_pre, dw_down, dx, dw_in
 
 
 def finish_kernel(x_ref, d_pre_ref, part_ref, down_ref, dw_in, dw_down, buf, copy_sem, buf_sem):
@@ -706,8 +706,7 @@
 
 def solution(mesh):
     def body(x, dy, pre, w_in, w_down):
-        x_all, _, d_pre, _, _, dw_down = forward(x, dy, pre, w_down)
-        dx, dw_in = scatter(x_all, d_pre, w_in, x.shape[0])
+        x_all, d_pre, dw_down, dx, dw_in = backward(x, dy, pre, w_in, w_down)
         dw_in, dw_down = finish(x_all, d_pre, dw_in, dw_down)
         return dx, dw_in, dw_down
 

time: 436 us -> 440 us (level)
    pallas_call x2 -> x1, Pallas kernels: 379 us -> 382 us  [backward(): pl.pallas_call(backward_kernel, in_specs=[ANY] * 5, out_specs=[ANY] * 10,...]
where the time goes in v5:
time: 440 us; the launch traced here: 439 us
  Pallas kernels  435 us (99%)
    pallas_call x1, Pallas kernels, backward(): pl.pallas_call(backward_kernel, in_specs=[ANY] * 5, out_specs=[ANY] * 10,...  382 us
    pallas_call x1, Pallas kernels, finish(): pl.pallas_call(finish_kernel, grid=(8,), in_specs=[pl.BlockSpec((tokens,...  52.8 us

profile of v5, /device:TPU:0, one launch (start us, length us, event | category | flops | bytes accessed | tf_op | source)
XLA Modules:
  0.0 438.9 jit_solution(8420735310986169524)
XLA Ops:
  0.6 382.4 %backward.1 = (bf16[2048,8192]{1,0:T(8,128)(2,1)}, bf16[2048,8192]{1,0:T(8,128)(2,1)}, bf16[2048,2048]{1,0:T(8,128)(2,1)}, bf16[2048,2048]{1,0:T(8,128)(2,1)}, f...) custom-call(bf16[128,8192]{1,0:T(8,128)(2,1)} %x.1, ...), custom_call_target="tpu_custom_call" | custom-call | flops 240518168576 | bytes 800000000 | tf_op jit(solution)/shard_map/backward/pallas_call | solution.py:625
  383.0 52.8 %finish.1 = (bf16[8192,2048]{1,0:T(8,128)(2,1)}, bf16[2048,8192]{1,0:T(8,128)(2,1)}) custom-call(bf16[2048,8192]{1,0:T(8,128)(2,1)} %get-tuple-element.11.x_ref, bf16[2048,2048]{1,0:T(8,128)(2,1)} %get-tuple-element.12.d_pre_ref, bf16[4096,2048]{1,0:T(8,128)(2,1)} %get-tuple-element.13.part_ref, bf16[2048,8192]{1,0:T(8,128)(2,1)} %get-tuple-element.14.down_ref), custom_call_target="tpu_custom_call" | custom-call | flops 34359738368 | bytes 140000000 | tf_op jit(solution)/shard_map/finish/pallas_call | solution.py:689
  435.8 3.1 copy.9

commit v6 on v5

--- a/solution.py
+++ b/solution.py
@@ -156,8 +156,8 @@
 HERE = [(0, 0, 0)]
 
 
-def backward_kernel(x, dy, pre, w_down, w_in, x_all, dy_all, d_pre, hidden, slope, dw_down, dx, dw_in, ici, d2d,
-                    send, recv, out, back, w_sem, load_sem, store_sem, own_sem, *scatter_sems):
+def backward_kernel(x, dy, pre, w_down, w_in, x_all, dy_all, d_pre, hidden, dw_down, dx, dw_in, ici, d2d,
+                    send, recv, out, back, w_sem, load_sem, pre_sem, hidden_sem, store_sem, own_sem, *scatter_sems):
     place = Place()
     shard, width = dy.shape
     half = shard // 2
@@ -169,135 +169,169 @@
     gather_x = Gather(place, x, x_all, sems, 48, 1)
     gather_dy.begin()
     mine = gather_dy.rows_of(HERE[0], place.core)
-
-    def gradient(weights):
+    batches = [(HERE, None), (NEAR, 0), (NEAR, 1), (MIDDLE, 0), (MIDDLE, 1), (FAR, None)]
+
+    def parts(n):
+        chips, h = batches[n]
+        size = shard if h is None else half
+        cores = (place.core, 1 - place.core)
+        return [(gather_dy.rows_of(r, c, h), pl.ds(k * size, size)) for k, (r, c) in enumerate((r, c) for r in chips for c in cores)]
+
+    def rows_in(n):
+        return sum(part.size for _, part in parts(n))
+
+    def gradient(weights, lhs, slopes, result, values):
         def load_weights(j):
-            part = pl.ds(j * block, block)
+            part = rows(j * block, block)
             return pltpu.make_async_copy(w_down.at[part], weights.at[part], w_sem.at[j])
 
+        def pre_loads(n):
+            return [
+                pltpu.make_async_copy(pre.at[src], values.at[n % 2, part], pre_sem.at[6 * (n % 2) + k])
+                for k, (src, part) in enumerate(parts(n))
+            ]
+
+        def hidden_stores(n):
+            return [
+                pltpu.make_async_copy(values.at[n % 2, part], hidden.at[dst], hidden_sem.at[6 * (n % 2) + k])
+                for k, (dst, part) in enumerate(parts(n))
+            ]
+
+        def row_load(n, k):
+            src, part = parts(n)[k]
+            there = dy if (n == 0 and k == 0) else dy_all.at[src]
+            return pltpu.make_async_copy(there, lhs.at[n % 2, part], load_sem.at[6 * (n % 2) + k])
+
+        def stores(n):
+            return [
+                pltpu.make_async_copy(result.at[n % 2, part], d_pre.at[dst], store_sem.at[6 * (n % 2) + k])
+                for k, (dst, part) in enumerate(parts(n))
+            ]
+
+        def gelu(n):
+            for copy in pre_loads(n):
+                copy.wait()
+            slot, some = n % 2, 32 if shard >= 64 else 16
+
+            @pl.loop(0, rows_in(n) // some)
+            def _(i):
+                part = rows(i * some, some)
+                value, pull = jax.vjp(act, values[slot, part, :].astype(F32))
+                slopes[slot, part, :] = pull(jnp.ones_like(value))[0]
+                values[slot, part, :] = value.astype(BF16)
+
+            for copy in hidden_stores(n):
+                copy.start()
+
+        own_row = pltpu.make_async_copy(lhs.at[0, pl.ds(0, shard)], dy_all.at[mine], own_sem.at[0])
+
+        for copy in pre_loads(0):
+            copy.start()
+        row_load(0, 0).start()
+        for copy in pre_loads(1):
+            copy.start()
         for j in range(4):
             load_weights(j).start()
-
-        def before(x_buf):
-            taken = pltpu.make_async_copy(x, x_buf, own_sem.at[0])
-            taken.start()
-
-            def gelu(pre_ref, hidden_ref, slope_ref):
-                value, pull = jax.vjp(act, pre_ref[...].astype(F32))
-                hidden_ref[...] = value.astype(BF16)
-                slope_ref[...] = pull(jnp.ones_like(value))[0]
-
-            spec = pl.BlockSpec((shard, ff), lambda i: (i, 0))
-            pltpu.emit_pipeline(gelu, grid=(tokens // shard,), in_specs=[spec], out_specs=[spec, spec])(pre, hidden, slope)
-            taken.wait()
-            put = pltpu.make_async_copy(x_buf, x_all.at[mine], own_sem.at[1])
-            put.start()
-            for n in range(3):
-                gather_dy.act(n, 0)
-            gather_dy.shared_own()
-            put.wait()
-
-        pl.run_scoped(before, pltpu.VMEM((shard, width), BF16))
-
-        def chunks(lhs, slopes, result):
-            batches = [(HERE, None), (NEAR, 0), (NEAR, 1), (MIDDLE, 0), (MIDDLE, 1), (FAR, None)]
-
-            def parts(n):
-                chips, h = batches[n]
-                size = shard if h is None else half
-                cores = (place.core, 1 - place.core)
-                return [(gather_dy.rows_of(r, c, h), pl.ds(k * size, size)) for k, (r, c) in enumerate((r, c) for r in chips for c in cores)]
-
-            def rows_in(n):
-                return sum(part.size for _, part in parts(n))
-
-            def loads(n):
-                copies = []
-                for k, (src, part) in enumerate(parts(n)):
-                    at = 12 * (n % 2) + k
-                    there = dy if (n == 0 and k == 0) else dy_all.at[src]
-                    copies.append(pltpu.make_async_copy(there, lhs.at[n % 2, part], load_sem.at[at]))
-                    copies.append(pltpu.make_async_copy(slope.at[src], slopes.at[n % 2, part], load_sem.at[at + 6]))
-                return copies
-
-            def stores(n):
-                return [
-                    pltpu.make_async_copy(result.at[n % 2, part], d_pre.at[dst], store_sem.at[6 * (n % 2) + k])
-                    for k, (dst, part) in enumerate(parts(n))
-                ]
-
-            own = pltpu.make_async_copy(lhs.at[0, pl.ds(0, shard)], dy_all.at[mine], own_sem.at[0])
-
-            def ready(n):
-                chips, h = batches[n]
-                if n == 2:
-                    for k in range(3):
-                        gather_dy.act(k, 1)
-                if n in (3, 4):
-                    for k in (3, 4, 5):
-                        gather_dy.act(k, h)
-                if n == 5:
-                    gather_dy.act(6, 0)
-                    gather_dy.act(6, 1)
+        gelu(0)
+        gather_dy.shared_own()
+        row_load(0, 1).start()
+        gelu(1)
+        row_load(0, 0).wait()
+        own_row.start()
+        row_load(0, 1).wait()
+
+        passes = [
+            ([(0, 0)], [(1, 0)], [(2, 0)]),
+            ([(0, 1)], [(1, 1)], [(2, 1)]),
+            ([(3, 0)], [(4, 0)], [(5, 0)]),
+            ([(3, 1)], [(4, 1)], [(5, 1)]),
+            ([(6, 0)], [(6, 1)], []),
+            ([], [], []),
+        ]
+        for n in range(6):
+            if n:
+                for k in range(len(parts(n))):
+                    row_load(n, k).wait()
+            if n < 4:
+                for copy in hidden_stores(n):
+                    copy.wait()
+                for copy in pre_loads(n + 2):
+                    copy.start()
+            if n >= 2:
+                for copy in stores(n - 2):
+                    copy.wait()
+            size, slot = rows_in(n), n % 2
+
+            @pl.loop(0, 4)
+            def _(j):
+                if n == 0:
+                    load_weights(j).wait()
+                for at in (2, 3):
+                    if passes[n][at - 2]:
+                        @pl.when(j == at)
+                        def _():
+                            for k, h in passes[n][at - 2]:
+                                gather_dy.act(k, h)
+
+                columns = lanes(j * block, block)
+                d_hidden = dot(lhs[slot, :size], weights[rows(j * block, block), :], NT)
+                result[slot, :size, columns] = (d_hidden * slopes[slot, :size, columns]).astype(BF16)
+
+            for copy in stores(n):
+                copy.start()
+            if n == 3:
+                gather_x.begin()
+            if n < 4:
+                gelu(n + 2)
+            for k, h in passes[n][2]:
+                gather_dy.act(k, h)
+            if n < 5:
+                chips, h = batches[n + 1]
                 for h in (0, 1) if h is None else (h,):
                     gather_dy.shared_all(chips, h)
-                if n == 2:
-                    own.wait()
-                for copy in loads(n):
-                    copy.start()
-
-            when = (2, 3, 4, 4, 3)
-            for copy in loads(0):
-                copy.start()
-            for n in range(6):
-                for copy in loads(n):
-                    copy.wait()
-                if n == 0:
-                    own.start()
-                    for j in range(4):
-                        load_weights(j).wait()
-                if n >= 2:
-                    for copy in stores(n - 2):
-                        copy.wait()
-                size, slot = rows_in(n), n % 2
-
-                @pl.loop(0, 4)
-                def _(j):
-                    if n < 5 and when[n] < 4:
-                        @pl.when(j == when[n])
-                        def _():
-                            ready(n + 1)
-
-                    columns = lanes(j * block, block)
-                    d_hidden = dot(lhs[slot, :size], weights[rows(j * block, block), :], NT)
-                    result[slot, :size, columns] = (d_hidden * slopes[slot, :size, columns]).astype(BF16)
-
-                for copy in stores(n):
-                    copy.start()
-                if n < 5 and when[n] == 4:
-                    ready(n + 1)
-                if n == 3:
-                    gather_x.begin()
-            for n in (4, 5):
-                for copy in stores(n):
-                    copy.wait()
-
-        pl.run_scoped(chunks, pltpu.VMEM((2, 6 * half, width), BF16), pltpu.VMEM((2, 6 * half, ff), F32), pltpu.VMEM((2, 6 * half, ff), BF16))
-
-    pl.run_scoped(gradient, pltpu.VMEM((ff, width), BF16))
+                if n == 1:
+                    own_row.wait()
+                for k in range(len(parts(n + 1))):
+                    row_load(n + 1, k).start()
+        taken = pltpu.make_async_copy(x, lhs.at[0, pl.ds(0, shard)], own_sem.at[0])
+        taken.start()
+        for n in (4, 5):
+            for copy in hidden_stores(n):
+                copy.wait()
+            for copy in stores(n):
+                copy.wait()
+        taken.wait()
+        put = pltpu.make_async_copy(lhs.at[0, pl.ds(0, shard)], x_all.at[mine], own_sem.at[1])
+        put.start()
+        put.wait()
+
+    pl.run_scoped(
+        gradient,
+        pltpu.VMEM((ff, width), BF16),
+        pltpu.VMEM((2, 6 * half, width), BF16),
+        pltpu.VMEM((2, 6 * half, ff), F32),
+        pltpu.VMEM((2, 6 * half, ff), BF16),
+        pltpu.VMEM((2, 6 * half, ff), BF16),
+    )
 
     tm, tn = ff // 2, width // 8
 
-    def product(h_ref, dy_ref, o_ref):
-        at = pl.program_id(0) * 8 + pl.program_id(1)
-        for n, when in enumerate((1, 4, 7, 10, 13, 15)):
-            @pl.when(at == when)
-            def _():
-                gather_x.act(n)
-
-        o_ref[...] = dot(h_ref[...], dy_ref[...], TN).astype(BF16)
-
-    def down():
+    def down(loads):
+        def product(h_ref, dy_ref, o_ref):
+            at = pl.program_id(0) * 8 + pl.program_id(1)
+            for n, when in enumerate((1, 4, 7, 10, 13, 15)):
+                @pl.when(at == when)
+                def _():
+                    gather_x.act(n)
+
+            for n, some in enumerate(loads):
+                @pl.when(at == 2 + 2 * n)
+                def _():
+                    for copy in some:
+                        copy.start()
+
+            o_ref[...] = dot(h_ref[...], dy_ref[...], TN).astype(BF16)
+
         pltpu.emit_pipeline(
             product,
             grid=(2, 8),
@@ -390,7 +424,7 @@
             return [across(b), across(b, c)]
         return [across(c)] if k == 2 else [(0, 0, 0)]
 
-    def stage(k, items, out, lag_b, lag_c, prepare=None, filler=None):
+    def stage(k, items, out, lag_b, lag_c, prepare=None, filler=None, between=None):
         count = (4, 2, 1, 1)[k]
         size = n1 if k == 0 else n2
         base = (0, 16, 24, 32)[k]
@@ -498,6 +532,8 @@
                 def _():
                     fetch(i - lag_b)
 
+            if between is not None:
+                between()
             for i in range(items, items + lag_c):
                 j = i - lag_c
                 wait(sources(j))
@@ -516,16 +552,11 @@
         )
 
     loads1 = [lhs_loads(p, 0, stage_chips(p, 0), 8 * p) for p in range(3)]
-    loads2 = [c for p in range(3) for c in lhs_loads(p, 0, stage_chips(p, 1), 24 + 4 * p)]
-    loads3 = [c for p in range(3) for c in lhs_loads(p, 4 * shard, stage_chips(p, 2), 36 + 2 * p)]
+    loads2 = [lhs_loads(p, 0, stage_chips(p, 1), 24 + 4 * p) for p in range(3)]
+    loads3 = [lhs_loads(p, 4 * shard, stage_chips(p, 2), 36 + 2 * p) for p in range(3)]
     loads4 = lhs_loads(0, 6 * shard, stage_chips(0, 3), 42)
     right_load = pltpu.make_async_copy(d_pre, right, right_sem.at[0])
-    for i in range(4):
-        go(narrow_weights(i))
-    for some in loads1:
-        go(some)
-    right_load.start()
-    down()
+    down([[copy for i in range(4) for copy in narrow_weights(i)], loads1[0], loads1[1], loads1[2], [right_load]])
     for some in loads1:
         wait(some)
 
@@ -561,7 +592,7 @@
 
         def fill2(i):
             turn, on = lax.div(i + 1, 3), lax.div(lax.rem(i, 3), 2)
-            tiles(turn - on, turn - on + on * (2 * turn - 1))
+            tiles(turn, turn + on * turn)
 
         def fill3(i):
             turn, on = lax.div(i + 1, 3), lax.div(lax.rem(i, 3), 2)
@@ -573,28 +604,47 @@
 
         def early(out1):
             def prepare(i):
-                @pl.when(i == 5)
+                @pl.when(i == 3)
                 def _():
                     gather_x.act(6)
 
-            stage(0, 16, out1, 1, 3, prepare=prepare)
-            for some in (loads2, loads3, loads4):
-                go(some)
-            gather_x.shared_own()
-            gather_x.shared_all(CHIPS[1:], 0)
-            x_load(0).start()
-            x_load(1).start()
-            right_load.wait()
-            for some in (loads2, loads3, loads4):
-                wait(some)
-            stage(1, 8, out2, 0, 2, filler=fill2)
+                @pl.when(i == 12)
+                def _():
+                    gather_x.shared_own()
+                    gather_x.shared_all(CHIPS[1:], 0)
+                    x_load(0).start()
+                    x_load(1).start()
+                    go(loads2[2])
+                    go(loads3[2])
+
+                @pl.when(i == 15)
+                def _():
+                    go(loads2[0])
+                    go(loads3[0])
+                    go(loads4)
+
+            def between():
+                go(loads2[1])
+                go(loads3[1])
+                right_load.wait()
+                tiles(0, 1)
+
+            def prepare2(i):
+                for p in range(3):
+                    @pl.when(i == p)
+                    def _():
+                        wait(loads2[p])
+
+            stage(0, 16, out1, 1, 3, prepare=prepare, between=between)
+            stage(1, 8, out2, 1, 3, prepare=prepare2, filler=fill2, between=lambda: tiles(4, 5))
             for i in range(16):
                 onward(0, i, 4, narrow(i)[0], lanes(narrow(i)[2], n1), 0, out1.at[i]).wait_send()
 
         pl.run_scoped(early, pltpu.VMEM((16, 4 * shard, n1), BF16))
-        tiles(4, 5)
 
         def late(out3, out4):
+            for some in loads3 + [loads4]:
+                wait(some)
             stage(2, 8, out3, 2, 5, filler=fill3)
             stage(3, 8, out4, 2, 5, filler=fill4)
             dw_store(6).wait()
@@ -619,26 +669,25 @@
     tokens, ff = pre.shape
     dma = pltpu.SemaphoreType.DMA
 
-    def shape(*size, dtype=BF16):
-        return jax.ShapeDtypeStruct(size, dtype)
-
-    x_all, _, d_pre, _, _, dw_down, dx, dw_in, _, _ = pl.pallas_call(
+    def shape(*size):
+        return jax.ShapeDtypeStruct(size, BF16)
+
+    x_all, _, d_pre, _, dw_down, dx, dw_in, _, _ = pl.pallas_call(
         backward_kernel,
         in_specs=[ANY] * 5,
-        out_specs=[ANY] * 10,
+        out_specs=[ANY] * 9,
         out_shape=[
             shape(tokens, width),
             shape(tokens, width),
             shape(tokens, ff),
             shape(tokens, ff),
-            shape(tokens, ff, dtype=F32),
             shape(ff, width),
             shape(shard, width),
             shape(width // 2, ff),
             shape(7 * shard, width),
             shape(8 * shard, width),
         ],
-        scratch_shapes=[dma((n,)) for n in (72, 72, 72, 72, 4, 24, 12, 2, 32, 32, 40, 40, 4, 44, 24, 8, 2, 2, 1)],
+        scratch_shapes=[dma((n,)) for n in (72, 72, 72, 72, 4, 12, 12, 12, 12, 2, 32, 32, 40, 40, 4, 44, 24, 8, 2, 2, 1)],
         compiler_params=pltpu.CompilerParams(collective_id=0, has_side_effects=True, vmem_limit_bytes=VMEM_LIMIT),
         cost_estimate=pl.CostEstimate(flops=7 * tokens * ff * width, bytes_accessed=800_000_000, transcendentals=tokens * ff),
         name="backward",

time: 440 us -> 418 us (0.950)
  Pallas kernels: 435 us -> 414 us
    pallas_call x1, Pallas kernels: 382 us -> 361 us  [backward(): pl.pallas_call(backward_kernel, in_specs=[ANY] * 5, out_specs=[ANY] * 9,...]
where the time goes in v6:
time: 418 us
  Pallas kernels  414 us (99%)
    pallas_call x1, Pallas kernels, backward(): pl.pallas_call(backward_kernel, in_specs=[ANY] * 5, out_specs=[ANY] * 9,...  361 us
    pallas_call x1, Pallas kernels, finish(): pl.pallas_call(finish_kernel, grid=(8,), in_specs=[pl.BlockSpec((tokens,...  52.8 us

profile of v6, /device:TPU:0, one launch (start us, length us, event | category | flops | bytes accessed | tf_op | source)
XLA Modules:
  0.0 417.6 jit_solution(4274859187528175919)
XLA Ops:
  0.6 361.1 %backward.1 = (bf16[2048,8192]{1,0:T(8,128)(2,1)}, bf16[2048,8192]{1,0:T(8,128)(2,1)}, bf16[2048,2048]{1,0:T(8,128)(2,1)}, bf16[2048,2048]{1,0:T(8,128)(2,1)}, b...) custom-call(bf16[128,8192]{1,0:T(8,128)(2,1)} %x.1, ...), custom_call_target="tpu_custom_call" | custom-call | flops 240518168576 | bytes 800000000 | tf_op jit(solution)/shard_map/backward/pallas_call | solution.py:675
  361.8 52.8 %finish.1 = (bf16[8192,2048]{1,0:T(8,128)(2,1)}, bf16[2048,8192]{1,0:T(8,128)(2,1)}) custom-call(bf16[2048,8192]{1,0:T(8,128)(2,1)} %get-tuple-element.11.x_ref, bf16[2048,2048]{1,0:T(8,128)(2,1)} %get-tuple-element.12.d_pre_ref, bf16[4096,2048]{1,0:T(8,128)(2,1)} %get-tuple-element.13.part_ref, bf16[2048,8192]{1,0:T(8,128)(2,1)} %get-tuple-element.14.down_ref), custom_call_target="tpu_custom_call" | custom-call | flops 34359738368 | bytes 140000000 | tf_op jit(solution)/shard_map/finish/pallas_call | solution.py:738
  414.6 3.1 copy.9

commit v7 on v6

--- a/solution.py
+++ b/solution.py
@@ -9,9 +9,9 @@
 
 VMEM_LIMIT = 67_000_000
 WEIGHT = (4, 2, 1)
+HELD = 6
 F32, BF16 = jnp.float32, jnp.bfloat16
 ANY = pl.BlockSpec(memory_space=pl.ANY)
-CHIPS = [(a, b, c) for a in (0, 1) for b in (0, 1) for c in (0, 1)]
 
 
 def act(pre):
@@ -23,6 +23,10 @@
 
 
 NT, TN = ((1,), (1,)), ((0,), (0,))
+
+
+def odd(i):
+    return lax.rem(i, 2)
 
 
 def rows(start, size):
@@ -69,6 +73,11 @@
 
 def across(*dims):
     return tuple(int(d in dims) for d in range(3))
+
+
+HERE, NEAR, FAR = [across()], [across(d) for d in range(3)], [across(*range(3))]
+MIDDLE = [across(*order(d)[:2]) for d in range(3)]
+OTHERS = NEAR + MIDDLE + FAR
 
 
 class Gather:
@@ -145,15 +154,9 @@
         self.share_own().wait_send()
         for h in range(self.halves):
             for p in range(3):
-                for r in CHIPS[1:]:
+                for r in OTHERS:
                     self.hop(p, r, h).wait_send()
                     self.share(p, r, h).wait_send()
-
-
-NEAR = [(1, 0, 0), (0, 1, 0), (0, 0, 1)]
-MIDDLE = [(1, 1, 0), (0, 1, 1), (1, 0, 1)]
-FAR = [(1, 1, 1)]
-HERE = [(0, 0, 0)]
 
 
 def backward_kernel(x, dy, pre, w_down, w_in, x_all, dy_all, d_pre, hidden, dw_down, dx, dw_in, ici, d2d,
@@ -223,36 +226,43 @@
             for copy in hidden_stores(n):
                 copy.start()
 
-        own_row = pltpu.make_async_copy(lhs.at[0, pl.ds(0, shard)], dy_all.at[mine], own_sem.at[0])
+        first = pl.ds(0, shard)
+        own_row = pltpu.make_async_copy(lhs.at[0, first], dy_all.at[mine], own_sem.at[0])
+        own_x = [
+            pltpu.make_async_copy(x, lhs.at[1, first], own_sem.at[1]),
+            pltpu.make_async_copy(lhs.at[1, first], x_all.at[mine], own_sem.at[1]),
+        ]
+
+        def arrivals(n):
+            chips, h = batches[n]
+            if chips is FAR:
+                return [(6, 0), (6, 1)]
+            return [(k + 3 * (chips is MIDDLE), h) for k in range(3)]
+
+        def row_loads(n, mine):
+            return [row_load(n, k) for k in range(1 - mine, len(parts(n)), 2)]
 
         for copy in pre_loads(0):
             copy.start()
         row_load(0, 0).start()
+        load_weights(0).start()
         for copy in pre_loads(1):
             copy.start()
-        for j in range(4):
-            load_weights(j).start()
         gelu(0)
         gather_dy.shared_own()
         row_load(0, 1).start()
-        gelu(1)
+        for j in range(1, 4):
+            load_weights(j).start()
+        own_x[0].start()
         row_load(0, 0).wait()
         own_row.start()
         row_load(0, 1).wait()
 
-        passes = [
-            ([(0, 0)], [(1, 0)], [(2, 0)]),
-            ([(0, 1)], [(1, 1)], [(2, 1)]),
-            ([(3, 0)], [(4, 0)], [(5, 0)]),
-            ([(3, 1)], [(4, 1)], [(5, 1)]),
-            ([(6, 0)], [(6, 1)], []),
-            ([], [], []),
-        ]
         for n in range(6):
             if n:
-                for k in range(len(parts(n))):
-                    row_load(n, k).wait()
-            if n < 4:
+                for copy in row_loads(n, True) + row_loads(n, False):
+                    copy.wait()
+            if n < 4 and n != 1:
                 for copy in hidden_stores(n):
                     copy.wait()
                 for copy in pre_loads(n + 2):
@@ -261,17 +271,16 @@
                 for copy in stores(n - 2):
                     copy.wait()
             size, slot = rows_in(n), n % 2
+            pieces = arrivals(n + 1) if n < 5 else []
 
             @pl.loop(0, 4)
             def _(j):
                 if n == 0:
                     load_weights(j).wait()
-                for at in (2, 3):
-                    if passes[n][at - 2]:
-                        @pl.when(j == at)
-                        def _():
-                            for k, h in passes[n][at - 2]:
-                                gather_dy.act(k, h)
+                for at, (k, h) in enumerate(pieces[:2]):
+                    @pl.when(j == at + 2)
+                    def _():
+                        gather_dy.act(k, h)
 
                 columns = lanes(j * block, block)
                 d_hidden = dot(lhs[slot, :size], weights[rows(j * block, block), :], NT)
@@ -279,31 +288,34 @@
 
             for copy in stores(n):
                 copy.start()
+            if n == 0:
+                own_x[0].wait()
+                own_x[1].start()
+                gelu(1)
+                own_x[1].wait()
+                for copy in hidden_stores(1):
+                    copy.wait()
+                for copy in pre_loads(3):
+                    copy.start()
             if n == 3:
                 gather_x.begin()
             if n < 4:
                 gelu(n + 2)
-            for k, h in passes[n][2]:
+            for k, h in pieces[2:]:
                 gather_dy.act(k, h)
             if n < 5:
+                if n == 1:
+                    own_row.wait()
+                for copy in row_loads(n + 1, True):
+                    copy.start()
                 chips, h = batches[n + 1]
                 for h in (0, 1) if h is None else (h,):
                     gather_dy.shared_all(chips, h)
-                if n == 1:
-                    own_row.wait()
-                for k in range(len(parts(n + 1))):
-                    row_load(n + 1, k).start()
-        taken = pltpu.make_async_copy(x, lhs.at[0, pl.ds(0, shard)], own_sem.at[0])
-        taken.start()
+                for copy in row_loads(n + 1, False):
+                    copy.start()
         for n in (4, 5):
-            for copy in hidden_stores(n):
+            for copy in hidden_stores(n) + stores(n):
                 copy.wait()
-            for copy in stores(n):
-                copy.wait()
-        taken.wait()
-        put = pltpu.make_async_copy(lhs.at[0, pl.ds(0, shard)], x_all.at[mine], own_sem.at[1])
-        put.start()
-        put.wait()
 
     pl.run_scoped(
         gradient,
@@ -318,17 +330,27 @@
 
     def down(loads):
         def product(h_ref, dy_ref, o_ref):
-            at = pl.program_id(0) * 8 + pl.program_id(1)
-            for n, when in enumerate((1, 4, 7, 10, 13, 15)):
-                @pl.when(at == when)
-                def _():
-                    gather_x.act(n)
-
-            for n, some in enumerate(loads):
-                @pl.when(at == 2 + 2 * n)
-                def _():
-                    for copy in some:
-                        copy.start()
+            at = pl.program_id(0) * pl.num_programs(1) + pl.program_id(1)
+            group, place_in = lax.div(at, 3), lax.rem(at, 3)
+
+            @pl.when(place_in == 1)
+            def _():
+                for n in range(5):
+                    @pl.when(group == n)
+                    def _():
+                        gather_x.act(n)
+
+            @pl.when(place_in == 2)
+            def _():
+                for n, some in enumerate(loads):
+                    @pl.when(group == n)
+                    def _():
+                        for copy in some:
+                            copy.start()
+
+            @pl.when(at == 15)
+            def _():
+                gather_x.act(5)
 
             o_ref[...] = dot(h_ref[...], dy_ref[...], TN).astype(BF16)
 
@@ -358,7 +380,7 @@
 
     def pick(i, group):
         k = lax.div(i, 3 * group)
-        p = (1 - k) * lax.rem(i, 3) + k * lax.rem(i, 2)
+        p = (1 - k) * lax.rem(i, 3) + k * odd(i)
         t = (1 - k) * lax.div(i, 3) + k * (group + lax.div(i - 3 * group, 2))
         return p, t
 
@@ -382,7 +404,7 @@
         return [pltpu.make_async_copy(w_in.at[rows(narrow(i)[2], n1)], weights.at[rows(slot * n1, n1)], w_sem.at[slot])]
 
     def wide_weights(i):
-        start, slot = wide(i)[2], lax.rem(i, 2)
+        start, slot = wide(i)[2], odd(i)
         return [
             pltpu.make_async_copy(w_in.at[rows(start + h * n1, n1)], weights.at[rows(slot * n2 + h * n1, n1)], w_sem.at[2 * slot + h])
             for h in (0, 1)
@@ -405,8 +427,8 @@
                 loads.append(pltpu.make_async_copy(src, lhs_buf.at[p, pl.ds(first + n * shard, shard)], load_sem.at[base + n]))
         return loads
 
-    def exchange(k, i, count, size, columns, base, part):
-        region = (0, 4, 6, 7)[k]
+    def exchange(k, i, count, columns, base, part):
+        region = (0, 4, 6)[k]
         dst = d2d.at[pl.ds(region * shard, count * shard), columns]
         return remote(part, dst, d2d_send.at[base + i], d2d_recv.at[base + i], place.sibling)
 
@@ -422,23 +444,23 @@
             return [tuple(across(a)[d] + s * across(b)[d] + t * across(c)[d] for d in range(3)) for s, t in tail]
         if k == 1:
             return [across(b), across(b, c)]
-        return [across(c)] if k == 2 else [(0, 0, 0)]
-
-    def stage(k, items, out, lag_b, lag_c, prepare=None, filler=None, between=None):
-        count = (4, 2, 1, 1)[k]
+        return [across(c)] + HERE
+
+    def stage(k, items, out, between, prepare=None, filler=None, keep=None, lag_b=1, lag_c=3):
+        count, moved = (4, 2, 1)[k], (4, 2, 2)[k]
         size = n1 if k == 0 else n2
-        base = (0, 16, 24, 32)[k]
+        base = (0, 16, 24)[k]
         locate = narrow if k == 0 else wide
-        slots, n_term, n_staged = lag_c, 2, lag_c - lag_b + 1
+        slots, n_term, n_staged = lag_c, 2, lag_c
         n_in = 1 + k
-        from_ici = [(), ((2, 4),), ((1, 2), (5, 6)), ((0, 1), (4, 5), (6, 7))][k]
+        from_ici = [(), ((2, 4),), ((1, 2), (5, 6))][k]
 
         def body(acc, term, staged):
             def columns(i):
                 return lanes(locate(i)[2], size)
 
             def sources(i):
-                region = (0, 4, 6, 7)[k]
+                region = (0, 4, 6)[k]
                 views = [d2d.at[pl.ds(region * shard, count * shard), columns(i)]]
                 views += [ici.at[pl.ds(a * shard, (b - a) * shard), columns(i)] for a, b in from_ici]
                 slot = lax.rem(i, n_staged)
@@ -447,25 +469,23 @@
                 ]
 
             def send(i):
-                return exchange(k, i, count, size, columns(i), base, term.at[lax.rem(i, n_term)])
+                return exchange(k, i, moved, columns(i), base, term.at[lax.rem(i, n_term)])
 
             def leave(i):
-                if k < 3:
-                    return onward(k, i, count, locate(i)[0], columns(i), base, out.at[i])
-                return pltpu.make_async_copy(out.at[i], dx.at[:, columns(i)], dx_sem.at[i])
+                return onward(k, i, count, locate(i)[0], columns(i), base, out.at[i])
 
             def fetch(j):
-                view = d2d.at[pl.ds(0, count * shard), columns(j)]
+                view = d2d.at[pl.ds(0, moved * shard), columns(j)]
                 remote(view, view, d2d_send.at[base + j], d2d_recv.at[base + j], place.sibling).wait_recv()
                 p, t, start = locate(j)
                 if k == 1:
-                    for h in (0, 1):
+                    for h in range(2):
                         n = unpick(p, 2 * t + h, 4)
                         view = ici.at[pl.ds(0, 4 * shard), lanes(start + h * n1, n1)]
                         remote(view, view, ici_send.at[n], ici_recv.at[n], place.sibling).wait_recv()
-                elif k > 1:
-                    n = (16, 24)[k - 2] + j
-                    view = ici.at[pl.ds(0, (2, 1)[k - 2] * shard), columns(j)]
+                elif k == 2:
+                    n = 16 + j
+                    view = ici.at[pl.ds(0, 2 * shard), columns(j)]
                     remote(view, view, ici_send.at[n], ici_recv.at[n], place.sibling).wait_recv()
                 go(sources(j))
 
@@ -491,15 +511,16 @@
                 def _():
                     wait(sources(i - lag_c))
 
-                add(lax.max(i - lag_c, 0), slot, lax.rem(i + n_staged * lag_c - lag_c, n_staged))
+                add(lax.max(i - lag_c, 0), slot, lax.rem(i, n_staged))
                 if k == 0:
                     w = weights[rows(lax.rem(i, 4) * n1, n1), :]
                 else:
-                    w = weights[rows(lax.rem(i, 2) * n2, n2), :]
-                where = ((0, 8), (0, 4), (4, 2), (6, 2))[k]
-                value = dot(lhs_buf[0 if k == 3 else p, pl.ds(where[0] * shard, where[1] * shard)], w, NT)
-                term[lax.rem(i, n_term)] = value[: count * shard].astype(BF16)
-                acc[slot] = value[count * shard :]
+                    w = weights[rows(odd(i) * n2, n2), :]
+                value = dot(lhs_buf[p, pl.ds((k // 2) * 4 * shard, 2 * moved * shard)], w, NT)
+                term[lax.rem(i, n_term)] = value[: moved * shard].astype(BF16)
+                acc[slot] = value[moved * shard : (moved + count) * shard]
+                if k == 2:
+                    keep[i] = value[(moved + count) * shard :]
                 send(i).start()
 
                 @pl.when(i >= lag_c)
@@ -518,8 +539,8 @@
                     @pl.when(i == items - 1)
                     def _():
                         go(wide_weights(1))
-                elif k < 3:
-                    go(wide_weights(lax.rem(i + 2, 8)))
+                elif k == 1:
+                    go(wide_weights(lax.rem(i + 2, items)))
                 else:
                     @pl.when(i + 2 < items)
                     def _():
@@ -532,47 +553,44 @@
                 def _():
                     fetch(i - lag_b)
 
-            if between is not None:
-                between()
-            for i in range(items, items + lag_c):
-                j = i - lag_c
+            between()
+            for j in range(items - lag_b, items):
+                fetch(j)
+            for j in range(items - lag_c, items):
                 wait(sources(j))
                 add(j, j % slots, j % n_staged)
                 leave(j).start()
-                if i - lag_b < items:
-                    fetch(i - lag_b)
             for i in range(items - n_term, items):
                 send(i).wait_send()
 
         pl.run_scoped(
             body,
             pltpu.VMEM((slots, count * shard, size), F32),
-            pltpu.VMEM((n_term, count * shard, size), BF16),
+            pltpu.VMEM((n_term, moved * shard, size), BF16),
             pltpu.VMEM((n_staged, n_in, count * shard, size), BF16),
         )
 
     loads1 = [lhs_loads(p, 0, stage_chips(p, 0), 8 * p) for p in range(3)]
     loads2 = [lhs_loads(p, 0, stage_chips(p, 1), 24 + 4 * p) for p in range(3)]
-    loads3 = [lhs_loads(p, 4 * shard, stage_chips(p, 2), 36 + 2 * p) for p in range(3)]
-    loads4 = lhs_loads(0, 6 * shard, stage_chips(0, 3), 42)
+    loads3 = [lhs_loads(p, 4 * shard, stage_chips(p, 2), 36 + 4 * p) for p in range(3)]
     right_load = pltpu.make_async_copy(d_pre, right, right_sem.at[0])
-    down([[copy for i in range(4) for copy in narrow_weights(i)], loads1[0], loads1[1], loads1[2], [right_load]])
+    down([[copy for i in range(4) for copy in narrow_weights(i)], *loads1, [right_load]])
     for some in loads1:
         wait(some)
 
     def main(out2, x_buf, dw_buf):
         def x_load(i):
-            slot = lax.rem(i, 2)
+            slot = odd(i)
             return pltpu.make_async_copy(x_all.at[:, lanes(i * n1, n1)], x_buf.at[slot], x_sem.at[slot])
 
         def dw_store(i):
-            slot = lax.rem(i, 2)
+            slot = odd(i)
             return pltpu.make_async_copy(dw_buf.at[slot], dw_in.at[rows(i * n1, n1)], dw_sem.at[slot])
 
         def tiles(a, b):
             @pl.loop(a, b)
             def _(i):
-                slot = lax.rem(i, 2)
+                slot = odd(i)
                 x_load(i).wait()
 
                 @pl.when(i >= 2)
@@ -586,21 +604,17 @@
 
                 dw_store(i).start()
 
-                @pl.when(i + 2 < 8)
+                @pl.when(i + 2 < HELD)
                 def _():
                     x_load(i + 2).start()
 
         def fill2(i):
             turn, on = lax.div(i + 1, 3), lax.div(lax.rem(i, 3), 2)
-            tiles(turn, turn + on * turn)
+            tiles(turn, turn + on)
 
         def fill3(i):
-            turn, on = lax.div(i + 1, 3), lax.div(lax.rem(i, 3), 2)
-            tiles(4 + turn, 4 + turn + on)
-
-        def fill4(i):
             on = lax.div(lax.rem(i, 3), 2) * lax.div(i, 3)
-            tiles(7, 7 + on)
+            tiles(4, 4 + on)
 
         def early(out1):
             def prepare(i):
@@ -611,21 +625,17 @@
                 @pl.when(i == 12)
                 def _():
                     gather_x.shared_own()
-                    gather_x.shared_all(CHIPS[1:], 0)
+                    gather_x.shared_all(OTHERS, 0)
                     x_load(0).start()
                     x_load(1).start()
-                    go(loads2[2])
-                    go(loads3[2])
+                    go(loads2[2] + loads3[2])
 
                 @pl.when(i == 15)
                 def _():
-                    go(loads2[0])
-                    go(loads3[0])
-                    go(loads4)
+                    go(loads2[0] + loads3[0])
 
             def between():
-                go(loads2[1])
-                go(loads3[1])
+                go(loads2[1] + loads3[1])
                 right_load.wait()
                 tiles(0, 1)
 
@@ -633,28 +643,59 @@
                 for p in range(3):
                     @pl.when(i == p)
                     def _():
-                        wait(loads2[p])
-
-            stage(0, 16, out1, 1, 3, prepare=prepare, between=between)
-            stage(1, 8, out2, 1, 3, prepare=prepare2, filler=fill2, between=lambda: tiles(4, 5))
+                        wait(loads2[p] + loads3[p])
+
+            stage(0, 16, out1, between, prepare=prepare)
+            stage(1, 8, out2, lambda: tiles(3, 4), prepare=prepare2, filler=fill2)
             for i in range(16):
                 onward(0, i, 4, narrow(i)[0], lanes(narrow(i)[2], n1), 0, out1.at[i]).wait_send()
 
         pl.run_scoped(early, pltpu.VMEM((16, 4 * shard, n1), BF16))
 
-        def late(out3, out4):
-            for some in loads3 + [loads4]:
-                wait(some)
-            stage(2, 8, out3, 2, 5, filler=fill3)
-            stage(3, 8, out4, 2, 5, filler=fill4)
-            dw_store(6).wait()
-            dw_store(7).wait()
+        def late(out3, keep):
+            stage(2, 8, out3, lambda: tiles(5, 6), filler=fill3, keep=keep)
+            pl.run_scoped(functools.partial(final, keep), pltpu.VMEM((8, shard, n2), BF16), pltpu.VMEM((4, 4, shard, n2), BF16))
             for i in range(8):
                 onward(1, i, 2, wide(i)[0], lanes(wide(i)[2], n2), 16, out2.at[i]).wait_send()
                 onward(2, i, 1, wide(i)[0], lanes(wide(i)[2], n2), 24, out3.at[i]).wait_send()
-                pltpu.make_async_copy(out4.at[i], dx.at[:, lanes(wide(i)[2], n2)], dx_sem.at[i]).wait()
-
-        pl.run_scoped(late, pltpu.VMEM((8, shard, n2), BF16), pltpu.VMEM((8, shard, n2), BF16))
+
+        def final(keep, out4, staged):
+            def columns(i):
+                return lanes(wide(i)[2], n2)
+
+            def sources(i):
+                views = [d2d.at[pl.ds(7 * shard, shard), columns(i)]]
+                views += [ici.at[pl.ds(n * shard, shard), columns(i)] for n in (0, 4, 6)]
+                slot = lax.rem(i, 4)
+                return [pltpu.make_async_copy(view, staged.at[slot, n], stage_sem.at[4 * slot + n]) for n, view in enumerate(views)]
+
+            def store(i):
+                return pltpu.make_async_copy(out4.at[i], dx.at[:, columns(i)], dx_sem.at[i])
+
+            @pl.loop(0, 8 + 3)
+            def _(i):
+                @pl.when(i >= 3)
+                def _():
+                    j = i - 3
+                    wait(sources(j))
+                    total = keep[j]
+                    for n in range(4):
+                        total = total + staged[lax.rem(j, 4), n].astype(F32)
+                    out4[j] = total.astype(BF16)
+                    store(j).start()
+
+                @pl.when(i < 8)
+                def _():
+                    view = ici.at[pl.ds(0, shard), columns(i)]
+                    remote(view, view, ici_send.at[24 + i], ici_recv.at[24 + i], place.sibling).wait_recv()
+                    go(sources(i))
+
+            dw_store(HELD - 2).wait()
+            dw_store(HELD - 1).wait()
+            for i in range(8):
+                store(i).wait()
+
+        pl.run_scoped(late, pltpu.VMEM((8, shard, n2), BF16), pltpu.VMEM((8, shard, n2), F32))
 
     pl.run_scoped(
         main,
@@ -683,11 +724,11 @@
             shape(tokens, ff),
             shape(ff, width),
             shape(shard, width),
-            shape(width // 2, ff),
+            shape(HELD * width // 16, ff),
             shape(7 * shard, width),
             shape(8 * shard, width),
         ],
-        scratch_shapes=[dma((n,)) for n in (72, 72, 72, 72, 4, 12, 12, 12, 12, 2, 32, 32, 40, 40, 4, 44, 24, 8, 2, 2, 1)],
+        scratch_shapes=[dma((n,)) for n in [72] * 4 + [4] + [12] * 4 + [2] + [32] * 4 + [4, 48, 16, 8, 2, 2, 1]],
         compiler_params=pltpu.CompilerParams(collective_id=0, has_side_effects=True, vmem_limit_bytes=VMEM_LIMIT),
         cost_estimate=pl.CostEstimate(flops=7 * tokens * ff * width, bytes_accessed=800_000_000, transcendentals=tokens * ff),
         name="backward",
@@ -695,38 +736,77 @@
     return x_all, d_pre, dw_down, dx, dw_in
 
 
-def finish_kernel(x_ref, d_pre_ref, part_ref, down_ref, dw_in, dw_down, buf, copy_sem, buf_sem):
-    i = pl.program_id(0)
-    n, ff = part_ref.shape
-    count = pl.num_programs(0)
-    slot = lax.rem(i, 2)
-    copies = [
-        pltpu.make_async_copy(part_ref, dw_in.at[rows(i * n, n)], copy_sem.at[0]),
-        pltpu.make_async_copy(down_ref, dw_down.at[rows(i * down_ref.shape[0], down_ref.shape[0])], copy_sem.at[1]),
-    ]
+def finish_kernel(x_ref, d_pre, part, down, dw_in, dw_down, right, buf, copies, tiles, right_sem, buf_sem, in_sem, out_sem):
+    i, steps = pl.program_id(0), 16 - HELD
+    n, ff = buf.shape[1:]
+    slot = odd(i)
+    piece = down.shape[0] // 16
+
+    def right_load(h):
+        half = pl.ds(h * (ff // 2), ff // 2)
+        return pltpu.make_async_copy(d_pre.at[:, half], right.at[h], right_sem.at[h])
 
     def store(i):
-        slot = lax.rem(i, 2)
-        return pltpu.make_async_copy(buf.at[slot], dw_in.at[rows((count + i) * n, n)], buf_sem.at[slot])
-
-    for copy in copies:
-        copy.start()
+        slot = odd(i)
+        return pltpu.make_async_copy(buf.at[slot], dw_in.at[rows((HELD + i) * n, n)], buf_sem.at[slot])
+
+    after = steps - HELD
+
+    def moves(i, n_):
+        at = 3 * odd(i) + n_
+        held = copies.at[2 * odd(i) + n_] if n_ < 2 else tiles.at[odd(i)]
+        where, k, size = (down, 2 * i + n_, piece) if n_ < 2 else (part, i - after, n)
+        to = dw_down if n_ < 2 else dw_in
+        span = rows(k * size, size)
+        return (
+            pltpu.make_async_copy(where.at[span], held, in_sem.at[at]),
+            pltpu.make_async_copy(held, to.at[span], out_sem.at[at]),
+        )
+
+    def each(i, f):
+        for n_ in range(3):
+            @pl.when((i < 8) if n_ < 2 else ((i >= after) & (i < steps)))
+            def _():
+                f(*moves(i, n_))
+
+    @pl.when(i == 0)
+    def _():
+        right_load(0).start()
+        right_load(1).start()
+        each(i, lambda into, out_of: into.start())
 
     @pl.when(i >= 2)
     def _():
         store(i - 2).wait()
 
-    @pl.loop(0, 2)
-    def _(h):
-        half = lanes(h * (ff // 2), ff // 2)
-        buf[slot, :, half] = dot(x_ref[...], d_pre_ref[:, half], TN).astype(BF16)
+    @pl.when(i > 0)
+    def _():
+        each(i - 1, lambda into, out_of: out_of.wait())
+
+    @pl.when(i + 1 < steps)
+    def _():
+        each(i + 1, lambda into, out_of: into.start())
+
+    @pl.when(i > 0)
+    def _():
+        each(i, lambda into, out_of: (into.wait(), out_of.start()))
+
+    for h in range(2):
+        @pl.when(i == 0)
+        def _():
+            right_load(h).wait()
+
+        buf[slot, :, pl.ds(h * (ff // 2), ff // 2)] = dot(x_ref[...], right[h], TN).astype(BF16)
 
     store(i).start()
-    for copy in copies:
-        copy.wait()
-
-    @pl.when(i == count - 1)
+
+    @pl.when(i == 0)
     def _():
+        each(i, lambda into, out_of: (into.wait(), out_of.start()))
+
+    @pl.when(i == steps - 1)
+    def _():
+        each(i, lambda into, out_of: out_of.wait())
         store(i - 1).wait()
         store(i).wait()
 
@@ -735,18 +815,23 @@
     tokens, ff = d_pre.shape
     width = x_all.shape[1]
     n = width // 16
+    dma = pltpu.SemaphoreType.DMA
     return pl.pallas_call(
         finish_kernel,
-        grid=(8,),
-        in_specs=[
-            pl.BlockSpec((tokens, n), lambda i: (0, 8 + i)),
-            pl.BlockSpec((tokens, ff), lambda i: (0, 0)),
-            pl.BlockSpec((n, ff), lambda i: (i, 0)),
-            pl.BlockSpec((ff // 8, width), lambda i: (i, 0)),
-        ],
+        grid=(16 - HELD,),
+        in_specs=[pl.BlockSpec((tokens, n), lambda i: (0, HELD + i)), ANY, ANY, ANY],
         out_specs=[ANY] * 2,
         out_shape=[jax.ShapeDtypeStruct((width, ff), BF16), jax.ShapeDtypeStruct((ff, width), BF16)],
-        scratch_shapes=[pltpu.VMEM((2, n, ff), BF16), pltpu.SemaphoreType.DMA((2,)), pltpu.SemaphoreType.DMA((2,))],
+        scratch_shapes=[
+            pltpu.VMEM((2, tokens, ff // 2), BF16),
+            pltpu.VMEM((2, n, ff), BF16),
+            pltpu.VMEM((4, ff // 16, width), BF16),
+            pltpu.VMEM((2, n, ff), BF16),
+            dma((2,)),
+            dma((2,)),
+            dma((6,)),
+            dma((6,)),
+        ],
         compiler_params=pltpu.CompilerParams(dimension_semantics=("arbitrary",), vmem_limit_bytes=VMEM_LIMIT),
         cost_estimate=pl.CostEstimate(flops=tokens * ff * width, bytes_accessed=140_000_000, transcendentals=0),
         name="finish",

time: 418 us -> 419 us (level)
    pallas_call x1, Pallas kernels: 52.8 us -> 60.8 us  [finish(): pl.pallas_call(finish_kernel, grid=(16 - HELD,), in_specs=[pl.BlockSpec((...]
    pallas_call x1, Pallas kernels: 361 us -> 354 us  [backward(): pl.pallas_call(backward_kernel, in_specs=[ANY] * 5, out_specs=[ANY] * 9,...]
where the time goes in v7:
time: 419 us; the launch traced here: 418 us
  Pallas kernels  415 us (99%)
    pallas_call x1, Pallas kernels, backward(): pl.pallas_call(backward_kernel, in_specs=[ANY] * 5, out_specs=[ANY] * 9,...  354 us
    pallas_call x1, Pallas kernels, finish(): pl.pallas_call(finish_kernel, grid=(16 - HELD,), in_specs=[pl.BlockSpec((...  60.8 us

profile of v7, /device:TPU:0, one launch (start us, length us, event | category | flops | bytes accessed | tf_op | source)
XLA Modules:
  0.0 418.3 jit_solution(15652529093830525834)
XLA Ops:
  0.6 353.8 %backward.1 = (bf16[2048,8192]{1,0:T(8,128)(2,1)}, bf16[2048,8192]{1,0:T(8,128)(2,1)}, bf16[2048,2048]{1,0:T(8,128)(2,1)}, bf16[2048,2048]{1,0:T(8,128)(2,1)}, b...) custom-call(bf16[128,8192]{1,0:T(8,128)(2,1)} %x.1, ...), custom_call_target="tpu_custom_call" | custom-call | flops 240518168576 | bytes 800000000 | tf_op jit(solution)/shard_map/backward/pallas_call | solution.py:716
  354.4 60.8 %finish.1 = (bf16[8192,2048]{1,0:T(8,128)(2,1)}, bf16[2048,8192]{1,0:T(8,128)(2,1)}) custom-call(bf16[2048,8192]{1,0:T(8,128)(2,1)} %get-tuple-element.11.x_ref, bf16[2048,2048]{1,0:T(8,128)(2,1)} %get-tuple-element.12.d_pre, bf16[3072,2048]{1,0:T(8,128)(2,1)} %get-tuple-element.13.part, bf16[2048,8192]{1,0:T(8,128)(2,1)} %get-tuple-element.14.down), custom_call_target="tpu_custom_call" | custom-call | flops 34359738368 | bytes 140000000 | tf_op jit(solution)/shard_map/finish/pallas_call | solution.py:819
  415.2 3.1 copy.9

commit v8 on v7

--- a/solution.py
+++ b/solution.py
@@ -9,7 +9,7 @@
 
 VMEM_LIMIT = 67_000_000
 WEIGHT = (4, 2, 1)
-HELD = 6
+HELD = 8
 F32, BF16 = jnp.float32, jnp.bfloat16
 ANY = pl.BlockSpec(memory_space=pl.ANY)
 
@@ -81,13 +81,13 @@
 
 
 class Gather:
-    def __init__(self, place, src, dst, sems, base, halves):
+    def __init__(self, place, src, dst, sems, base, halves, shares):
         self.place, self.src, self.dst, self.halves = place, src, dst, halves
         self.shard, width = src.shape
         self.size = self.shard // halves
         self.send, self.recv, self.out, self.back = (functools.partial(lambda s, i: s.at[base + i], s) for s in sems)
         tiles = width // 128
-        ends = [128 * (tiles * k // 3) for k in range(4)]
+        ends = [128 * (tiles * sum(shares[:k]) // sum(shares)) for k in range(4)]
         self.columns = [pl.ds(ends[k], ends[k + 1] - ends[k]) for k in range(3)]
 
     def rows_of(self, r, core, h=None):
@@ -168,8 +168,8 @@
     block = ff // 4
     place.barrier()
     sems = (send, recv, out, back)
-    gather_dy = Gather(place, dy, dy_all, sems, 0, 2)
-    gather_x = Gather(place, x, x_all, sems, 48, 1)
+    gather_dy = Gather(place, dy, dy_all, sems, 0, 2, (22, 21, 21))
+    gather_x = Gather(place, x, x_all, sems, 48, 1, (25, 22, 17))
     gather_dy.begin()
     mine = gather_dy.rows_of(HERE[0], place.core)
     batches = [(HERE, None), (NEAR, 0), (NEAR, 1), (MIDDLE, 0), (MIDDLE, 1), (FAR, None)]
@@ -610,11 +610,11 @@
 
         def fill2(i):
             turn, on = lax.div(i + 1, 3), lax.div(lax.rem(i, 3), 2)
-            tiles(turn, turn + on)
+            tiles(turn, turn + on * turn)
 
         def fill3(i):
-            on = lax.div(lax.rem(i, 3), 2) * lax.div(i, 3)
-            tiles(4, 4 + on)
+            turn, on = lax.div(i + 1, 3), lax.div(lax.rem(i, 3), 2)
+            tiles(4 + turn, 4 + turn + on)
 
         def early(out1):
             def prepare(i):
@@ -646,14 +646,14 @@
                         wait(loads2[p] + loads3[p])
 
             stage(0, 16, out1, between, prepare=prepare)
-            stage(1, 8, out2, lambda: tiles(3, 4), prepare=prepare2, filler=fill2)
+            stage(1, 8, out2, lambda: tiles(4, 5), prepare=prepare2, filler=fill2)
             for i in range(16):
                 onward(0, i, 4, narrow(i)[0], lanes(narrow(i)[2], n1), 0, out1.at[i]).wait_send()
 
         pl.run_scoped(early, pltpu.VMEM((16, 4 * shard, n1), BF16))
 
         def late(out3, keep):
-            stage(2, 8, out3, lambda: tiles(5, 6), filler=fill3, keep=keep)
+            stage(2, 8, out3, lambda: tiles(7, 8), filler=fill3, keep=keep)
             pl.run_scoped(functools.partial(final, keep), pltpu.VMEM((8, shard, n2), BF16), pltpu.VMEM((4, 4, shard, n2), BF16))
             for i in range(8):
                 onward(1, i, 2, wide(i)[0], lanes(wide(i)[2], n2), 16, out2.at[i]).wait_send()
@@ -736,112 +736,81 @@
     return x_all, d_pre, dw_down, dx, dw_in
 
 
-def finish_kernel(x_ref, d_pre, part, down, dw_in, dw_down, right, buf, copies, tiles, right_sem, buf_sem, in_sem, out_sem):
-    i, steps = pl.program_id(0), 16 - HELD
-    n, ff = buf.shape[1:]
-    slot = odd(i)
-    piece = down.shape[0] // 16
-
-    def right_load(h):
-        half = pl.ds(h * (ff // 2), ff // 2)
-        return pltpu.make_async_copy(d_pre.at[:, half], right.at[h], right_sem.at[h])
+def finish_kernel(x_ref, d_pre_ref, part_ref, down_ref, dx_part, dw_in, dw_down, dx, buf, dx_buf, copy_sem, buf_sem, dx_sem):
+    i = pl.program_id(0)
+    n, ff = part_ref.shape
+    count = pl.num_programs(0)
+    slot = lax.rem(i, 2)
+    copies = [
+        pltpu.make_async_copy(part_ref, dw_in.at[rows(i * n, n)], copy_sem.at[0]),
+        pltpu.make_async_copy(down_ref, dw_down.at[rows(i * down_ref.shape[0], down_ref.shape[0])], copy_sem.at[1]),
+    ]
 
     def store(i):
-        slot = odd(i)
-        return pltpu.make_async_copy(buf.at[slot], dw_in.at[rows((HELD + i) * n, n)], buf_sem.at[slot])
-
-    after = steps - HELD
-
-    def moves(i, n_):
-        at = 3 * odd(i) + n_
-        held = copies.at[2 * odd(i) + n_] if n_ < 2 else tiles.at[odd(i)]
-        where, k, size = (down, 2 * i + n_, piece) if n_ < 2 else (part, i - after, n)
-        to = dw_down if n_ < 2 else dw_in
-        span = rows(k * size, size)
-        return (
-            pltpu.make_async_copy(where.at[span], held, in_sem.at[at]),
-            pltpu.make_async_copy(held, to.at[span], out_sem.at[at]),
-        )
-
-    def each(i, f):
-        for n_ in range(3):
-            @pl.when((i < 8) if n_ < 2 else ((i >= after) & (i < steps)))
-            def _():
-                f(*moves(i, n_))
+        slot = lax.rem(i, 2)
+        return pltpu.make_async_copy(buf.at[slot], dw_in.at[rows((count + i) * n, n)], buf_sem.at[slot])
+
+    for copy in copies:
+        copy.start()
+
+    through = [pltpu.make_async_copy(dx_part, dx_buf, dx_sem.at[0]), pltpu.make_async_copy(dx_buf, dx, dx_sem.at[1])]
 
     @pl.when(i == 0)
     def _():
-        right_load(0).start()
-        right_load(1).start()
-        each(i, lambda into, out_of: into.start())
+        through[0].start()
+
+    @pl.when(i == 1)
+    def _():
+        through[0].wait()
+        through[1].start()
 
     @pl.when(i >= 2)
     def _():
         store(i - 2).wait()
 
-    @pl.when(i > 0)
+    @pl.loop(0, 2)
+    def _(h):
+        half = lanes(h * (ff // 2), ff // 2)
+        buf[slot, :, half] = dot(x_ref[...], d_pre_ref[:, half], TN).astype(BF16)
+
+    store(i).start()
+    for copy in copies:
+        copy.wait()
+
+    @pl.when(i == count - 1)
     def _():
-        each(i - 1, lambda into, out_of: out_of.wait())
-
-    @pl.when(i + 1 < steps)
-    def _():
-        each(i + 1, lambda into, out_of: into.start())
-
-    @pl.when(i > 0)
-    def _():
-        each(i, lambda into, out_of: (into.wait(), out_of.start()))
-
-    for h in range(2):
-        @pl.when(i == 0)
-        def _():
-            right_load(h).wait()
-
-        buf[slot, :, pl.ds(h * (ff // 2), ff // 2)] = dot(x_ref[...], right[h], TN).astype(BF16)
-
-    store(i).start()
-
-    @pl.when(i == 0)
-    def _():
-        each(i, lambda into, out_of: (into.wait(), out_of.start()))
-
-    @pl.when(i == steps - 1)
-    def _():
-        each(i, lambda into, out_of: out_of.wait())
+        through[1].wait()
         store(i - 1).wait()
         store(i).wait()
 
 
-def finish(x_all, d_pre, dw_in_part, dw_down_part):
+def finish(x_all, d_pre, dw_in_part, dw_down_part, dx_part):
     tokens, ff = d_pre.shape
     width = x_all.shape[1]
     n = width // 16
-    dma = pltpu.SemaphoreType.DMA
     return pl.pallas_call(
         finish_kernel,
-        grid=(16 - HELD,),
-        in_specs=[pl.BlockSpec((tokens, n), lambda i: (0, HELD + i)), ANY, ANY, ANY],
-        out_specs=[ANY] * 2,
-        out_shape=[jax.ShapeDtypeStruct((width, ff), BF16), jax.ShapeDtypeStruct((ff, width), BF16)],
-        scratch_shapes=[
-            pltpu.VMEM((2, tokens, ff // 2), BF16),
-            pltpu.VMEM((2, n, ff), BF16),
-            pltpu.VMEM((4, ff // 16, width), BF16),
-            pltpu.VMEM((2, n, ff), BF16),
-            dma((2,)),
-            dma((2,)),
-            dma((6,)),
-            dma((6,)),
+        grid=(8,),
+        in_specs=[
+            pl.BlockSpec((tokens, n), lambda i: (0, 8 + i)),
+            pl.BlockSpec((tokens, ff), lambda i: (0, 0)),
+            pl.BlockSpec((n, ff), lambda i: (i, 0)),
+            pl.BlockSpec((ff // 8, width), lambda i: (i, 0)),
+            ANY,
         ],
+        out_specs=[ANY] * 3,
+        out_shape=[jax.ShapeDtypeStruct(size, BF16) for size in ((width, ff), (ff, width), dx_part.shape)],
+        scratch_shapes=[pltpu.VMEM((2, n, ff), BF16), pltpu.VMEM(dx_part.shape, BF16)] + [pltpu.SemaphoreType.DMA((2,))] * 3,
         compiler_params=pltpu.CompilerParams(dimension_semantics=("arbitrary",), vmem_limit_bytes=VMEM_LIMIT),
         cost_estimate=pl.CostEstimate(flops=tokens * ff * width, bytes_accessed=140_000_000, transcendentals=0),
         name="finish",
-    )(x_all, d_pre, dw_in_part, dw_down_part)
+    )(x_all, d_pre, dw_in_part, dw_down_part, dx_part)
 
 
 def solution(mesh):
     def body(x, dy, pre, w_in, w_down):
         x_all, d_pre, dw_down, dx, dw_in = backward(x, dy, pre, w_in, w_down)
-        dw_in, dw_down = finish(x_all, d_pre, dw_in, dw_down)
+        dw_in, dw_down, dx = finish(x_all, d_pre, dw_in, dw_down, dx)
         return dx, dw_in, dw_down
 
     return jax.shard_map(

time: 419 us -> 417 us (level)
    pallas_call x1, Pallas kernels: 354 us -> 362 us  [backward(): pl.pallas_call(backward_kernel, in_specs=[ANY] * 5, out_specs=[ANY] * 9,...]
    pallas_call x1, Pallas kernels: 60.8 us -> 53.4 us  [finish(): pl.pallas_call(finish_kernel, grid=(8,), in_specs=[pl.BlockSpec((tokens,...]
where the time goes in v8:
time: 417 us; the launch traced here: 416 us
  Pallas kernels  415 us (100%)
    pallas_call x1, Pallas kernels, backward(): pl.pallas_call(backward_kernel, in_specs=[ANY] * 5, out_specs=[ANY] * 9,...  362 us
    pallas_call x1, Pallas kernels, finish(): pl.pallas_call(finish_kernel, grid=(8,), in_specs=[pl.BlockSpec((tokens,...  53.4 us

profile of v8, /device:TPU:0, one launch (start us, length us, event | category | flops | bytes accessed | tf_op | source)
XLA Modules:
  0.0 416.2 jit_solution(8325248039923440647)
XLA Ops:
  0.6 361.9 %backward.1 = (bf16[2048,8192]{1,0:T(8,128)(2,1)}, bf16[2048,8192]{1,0:T(8,128)(2,1)}, bf16[2048,2048]{1,0:T(8,128)(2,1)}, bf16[2048,2048]{1,0:T(8,128)(2,1)}, b...) custom-call(bf16[128,8192]{1,0:T(8,128)(2,1)} %x.1, ...), custom_call_target="tpu_custom_call" | custom-call | flops 240518168576 | bytes 800000000 | tf_op jit(solution)/shard_map/backward/pallas_call | solution.py:716
  362.6 53.4 %finish.1 = (bf16[8192,2048]{1,0:T(8,128)(2,1)}, bf16[2048,8192]{1,0:T(8,128)(2,1)}, bf16[128,8192]{1,0:T(8,128)(2,1)}) custom-call(bf16[2048,8192]{1,0:T(8,128)(2,1)} %get-tuple-element.11.x_ref, bf16[2048,2048]{1,0:T(8,128)(2,1)} %get-tuple-element.12.d_pre_ref, bf16[4096,2048]{1,0:T(8,128)(2,1)} %get-tuple-element.13.part_ref, ...), custom_call_target="tpu_custom_call" | custom-call | flops 34359738368 | bytes 140000000 | tf_op jit(solution)/shard_map/finish/pallas_call | solution.py:791

commit v9 on v8

--- a/solution.py
+++ b/solution.py
@@ -333,10 +333,10 @@
             at = pl.program_id(0) * pl.num_programs(1) + pl.program_id(1)
             group, place_in = lax.div(at, 3), lax.rem(at, 3)
 
-            @pl.when(place_in == 1)
+            @pl.when(place_in == 0)
             def _():
                 for n in range(5):
-                    @pl.when(group == n)
+                    @pl.when(group == n + 1)
                     def _():
                         gather_x.act(n)
 
@@ -347,10 +347,6 @@
                     def _():
                         for copy in some:
                             copy.start()
-
-            @pl.when(at == 15)
-            def _():
-                gather_x.act(5)
 
             o_ref[...] = dot(h_ref[...], dy_ref[...], TN).astype(BF16)
 
@@ -553,13 +549,19 @@
                 def _():
                     fetch(i - lag_b)
 
-            between()
-            for j in range(items - lag_b, items):
-                fetch(j)
-            for j in range(items - lag_c, items):
+            def close(j):
                 wait(sources(j))
                 add(j, j % slots, j % n_staged)
                 leave(j).start()
+
+            def midway():
+                fetch(items - 1)
+                close(items - 2)
+
+            close(items - 3)
+            between(midway)
+            close(items - 1)
+
             for i in range(items - n_term, items):
                 send(i).wait_send()
 
@@ -587,7 +589,7 @@
             slot = odd(i)
             return pltpu.make_async_copy(dw_buf.at[slot], dw_in.at[rows(i * n1, n1)], dw_sem.at[slot])
 
-        def tiles(a, b):
+        def tiles(a, b, midway=None):
             @pl.loop(a, b)
             def _(i):
                 slot = odd(i)
@@ -599,6 +601,11 @@
 
                 @pl.loop(0, 2)
                 def _(h):
+                    if midway is not None:
+                        @pl.when(h == 1)
+                        def _():
+                            midway()
+
                     part = lanes(h * (ff // 2), ff // 2)
                     dw_buf[slot, :, part] = dot(x_buf[slot], right[:, part], TN).astype(BF16)
 
@@ -618,9 +625,10 @@
 
         def early(out1):
             def prepare(i):
-                @pl.when(i == 3)
-                def _():
-                    gather_x.act(6)
+                for n in (5, 6):
+                    @pl.when(i == 6 * n - 27)
+                    def _():
+                        gather_x.act(n)
 
                 @pl.when(i == 12)
                 def _():
@@ -634,10 +642,10 @@
                 def _():
                     go(loads2[0] + loads3[0])
 
-            def between():
+            def between(midway):
                 go(loads2[1] + loads3[1])
                 right_load.wait()
-                tiles(0, 1)
+                tiles(0, 1, midway)
 
             def prepare2(i):
                 for p in range(3):
@@ -646,14 +654,14 @@
                         wait(loads2[p] + loads3[p])
 
             stage(0, 16, out1, between, prepare=prepare)
-            stage(1, 8, out2, lambda: tiles(4, 5), prepare=prepare2, filler=fill2)
+            stage(1, 8, out2, lambda midway: tiles(4, 5, midway), prepare=prepare2, filler=fill2)
             for i in range(16):
                 onward(0, i, 4, narrow(i)[0], lanes(narrow(i)[2], n1), 0, out1.at[i]).wait_send()
 
         pl.run_scoped(early, pltpu.VMEM((16, 4 * shard, n1), BF16))
 
         def late(out3, keep):
-            stage(2, 8, out3, lambda: tiles(7, 8), filler=fill3, keep=keep)
+            stage(2, 8, out3, lambda midway: tiles(7, 8, midway), filler=fill3, keep=keep)
             pl.run_scoped(functools.partial(final, keep), pltpu.VMEM((8, shard, n2), BF16), pltpu.VMEM((4, 4, shard, n2), BF16))
             for i in range(8):
                 onward(1, i, 2, wide(i)[0], lanes(wide(i)[2], n2), 16, out2.at[i]).wait_send()

time: 417 us -> 403 us (0.966)
  Pallas kernels: 415 us -> 402 us
    pallas_call x1, Pallas kernels: 362 us -> 349 us  [backward(): pl.pallas_call(backward_kernel, in_specs=[ANY] * 5, out_specs=[ANY] * 9,...]
where the time goes in v9:
time: 403 us
  Pallas kernels  402 us (100%)
    pallas_call x1, Pallas kernels, backward(): pl.pallas_call(backward_kernel, in_specs=[ANY] * 5, out_specs=[ANY] * 9,...  349 us
    pallas_call x1, Pallas kernels, finish(): pl.pallas_call(finish_kernel, grid=(8,), in_specs=[pl.BlockSpec((tokens,...  53.4 us

profile of v9, /device:TPU:0, one launch (start us, length us, event | category | flops | bytes accessed | tf_op | source)
XLA Modules:
  0.0 403.2 jit_solution(5901214097132271511)
XLA Ops:
  0.6 348.9 %backward.1 = (bf16[2048,8192]{1,0:T(8,128)(2,1)}, bf16[2048,8192]{1,0:T(8,128)(2,1)}, bf16[2048,2048]{1,0:T(8,128)(2,1)}, bf16[2048,2048]{1,0:T(8,128)(2,1)}, b...) custom-call(bf16[128,8192]{1,0:T(8,128)(2,1)} %x.1, ...), custom_call_target="tpu_custom_call" | custom-call | flops 240518168576 | bytes 800000000 | tf_op jit(solution)/shard_map/backward/pallas_call | solution.py:724
  349.6 53.4 %finish.1 = (bf16[8192,2048]{1,0:T(8,128)(2,1)}, bf16[2048,8192]{1,0:T(8,128)(2,1)}, bf16[128,8192]{1,0:T(8,128)(2,1)}) custom-call(bf16[2048,8192]{1,0:T(8,128)(2,1)} %get-tuple-element.11.x_ref, bf16[2048,2048]{1,0:T(8,128)(2,1)} %get-tuple-element.12.d_pre_ref, bf16[4096,2048]{1,0:T(8,128)(2,1)} %get-tuple-element.13.part_ref, ...), custom_call_target="tpu_custom_call" | custom-call | flops 34359738368 | bytes 140000000 | tf_op jit(solution)/shard_map/finish/pallas_call | solution.py:799

commit v10 on v9

--- a/solution.py
+++ b/solution.py
@@ -281,6 +281,9 @@
                     @pl.when(j == at + 2)
                     def _():
                         gather_dy.act(k, h)
+                        if at + 1 == len(pieces):
+                            for copy in row_loads(n + 1, True):
+                                copy.start()
 
                 columns = lanes(j * block, block)
                 d_hidden = dot(lhs[slot, :size], weights[rows(j * block, block), :], NT)
@@ -306,7 +309,7 @@
             if n < 5:
                 if n == 1:
                     own_row.wait()
-                for copy in row_loads(n + 1, True):
+                for copy in row_loads(n + 1, True) if pieces[2:] else []:
                     copy.start()
                 chips, h = batches[n + 1]
                 for h in (0, 1) if h is None else (h,):

time: 403 us -> 403 us (level)
  no operation moved by 1% of the time
where the time goes in v10:
time: 403 us
  Pallas kernels  402 us (100%)
    pallas_call x1, Pallas kernels, backward(): pl.pallas_call(backward_kernel, in_specs=[ANY] * 5, out_specs=[ANY] * 9,...  348 us
    pallas_call x1, Pallas kernels, finish(): pl.pallas_call(finish_kernel, grid=(8,), in_specs=[pl.BlockSpec((tokens,...  53.4 us

profile of v10, /device:TPU:0, one launch (start us, length us, event | category | flops | bytes accessed | tf_op | source)
XLA Modules:
  0.0 402.7 jit_solution(15833776703776887486)
XLA Ops:
  0.6 348.4 %backward.1 = (bf16[2048,8192]{1,0:T(8,128)(2,1)}, bf16[2048,8192]{1,0:T(8,128)(2,1)}, bf16[2048,2048]{1,0:T(8,128)(2,1)}, bf16[2048,2048]{1,0:T(8,128)(2,1)}, b...) custom-call(bf16[128,8192]{1,0:T(8,128)(2,1)} %x.1, ...), custom_call_target="tpu_custom_call" | custom-call | flops 240518168576 | bytes 800000000 | tf_op jit(solution)/shard_map/backward/pallas_call | solution.py:727
  349.1 53.4 %finish.1 = (bf16[8192,2048]{1,0:T(8,128)(2,1)}, bf16[2048,8192]{1,0:T(8,128)(2,1)}, bf16[128,8192]{1,0:T(8,128)(2,1)}) custom-call(bf16[2048,8192]{1,0:T(8,128)(2,1)} %get-tuple-element.11.x_ref, bf16[2048,2048]{1,0:T(8,128)(2,1)} %get-tuple-element.12.d_pre_ref, bf16[4096,2048]{1,0:T(8,128)(2,1)} %get-tuple-element.13.part_ref, ...), custom_call_target="tpu_custom_call" | custom-call | flops 34359738368 | bytes 140000000 | tf_op jit(solution)/shard_map/finish/pallas_call | solution.py:802
